TPU v7x, 8 devices: a whole 2x2x1 slice. The times are simulated.
8 devices in a mesh: dp: 2 (over z, y), tp: 4 (over x, core).
Axes of the slice: x: 2, y: 2, z: 1, core: 2. Of those that a mesh axis runs over, the one named last changes fastest.
Arguments:
- x_in: bfloat16 [8, 1024, 1280], P('dp', 'tp'), parts along dimension 0
- grad_y: bfloat16 [8, 1024, 1280], P('dp', 'tp'), parts along dimension 0
- pad_mask: int32 [8, 1024], P('dp'), parts along dimension 0
- ln1_gain: float32 [1280], replicated
- ln1_bias: float32 [1280], replicated
- w_qkv: bfloat16 [3, 1280, 20, 64], P(None, None, 'tp')
- b_qkv: float32 [3, 20, 64], P(None, 'tp')
- w_out: bfloat16 [20, 64, 1280], P('tp')
- b_out: float32 [1280], replicated
- ln2_gain: float32 [1280], replicated
- ln2_bias: float32 [1280], replicated
- w_up: bfloat16 [1280, 5120], P(None, 'tp')
- b_up: float32 [5120], P('tp')
- w_down: bfloat16 [5120, 1280], P('tp')
- b_down: float32 [1280], replicated
Outputs:
- output 1: bfloat16 [8, 1024, 1280], P('dp', 'tp'), parts along dimension 0
- output 2: bfloat16 [8, 1024, 1280], P('dp', 'tp'), parts along dimension 0
- output 3: float32 [2560], P('dp'), parts along dimension 0
- output 4: float32 [2560], P('dp'), parts along dimension 0
- output 5: float32 [6, 1280, 20, 64], P('dp', None, 'tp'), parts along dimension 0
- output 6: float32 [6, 20, 64], P('dp', 'tp'), parts along dimension 0
- output 7: float32 [40, 64, 1280], P(('dp', 'tp')), parts along dimension 0
- output 8: float32 [2560], P('dp'), parts along dimension 0
- output 9: float32 [2560], P('dp'), parts along dimension 0
- output 10: float32 [2560], P('dp'), parts along dimension 0
- output 11: float32 [2560, 5120], P('dp', 'tp'), parts along dimension 0
- output 12: float32 [10240], P(('dp', 'tp')), parts along dimension 0
- output 13: float32 [10240, 1280], P(('dp', 'tp')), parts along dimension 0
- output 14: float32 [2560], P('dp'), parts along dimension 0
There are 2 independent parts. A program takes and returns all parts, laid end to end along the dimension named above; an argument that names none is the same for every part.
All inputs are finite; a program needn't handle non-finite values.
Results may differ from a plain program's by a relative error of at most 0.0124897.
Values are sent between devices in bfloat16 or wider.
A program may use at most 1 GiB of HBM per device.

v0:
```python
import jax
import jax.numpy as jnp
from jax import lax
from jax.sharding import PartitionSpec as P

LN_EPS = 1e-5
ROPE_BASE = 10000.0
INV_SQRT2 = 0.7071067811865476
INV_SQRT_2PI = 0.3989422804014327
NEG_LARGE = -1e30


def layer_norm(values, ln_gain, ln_bias):
    centered = values - jnp.mean(values, axis=-1, keepdims=True)
    inv_std = lax.rsqrt(jnp.mean(centered * centered, axis=-1, keepdims=True) + LN_EPS)
    x_hat = centered * inv_std
    return x_hat * ln_gain + ln_bias, x_hat, inv_std


def layer_norm_grad(d_out, x_hat, inv_std, ln_gain):
    d_hat = d_out * ln_gain
    return inv_std * (d_hat - jnp.mean(d_hat, axis=-1, keepdims=True) - x_hat * jnp.mean(d_hat * x_hat, axis=-1, keepdims=True))


def rope_tables(seq_len, head_dim):
    half_dim = head_dim // 2
    inv_freq = ROPE_BASE ** (-2.0 * jnp.arange(half_dim, dtype=jnp.float32) / head_dim)
    angles = jnp.arange(seq_len, dtype=jnp.float32)[:, None] * inv_freq[None, :]
    angles = jnp.concatenate([angles, angles], axis=-1)
    return jnp.cos(angles)[:, None, :], jnp.sin(angles)[:, None, :]


def rotate(tensor, cos_tab, sin_tab):
    half_dim = tensor.shape[-1] // 2
    swapped = jnp.concatenate([-tensor[..., half_dim:], tensor[..., :half_dim]], axis=-1)
    return tensor * cos_tab + swapped * sin_tab


def rotate_back(grad_in, cos_tab, sin_tab):
    half_dim = grad_in.shape[-1] // 2
    scaled = grad_in * sin_tab
    swapped = jnp.concatenate([scaled[..., half_dim:], -scaled[..., :half_dim]], axis=-1)
    return grad_in * cos_tab + swapped


def solution(mesh):
    act_spec = P('dp', 'tp', None)
    rep_vec = P(None)
    part_vec = P('dp')
    in_specs = (act_spec, act_spec, P('dp', None), rep_vec, rep_vec, P(None, None, 'tp', None), P(None, 'tp', None),
                P('tp', None, None), rep_vec, rep_vec, rep_vec, P(None, 'tp'), P('tp'), P('tp', None), rep_vec)
    out_specs = (act_spec, act_spec, part_vec, part_vec, P('dp', None, 'tp', None), P('dp', 'tp', None),
                 P(('dp', 'tp'), None, None), part_vec, part_vec, part_vec, P('dp', 'tp'), P(('dp', 'tp')),
                 P(('dp', 'tp'), None), part_vec)

    def device_step(x_in, grad_y, pad_mask, ln1_gain, ln1_bias, w_qkv, b_qkv, w_out, b_out, ln2_gain, ln2_bias, w_up, b_up, w_down, b_down):
        seq_len = pad_mask.shape[1]
        head_dim = w_qkv.shape[3]
        q_scale = head_dim ** -0.5
        cos_tab, sin_tab = rope_tables(seq_len, head_dim)
        key_ok = (pad_mask > 0)[:, None, None, :]
        x_f = x_in.astype(jnp.float32)
        h1_f, x_hat1, inv_std1 = layer_norm(x_f, ln1_gain, ln1_bias)
        h1_full = lax.all_gather(h1_f.astype(jnp.bfloat16), 'tp', axis=1, tiled=True)
        qkv_all = jnp.einsum('bsd,idhk->ibshk', h1_full, w_qkv, preferred_element_type=jnp.float32) + b_qkv[:, None, None]
        q_rot = rotate(qkv_all[0] * q_scale, cos_tab, sin_tab).astype(jnp.bfloat16)
        k_rot = rotate(qkv_all[1], cos_tab, sin_tab).astype(jnp.bfloat16)
        v_heads = qkv_all[2].astype(jnp.bfloat16)
        scores = jnp.einsum('bqhk,bshk->bhqs', q_rot, k_rot, preferred_element_type=jnp.float32)
        attn_probs = jax.nn.softmax(jnp.where(key_ok, scores, NEG_LARGE), axis=-1)
        probs_low = attn_probs.astype(jnp.bfloat16)
        attn_o = jnp.einsum('bhqs,bshk->bqhk', probs_low, v_heads, preferred_element_type=jnp.float32).astype(jnp.bfloat16)
        attn_part = jnp.einsum('cril,ile->cre', attn_o, w_out, preferred_element_type=jnp.float32)
        attn_sum = lax.psum_scatter(attn_part, 'tp', scatter_dimension=1, tiled=True)
        x1_f = (x_f + (attn_sum + b_out)).astype(jnp.bfloat16).astype(jnp.float32)
        h2_f, x_hat2, inv_std2 = layer_norm(x1_f, ln2_gain, ln2_bias)
        h2_full = lax.all_gather(h2_f.astype(jnp.bfloat16), 'tp', axis=1, tiled=True)
        pre_act = jnp.einsum('bsd,df->bsf', h2_full, w_up, preferred_element_type=jnp.float32) + b_up
        erf_term = lax.erf(pre_act * INV_SQRT2)
        act_b = (0.5 * pre_act * (1.0 + erf_term)).astype(jnp.bfloat16)
        gelu_slope = 0.5 * (1.0 + erf_term) + pre_act * jnp.exp(-0.5 * pre_act * pre_act) * INV_SQRT_2PI
        mlp_part = jnp.einsum('bsf,fd->bsd', act_b, w_down, preferred_element_type=jnp.float32)
        mlp_sum = lax.psum_scatter(mlp_part, 'tp', scatter_dimension=1, tiled=True)
        y_out = (x1_f + (mlp_sum + b_down)).astype(jnp.bfloat16)
        dy_full = lax.all_gather(grad_y, 'tp', axis=1, tiled=True)
        dy_f = grad_y.astype(jnp.float32)
        grad_w_down = jnp.einsum('bsf,bsd->fd', act_b, dy_full, preferred_element_type=jnp.float32)
        d_act = jnp.einsum('bsd,fd->bsf', dy_full, w_down, preferred_element_type=jnp.float32)
        d_pre = d_act * gelu_slope
        grad_b_up = jnp.sum(d_pre, axis=(0, 1))
        d_pre_b = d_pre.astype(jnp.bfloat16)
        grad_w_up = jnp.einsum('bsd,bsf->df', h2_full, d_pre_b, preferred_element_type=jnp.float32)
        d_h2_part = jnp.einsum('bsf,df->bsd', d_pre_b, w_up, preferred_element_type=jnp.float32)
        d_h2 = lax.psum_scatter(d_h2_part, 'tp', scatter_dimension=1, tiled=True)
        d_x1 = dy_f + layer_norm_grad(d_h2, x_hat2, inv_std2, ln2_gain)
        mid_sums = lax.psum(jnp.stack([jnp.sum(dy_f, axis=(0, 1)), jnp.sum(d_h2 * x_hat2, axis=(0, 1)),
                                       jnp.sum(d_h2, axis=(0, 1)), jnp.sum(d_x1, axis=(0, 1))]), 'tp')
        d_x1_full = lax.all_gather(d_x1.astype(jnp.bfloat16), 'tp', axis=1, tiled=True)
        grad_w_out = jnp.einsum('bshk,bsd->hkd', attn_o, d_x1_full, preferred_element_type=jnp.float32)
        d_attn_o = jnp.einsum('bsd,hkd->bshk', d_x1_full, w_out, preferred_element_type=jnp.float32).astype(jnp.bfloat16)
        d_value = jnp.einsum('bhqs,bqhk->bshk', probs_low, d_attn_o, preferred_element_type=jnp.float32)
        d_probs = jnp.einsum('bqhk,bshk->bhqs', d_attn_o, v_heads, preferred_element_type=jnp.float32)
        d_scores = (attn_probs * (d_probs - jnp.sum(d_probs * attn_probs, axis=-1, keepdims=True))).astype(jnp.bfloat16)
        d_query = jnp.einsum('bhqs,bshk->bqhk', d_scores, k_rot, preferred_element_type=jnp.float32)
        d_key = jnp.einsum('bhqs,bqhk->bshk', d_scores, q_rot, preferred_element_type=jnp.float32)
        d_qkv = jnp.stack([rotate_back(d_query, cos_tab, sin_tab) * q_scale, rotate_back(d_key, cos_tab, sin_tab), d_value])
        grad_b_qkv = jnp.sum(d_qkv, axis=(1, 2))
        d_qkv_b = d_qkv.astype(jnp.bfloat16)
        grad_w_qkv = jnp.einsum('bsd,ibshk->idhk', h1_full, d_qkv_b, preferred_element_type=jnp.float32)
        d_h1_part = jnp.einsum('ibshk,idhk->bsd', d_qkv_b, w_qkv, preferred_element_type=jnp.float32)
        d_h1 = lax.psum_scatter(d_h1_part, 'tp', scatter_dimension=1, tiled=True)
        ln1_sums = lax.psum(jnp.stack([jnp.sum(d_h1 * x_hat1, axis=(0, 1)), jnp.sum(d_h1, axis=(0, 1))]), 'tp')
        grad_x = (d_x1 + layer_norm_grad(d_h1, x_hat1, inv_std1, ln1_gain)).astype(jnp.bfloat16)
        return (y_out, grad_x, ln1_sums[0], ln1_sums[1], grad_w_qkv, grad_b_qkv, grad_w_out, mid_sums[3],
                mid_sums[1], mid_sums[2], grad_w_up, grad_b_up, grad_w_down, mid_sums[0])

    return jax.shard_map(device_step, mesh=mesh, in_specs=in_specs, out_specs=out_specs, check_vma=False)
```

profile of v0, /device:TPU:0, one launch (start us, length us, event | category | flops | bytes accessed | tf_op | source)
XLA Modules:
  0.0 1310.2 jit_solution(10993734941030757731)
XLA Ops:
  18.8 67.6 %all-gather.5.cloned.1.call-done = bf16[4,1024,1280]{2,1,0:T(8,128)(2,1)} async-done(((bf16[4,256,1280]{2,1,0:T(8,128)(2,1)}), bf16[4,1024,1280]{2,1,0:T(8,128)(2,1)}) %all-gather.5.cloned.1.call-update) | async-done | bytes 10485776 | tf_op jit(solution)/shard_map/all_gather | solution.py:64
  124.5 35.0 %fusion.124 = (f32[4,5,1024]{2,1,0:T(8,128)S(1)}, f32[4,5,1024,1024]{2,3,1,0:T(8,128)}) fusion(pred[4,1024]{1,0:T(4,128)(4,1)S(1)} %copy-done.40, bf16[4,1024,5,64]{1,3,2,0:T(8,128)(2,1)} %get-tuple-element.49, bf16[4,1024,5,64]{1,3,2,0:T(8,128)(2,1)} %get-tuple-element.48), kind=kOutput, calls=%fused_computation.150 | convolution fusion | flops 2747270144 | bytes 89214976 | tf_op jit(solution)/shard_map/sub | solution.py:70
  159.5 36.6 %fusion.88 = bf16[4,5,64,1024]{3,2,1,0:T(8,128)(2,1)} fusion(f32[3,4,1024,5,64]{2,4,3,0,1:T(8,128)} %copy-done.7, f32[4,5,1024]{2,1,0:T(8,128)S(1)} %get-tuple-element.67, pred[4,1024]{1,0:T(4,128)(4,1)S(1)} %copy-done.40, bf16[4,1024,5,64]{1,3,2,0:T(8,128)(2,1)} %get-tuple-element.49, bf16[4,1024,5,64]{1,3,2,0:T(8,128)(2,1)} %get-tuple-element.48), kind=kOutput, calls=%fused_computation.118 | convolution fusion | flops 5453927424 | bytes 10571776 | tf_op jit(solution)/shard_map/bhqs,bshk->bqhk/dot_general | solution.py:72
  208.1 143.7 %reduce-scatter.5.cloned.1.call-done = f32[4,256,1280]{2,1,0:T(8,128)} async-done(((f32[4,1024,1280]{2,1,0:T(8,128)}), f32[4,256,1280]{2,1,0:T(8,128)}) %reduce-scatter.5.cloned.1.call-update) | async-done | bytes 5242896 | tf_op jit(solution)/shard_map/reduce_scatter | solution.py:74
  361.2 67.4 %all-gather.7.cloned.1.call-done = bf16[4,1024,1280]{2,1,0:T(8,128)(2,1)} async-done(((bf16[4,256,1280]{2,1,0:T(8,128)(2,1)}), bf16[4,1024,1280]{2,1,0:T(8,128)(2,1)}) %all-gather.7.cloned.1.call-update) | async-done | bytes 10485776 | tf_op jit(solution)/shard_map/all_gather | solution.py:77
  428.6 20.2 %multiply_convert_fusion.1 = (bf16[4,1024,1280]{2,1,0:T(8,128)(2,1)}, f32[4,1024,1280]{2,1,0:T(8,128)}) fusion(f32[1280]{0:T(1024)S(1)} %copy-done.44, bf16[4,1024,1280]{2,1,0:T(8,128)(2,1)} %all-gather.7.cloned.1.call-done, bf16[1280,1280]{1,0:T(8,128)(2,1)S(1)} %copy-done), kind=kOutput, calls=%fused_computation.15 | convolution fusion | flops 13453230080 | bytes 45224960 | tf_op jit(solution)/shard_map/bsd,df->bsf/dot_general | solution.py:78
  448.7 49.1 %all-gather.9.cloned.1.call-done = bf16[4,1024,1280]{2,1,0:T(8,128)(2,1)} async-done(((bf16[4,256,1280]{2,1,0:T(8,128)(2,1)}), bf16[4,1024,1280]{2,1,0:T(8,128)(2,1)}) %all-gather.9.cloned.1.call-update) | async-done | bytes 10485776 | tf_op jit(solution)/shard_map/all_gather | solution.py:85
  497.8 23.5 %fusion.125 = (f32[1280]{0:T(1024)}, bf16[4,1024,1280]{2,1,0:T(8,128)(2,1)S(1)}) fusion(f32[4,1024,1280]{2,1,0:T(8,128)} %get-tuple-element.70, bf16[4,1024,1280]{2,1,0:T(8,128)(2,1)} %all-gather.9.cloned.1.call-done, bf16[1280,1280]{1,0:T(8,128)(2,1)} %param.28), kind=kOutput, calls=%fused_computation.151 | convolution fusion | flops 13479443456 | bytes 45224960 | tf_op jit(solution)/shard_map/bsd,fd->bsf/dot_general | solution.py:88
  525.3 16.6 %fusion.66 = f32[4,1024,1280]{2,1,0:T(8,128)} fusion(bf16[4,1024,1280]{2,1,0:T(8,128)(2,1)S(1)} %get-tuple-element.75, bf16[1280,1280]{1,0:T(8,128)(2,1)S(1)} %copy-done), kind=kOutput, calls=%fused_computation.96 | convolution fusion | flops 13421772800 | bytes 34734080 | tf_op jit(solution)/shard_map/bsf,df->bsd/dot_general | solution.py:93
  543.9 19.1 %fusion.73 = f32[4,1024,1280]{2,1,0:T(8,128)} fusion(bf16[4,1024,1280]{2,1,0:T(8,128)(2,1)} %get-tuple-element.69, bf16[1280,1280]{1,0:T(8,128)(2,1)S(1)} %copy-done.42), kind=kOutput, calls=%fused_computation.103 | convolution fusion | flops 13421772800 | bytes 34734080 | tf_op jit(solution)/shard_map/bsf,fd->bsd/dot_general | solution.py:82
  563.1 123.0 %reduce-scatter.9.cloned.1.call-done = f32[4,256,1280]{2,1,0:T(8,128)} async-done(((f32[4,1024,1280]{2,1,0:T(8,128)}), f32[4,256,1280]{2,1,0:T(8,128)}) %reduce-scatter.9.cloned.1.call-update) | async-done | bytes 5242896 | tf_op jit(solution)/shard_map/reduce_scatter | solution.py:94
  690.9 141.6 %reduce-scatter.7.cloned.1.call-done = f32[4,256,1280]{2,1,0:T(8,128)} async-done(((f32[4,1024,1280]{2,1,0:T(8,128)}), f32[4,256,1280]{2,1,0:T(8,128)}) %reduce-scatter.7.cloned.1.call-update) | async-done | bytes 5242896 | tf_op jit(solution)/shard_map/reduce_scatter | solution.py:83
  845.6 40.1 %fusion.199 = bf16[4,5,1024,1024]{2,3,1,0:T(8,128)(2,1)} fusion(f32[4,5,1024]{2,1,0:T(8,128)S(1)} %copy-done.17, pred[4,1024]{1,0:T(4,128)(4,1)S(1)} %copy-done.41, bf16[4,1024,5,64]{1,3,2,0:T(8,128)(2,1)S(1)} %copy-done.11, bf16[4,1024,5,64]{1,3,2,0:T(8,128)(2,1)} %get-tuple-element.48), kind=kOutput, calls=%fused_computation.18.clone.clone.clone.1 | convolution fusion | flops 2768262144 | bytes 47271936 | tf_op jit(solution)/shard_map/sub | solution.py:70
  885.7 27.0 %all-gather.11.cloned.1.call-done = bf16[4,1024,1280]{2,1,0:T(8,128)(2,1)} async-done(((bf16[4,256,1280]{2,1,0:T(8,128)(2,1)}), bf16[4,1024,1280]{2,1,0:T(8,128)(2,1)}) %all-gather.11.cloned.1.call-update) | async-done | bytes 10485776 | tf_op jit(solution)/shard_map/all_gather | solution.py:98
  920.4 20.5 %fusion.85 = f32[1,4,1024,5,64]{2,4,3,1,0:T(8,128)} fusion(bf16[4,1024,5,64]{1,3,2,0:T(8,128)(2,1)S(1)} %fusion.91, bf16[4,5,1024,1024]{2,3,1,0:T(8,128)(2,1)} %fusion.199), kind=kOutput, calls=%fused_computation.117 | convolution fusion | flops 2684354560 | bytes 49807360 | tf_op jit(solution)/shard_map/bhqs,bqhk->bshk/dot_general | solution.py:101
  940.9 55.1 %multiply_reduce_fusion = (f32[4,5,1024]{2,1,0:T(8,128)S(1)}, f32[4,5,1024,1024]{2,3,1,0:T(8,128)}) fusion(f32[4,5,1024,1024]{2,3,1,0:T(8,128)} %get-tuple-element.68, f32[4,5,1024]{2,1,0:T(8,128)S(1)} %copy-done.17, bf16[4,1024,5,64]{1,3,2,0:T(8,128)(2,1)S(1)} %fusion.91, f32[3,4,1024,5,64]{2,4,3,0,1:T(8,128)} %copy-done.7), kind=kOutput, calls=%fused_computation.2 | convolution fusion | flops 2747248640 | bytes 173178880 | tf_op jit(solution)/shard_map/bqhk,bshk->bhqs/dot_general | solution.py:102
  996.0 65.7 %multiply_convert_fusion = bf16[4,5,1024,1024]{2,3,1,0:T(8,128)(2,1)} fusion(f32[4,5,1024,1024]{2,3,1,0:T(8,128)} %get-tuple-element.72, f32[4,5,1024]{2,1,0:T(8,128)S(1)} %get-tuple-element.71, f32[4,5,1024,1024]{2,3,1,0:T(8,128)} %get-tuple-element.68, f32[4,5,1024]{2,1,0:T(8,128)S(1)} %copy-done.17), kind=kLoop, calls=%fused_computation.1 | loop fusion | flops 83886080 | bytes 209879040 | tf_op jit(solution)/shard_map/convert_element_type | solution.py:103
  1061.7 20.5 %fusion.126 = f32[4,5,64,1024]{3,2,1,0:T(8,128)} fusion(bf16[4,1024,5,64]{1,3,2,0:T(8,128)(2,1)S(1)} %copy-done.12, bf16[4,5,1024,1024]{2,3,1,0:T(8,128)(2,1)} %multiply_convert_fusion), kind=kOutput, calls=%fused_computation.152 | convolution fusion | flops 2684354560 | bytes 49807360 | tf_op jit(solution)/shard_map/bhqs,bqhk->bshk/dot_general | solution.py:105
  1082.2 19.7 %bitcast_multiply_fusion.2 = (f32[4,1024,5,64]{1,3,2,0:T(8,128)S(1)}, f32[4,1024,5,64]{1,3,2,0:T(8,128)S(1)}, f32[4,5,64,1024]{3,2,1,0:T(8,128)}) fusion(f32[1024,64]{0,1:T(8,128)S(1)} %copy-done.9, f32[4,5,64,1024]{3,2,1,0:T(8,128)} %fusion.126, bf16[4,1024,5,64]{1,3,2,0:T(8,128)(2,1)} %get-tuple-element.48, ...), kind=kOutput, calls=%fused_computation.93 | convolution fusion | flops 2686976000 | bytes 65798144 | tf_op jit(solution)/shard_map/bhqs,bshk->bqhk/dot_general | solution.py:104
  1116.7 19.3 %convolution_bitcast_fusion = f32[4,1024,1280]{2,1,0:T(8,128)} fusion(bf16[3,1280,5,64]{1,3,2,0:T(8,128)(2,1)S(1)} %copy-done.43, f32[1,4,1024,5,64]{2,4,3,1,0:T(8,128)} %fusion.85, f32[1,4,1024,5,64]{2,4,3,1,0:T(8,128)} %get-tuple-element.61, f32[1,4,1024,5,64]{2,4,3,1,0:T(8,128)} %get-tuple-element.60), kind=kOutput, calls=%fused_computation.22 | convolution fusion | flops 10074193920 | bytes 39157760 | tf_op jit(solution)/shard_map/ibshk,idhk->bsd/dot_general | solution.py:110
  1136.0 21.8 %convolution_bitcast_fusion.2 = f32[1280,1280]{1,0:T(8,128)} fusion(bf16[4,1024,1280]{2,1,0:T(8,128)(2,1)} %get-tuple-element.69, bf16[4,1024,1280]{2,1,0:T(8,128)(2,1)} %all-gather.9.cloned.1.call-done), kind=kOutput, calls=%fused_computation.37 | convolution fusion | flops 13421772800 | bytes 27525120 | tf_op jit(solution)/shard_map/bsf,bsd->fd/dot_general | solution.py:87
  1157.8 21.8 %convolution_bitcast_fusion.3 = f32[1280,1280]{1,0:T(8,128)} fusion(bf16[4,1024,1280]{2,1,0:T(8,128)(2,1)} %all-gather.7.cloned.1.call-done, bf16[4,1024,1280]{2,1,0:T(8,128)(2,1)} %copy-done.46), kind=kOutput, calls=%fused_computation.38 | convolution fusion | flops 13421772800 | bytes 27525120 | tf_op jit(solution)/shard_map/bsd,bsf->df/dot_general | solution.py:92
  1189.0 16.9 %fusion.69 = f32[3,1280,5,64]{1,3,2,0:T(8,128)} fusion(bf16[4,1024,1280]{2,1,0:T(8,128)(2,1)} %all-gather.5.cloned.1.call-done, f32[1,4,1024,5,64]{2,4,3,1,0:T(8,128)S(1)} %bitcast.178, f32[1,4,1024,5,64]{2,4,3,1,0:T(8,128)S(1)} %bitcast.182, f32[1,4,1024,5,64]{2,4,3,1,0:T(8,128)S(1)} %bitcast.180), kind=kOutput, calls=%fused_computation.101 | convolution fusion | flops 10074193920 | bytes 31129600 | tf_op jit(solution)/shard_map/bsd,ibshk->idhk/dot_general | solution.py:109
  1205.9 74.2 %reduce-scatter.11.cloned.1.call-done = f32[4,256,1280]{2,1,0:T(8,128)} async-done(((f32[4,1024,1280]{2,1,0:T(8,128)}), f32[4,256,1280]{2,1,0:T(8,128)}) %reduce-scatter.11.cloned.1.call-update) | async-done | bytes 5242896 | tf_op jit(solution)/shard_map/reduce_scatter | solution.py:111
  (178 shorter events, 149.4 us)
Async XLA Ops:
  7.2 421.4 %copy-start = (bf16[1280,1280]{1,0:T(8,128)(2,1)S(1)}, bf16[1280,1280]{1,0:T(8,128)(2,1)}, u32[]{:S(2)}) copy-start(bf16[1280,1280]{1,0:T(8,128)(2,1)} %param.26) | copy-start | bytes 9830404
  7.2 79.1 %all-gather.5.cloned.1.call-start = ((), (), s32[]{:S(2)}) async-start(), calls=%async_computation.4 | async-start | bytes 13107200 | tf_op jit(solution)/shard_map/all_gather | solution.py:64
  15.5 336.3 %reduce-scatter.5.cloned.1.call-start = ((), (), s32[]{:S(2)}) async-start(), calls=%async_computation.5 | async-start | bytes 26214400 | tf_op jit(solution)/shard_map/reduce_scatter | solution.py:74
  18.1 96.7 %copy-start.8 = (f32[1024,64]{0,1:T(8,128)}, f32[1024,64]{0,1:T(8,128)S(1)}, u32[]{:S(2)}) copy-start(f32[1024,64]{0,1:T(8,128)S(1)} %get-tuple-element.66) | copy-start | bytes 786436
  207.6 144.2 %copy-start.39 = (f32[1280]{0:T(1024)S(1)}, f32[1280]{0:T(1024)}, u32[]{:S(2)}) copy-start(f32[1280]{0:T(1024)} %param.23) | copy-start | bytes 15364
  207.7 150.4 %copy-start.22 = (f32[1280]{0:T(1024)S(1)}, f32[1280]{0:T(1024)}, u32[]{:S(2)}) copy-start(f32[1280]{0:T(1024)} %param.24) | copy-start | bytes 15364
  207.7 150.4 %copy-start.38 = (f32[1280]{0:T(1024)S(1)}, f32[1280]{0:T(1024)}, u32[]{:S(2)}) copy-start(f32[1280]{0:T(1024)} %param.25) | copy-start | bytes 15364
  207.7 220.9 %all-gather.7.cloned.1.call-start = ((), (), s32[]{:S(2)}) async-start(), calls=%async_computation.6 | async-start | bytes 13107200 | tf_op jit(solution)/shard_map/all_gather | solution.py:77
  358.0 70.5 %copy-start.44 = (f32[1280]{0:T(1024)S(1)}, f32[1280]{0:T(1024)}, u32[]{:S(2)}) copy-start(f32[1280]{0:T(1024)} %param.27) | copy-start | bytes 15364
  360.6 137.3 %all-gather.9.cloned.1.call-start = ((), (), s32[]{:S(2)}) async-start(), calls=%async_computation.8 | async-start | bytes 13107200 | tf_op jit(solution)/shard_map/all_gather | solution.py:85
  361.2 324.9 %reduce-scatter.9.cloned.1.call-start = ((), (), s32[]{:S(2)}) async-start(), calls=%async_computation.9 | async-start | bytes 26214400 | tf_op jit(solution)/shard_map/reduce_scatter | solution.py:94
  541.9 290.6 %reduce-scatter.7.cloned.1.call-start = ((), (), s32[]{:S(2)}) async-start(), calls=%async_computation.7 | async-start | bytes 26214400 | tf_op jit(solution)/shard_map/reduce_scatter | solution.py:83
  563.0 123.1 %copy-start.5 = (bf16[4,256,1280]{2,1,0:T(8,128)(2,1)S(1)}, bf16[4,256,1280]{2,1,0:T(8,128)(2,1)}, u32[]{:S(2)}) copy-start(bf16[4,256,1280]{2,1,0:T(8,128)(2,1)} %copy-done.4) | copy-start | bytes 7864324
  563.0 123.1 %copy-start.19 = (f32[4,256]{1,0:T(4,128)S(1)}, f32[4,256]{1,0:T(4,128)}, u32[]{:S(2)}) copy-start(f32[4,256]{1,0:T(4,128)} %copy-done.18) | copy-start | bytes 12292
  563.0 123.1 %copy-start.23 = (f32[1280]{0:T(1024)S(1)}, f32[1280]{0:T(1024)}, u32[]{:S(2)}) copy-start(f32[1280]{0:T(1024)} %param.24) | copy-start | bytes 15364
  563.0 123.1 %copy-start.27 = (f32[4,256]{1,0:T(4,128)S(1)}, f32[4,256]{1,0:T(4,128)}, u32[]{:S(2)}) copy-start(f32[4,256]{1,0:T(4,128)} %copy-done.26) | copy-start | bytes 12292
  563.0 269.5 %copy-start.36 = (f32[1280]{0:T(1024)S(1)}, f32[1280]{0:T(1024)}, u32[]{:S(2)}) copy-start(f32[1280]{0:T(1024)} %param.29) | copy-start | bytes 15364
  563.0 349.7 %all-gather.11.cloned.1.call-start = ((), (), s32[]{:S(2)}) async-start(), calls=%async_computation.10 | async-start | bytes 13107200 | tf_op jit(solution)/shard_map/all_gather | solution.py:98
  844.7 435.4 %reduce-scatter.11.cloned.1.call-start = ((), (), s32[]{:S(2)}) async-start(), calls=%async_computation.11 | async-start | bytes 26214400 | tf_op jit(solution)/shard_map/reduce_scatter | solution.py:111
  996.0 65.7 %copy-start.12 = (bf16[4,1024,5,64]{1,3,2,0:T(8,128)(2,1)S(1)}, bf16[4,1024,5,64]{1,3,2,0:T(8,128)(2,1)}, u32[]{:S(2)}) copy-start(bf16[4,1024,5,64]{1,3,2,0:T(8,128)(2,1)} %get-tuple-element.49) | copy-start | bytes 7864324
  1189.0 91.1 %copy-start.3 = (bf16[4,256,1280]{2,1,0:T(8,128)(2,1)S(1)}, bf16[4,256,1280]{2,1,0:T(8,128)(2,1)}, u32[]{:S(2)}) copy-start(bf16[4,256,1280]{2,1,0:T(8,128)(2,1)} %param.15) | copy-start | bytes 7864324
  1189.0 91.1 %copy-start.21 = (f32[4,256]{1,0:T(4,128)S(1)}, f32[4,256]{1,0:T(4,128)}, u32[]{:S(2)}) copy-start(f32[4,256]{1,0:T(4,128)} %copy-done.20) | copy-start | bytes 12292
  1189.0 91.1 %copy-start.25 = (f32[1280]{0:T(1024)S(1)}, f32[1280]{0:T(1024)}, u32[]{:S(2)}) copy-start(f32[1280]{0:T(1024)} %param.18) | copy-start | bytes 15364
  1189.0 91.1 %copy-start.29 = (f32[4,256]{1,0:T(4,128)S(1)}, f32[4,256]{1,0:T(4,128)}, u32[]{:S(2)}) copy-start(f32[4,256]{1,0:T(4,128)} %copy-done.28) | copy-start | bytes 12292
  (39 other events, 460.9 us)
Sparse Core Ops, SparseCore 0:
  15.6 70.6 all-gather.4
  207.8 143.9 reduce-scatter.4
  360.7 67.8 all-gather.6
  430.0 67.8 all-gather.8
  542.1 143.9 reduce-scatter.8
  688.5 143.9 reduce-scatter.6
  844.8 67.8 all-gather.10
  1136.1 143.9 reduce-scatter.10
where the time goes:
time: 1310 us
  waiting for transfers between devices  694 us (53%)
  matrix products  427 us (33%)
  other arithmetic  140 us (11%)
  local copies, waits for them, and re-layouts  22.4 us (2%)
  between operations  14.9 us (1%)
    reduce_scatter x1, waiting for transfers between devices, device_step(): lax.psum_scatter(attn_part, 'tp', scatter_dimension=1, tiled=True)  144 us
    reduce_scatter x1, waiting for transfers between devices, device_step(): mlp_sum = lax.psum_scatter(mlp_part, 'tp', scatter_dimension=1, tiled=True)  142 us
    reduce_scatter x1, waiting for transfers between devices, device_step(): d_h2 = lax.psum_scatter(d_h2_part, 'tp', scatter_dimension=1, tiled=True)  123 us
    sub x2, matrix products, device_step(): attn_probs = jax.nn.softmax(jnp.where(key_ok, scores, NEG_LARGE), axis=-1)  75.2 us
    reduce_scatter x1, waiting for transfers between devices, device_step(): d_h1 = lax.psum_scatter(d_h1_part, 'tp', scatter_dimension=1, tiled=True)  74.2 us
    all_gather x1, waiting for transfers between devices, device_step(): lax.all_gather(h1_f.astype(jnp.bfloat16), 'tp', axis=1, tiled=True)  67.6 us
    all_gather x1, waiting for transfers between devices, device_step(): lax.all_gather(h2_f.astype(jnp.bfloat16), 'tp', axis=1, tiled=True)  67.4 us
    convert_element_type x1, other arithmetic, device_step(): (attn_probs * (d_probs - jnp.sum(d_probs * attn_probs, axis=-1, keepdims=...  65.7 us
  transfers between devices with their start and end apart: 8, of which 8 were waited for; matrix products, arithmetic and copies ran while one was open for 12% of the time, Pallas kernels for 0%

commit v1 on v0

v1 whole, which is shorter than its diff:
```python
import functools

import jax
import jax.numpy as jnp
from jax import lax
from jax.experimental import pallas as pl
from jax.experimental.pallas import tpu as pltpu
from jax.sharding import PartitionSpec as P

LN_EPS = 1e-5
ROPE_BASE = 10000.0
INV_SQRT2 = 0.7071067811865476
INV_SQRT_2PI = 0.3989422804014327
NEG_LARGE = -1e30
F32 = jnp.float32
BF16 = jnp.bfloat16
NT = (((1,), (1,)), ((), ()))
VMEM_LIMIT = 60 * 1024 * 1024
QB = 256


def layer_norm(values, ln_gain, ln_bias):
    centered = values - jnp.mean(values, axis=-1, keepdims=True)
    inv_std = lax.rsqrt(jnp.mean(centered * centered, axis=-1, keepdims=True) + LN_EPS)
    x_hat = centered * inv_std
    return x_hat * ln_gain + ln_bias, x_hat, inv_std


def layer_norm_grad(d_out, x_hat, inv_std, ln_gain):
    d_hat = d_out * ln_gain
    return inv_std * (d_hat - jnp.mean(d_hat, axis=-1, keepdims=True) - x_hat * jnp.mean(d_hat * x_hat, axis=-1, keepdims=True))


def rope_tables(seq_len, head_dim):
    half_dim = head_dim // 2
    inv_freq = ROPE_BASE ** (-2.0 * jnp.arange(half_dim, dtype=F32) / head_dim)
    angles = jnp.arange(seq_len, dtype=F32)[:, None] * inv_freq[None, :]
    cos_half, sin_half = jnp.cos(angles), jnp.sin(angles)
    cos_tab = jnp.concatenate([cos_half] * 4, axis=-1)
    sin_tab = jnp.concatenate([-sin_half, sin_half, -sin_half, sin_half], axis=-1)
    return cos_tab, sin_tab


def swap_halves(t, first_half):
    return jnp.where(first_half, pltpu.roll(t, 96, 1), pltpu.roll(t, 32, 1))


def pair_rows(ref0, ref1):
    return jnp.concatenate([r[i] for i in range(3) for r in (ref0, ref1)], axis=0)


def attn_fwd_kernel(h_ref, w0_ref, w1_ref, b_ref, cos_ref, sin_ref, mb_ref, wo0_ref, wo1_ref,
                    q_ref, k_ref, v_ref, o_ref, lse_ref, acc_ref, qs, ks, st):
    seq = h_ref.shape[0]
    lane = lax.broadcasted_iota(jnp.int32, (1, 128), 1)
    first_half = (lane % 64) < 32
    head0 = lane < 64
    w = pair_rows(w0_ref, w1_ref)
    t = lax.dot_general(h_ref[...], w, NT, preferred_element_type=F32)
    cos, sin = cos_ref[...], sin_ref[...]
    tq = (t[:, :128] + b_ref[0, 0:1]) * 0.125
    tk = t[:, 128:256] + b_ref[0, 1:2]
    q = (tq * cos + swap_halves(tq, first_half) * sin).astype(BF16)
    k = (tk * cos + swap_halves(tk, first_half) * sin).astype(BF16)
    v_ref[...] = (t[:, 256:] + b_ref[0, 2:3]).astype(BF16)
    q_ref[...] = q
    k_ref[...] = k
    q, k = q.astype(F32), k.astype(F32)
    mb = mb_ref[...]
    qs[0] = jnp.where(head0, q, jnp.where(lane == 64, 1.0, 0.0)).astype(BF16)
    qs[1] = jnp.where(head0, jnp.where(lane == 0, 1.0, 0.0), q).astype(BF16)
    ks[0] = jnp.where(head0, k, jnp.where(lane == 64, mb, 0.0)).astype(BF16)
    ks[1] = jnp.where(head0, jnp.where(lane == 0, mb, 0.0), k).astype(BF16)

    def block(j, carry):
        rows = pl.ds(pl.multiple_of(j * QB, QB), QB)
        outs, stats = [], []
        for head in range(2):
            s = lax.dot_general(qs[head, rows, :], ks[head], NT, preferred_element_type=F32)
            m = jnp.max(s, axis=-1, keepdims=True)
            e = jnp.exp(s - m)
            total = jnp.sum(e, axis=-1, keepdims=True)
            p = (e * (1.0 / total)).astype(BF16)
            outs.append(jnp.dot(p, v_ref[...], preferred_element_type=F32))
            stats.append(m + jnp.log(total))
        o_ref[rows, :] = jnp.where(head0, outs[0], outs[1]).astype(BF16)
        st[rows, :] = jnp.where(head0, stats[0], stats[1])
        return carry

    lax.fori_loop(0, seq // QB, block, 0)
    st_t = st[...].T
    lse_ref[0] = jnp.concatenate([st_t[0:1]] * 4 + [st_t[64:65]] * 4, axis=0)
    wo = jnp.concatenate([wo0_ref[0], wo1_ref[0]], axis=0)
    part = jnp.dot(o_ref[...], wo, preferred_element_type=F32)

    @pl.when(pl.program_id(0) == 0)
    def _():
        acc_ref[...] = part

    @pl.when(pl.program_id(0) > 0)
    def _():
        acc_ref[...] += part


def attn_fwd(h1, w0, w1, bias, cos_tab, sin_tab, mask_col, wo0, wo1):
    seq, dim = h1.shape
    heads = w0.shape[1] // 64
    full = lambda i: (0, 0)
    pair = pl.BlockSpec((seq, 128), lambda i: (0, i))
    head_w = pl.BlockSpec((3, 64, dim), lambda i: (0, i, 0))
    head_o = pl.BlockSpec((1, 64, dim), lambda i: (i, 0, 0))
    act = jax.ShapeDtypeStruct((seq, heads * 128), BF16)
    return pl.pallas_call(
        attn_fwd_kernel,
        grid=(heads,),
        in_specs=[pl.BlockSpec((seq, dim), full), head_w, head_w, pl.BlockSpec((1, 3, 128), lambda i: (i, 0, 0)),
                  pl.BlockSpec((seq, 128), full), pl.BlockSpec((seq, 128), full), pl.BlockSpec((seq, 128), full), head_o, head_o],
        out_specs=[pair, pair, pair, pair, pl.BlockSpec((1, 8, seq), lambda i: (i, 0, 0)), pl.BlockSpec((seq, dim), full)],
        out_shape=[act, act, act, act, jax.ShapeDtypeStruct((heads, 8, seq), F32), jax.ShapeDtypeStruct((seq, dim), F32)],
        scratch_shapes=[pltpu.VMEM((2, seq, 128), BF16), pltpu.VMEM((2, seq, 128), BF16), pltpu.VMEM((seq, 128), F32)],
        compiler_params=pltpu.CompilerParams(dimension_semantics=("arbitrary",), vmem_limit_bytes=VMEM_LIMIT),
        cost_estimate=pl.CostEstimate(flops=heads * 2 * seq * (dim * 512 + 4 * seq * 256), bytes_accessed=20_000_000, transcendentals=0),
        name="attn_fwd",
    )(h1, w0, w1, bias, cos_tab, sin_tab, mask_col, wo0, wo1)


def attn_bwd_kernel(h_ref, dx_ref, w0_ref, w1_ref, wo0_ref, wo1_ref, q_ref, k_ref, v_ref, o_ref, lse_ref, cos_ref, sin_ref, mb_ref,
                    dh_ref, gw0_ref, gw1_ref, gwo0_ref, gwo1_ref, gb_ref, qs, qz, ks, dos, kt, dqt, dk_acc, dv_acc):
    seq, dim = h_ref.shape
    lane = lax.broadcasted_iota(jnp.int32, (1, 128), 1)
    first_half = (lane % 64) < 32
    head0 = lane < 64
    dx = dx_ref[...]
    wo = jnp.concatenate([wo0_ref[0], wo1_ref[0]], axis=0)
    d_o = lax.dot_general(dx, wo, NT, preferred_element_type=F32)
    dos[0] = jnp.where(head0, d_o, 0.0).astype(BF16)
    dos[1] = jnp.where(head0, 0.0, d_o).astype(BF16)
    gwo = jnp.dot(o_ref[...].T, dx, preferred_element_type=F32)
    gwo0_ref[0] = gwo[:64]
    gwo1_ref[0] = gwo[64:]
    q, k, mb = q_ref[...].astype(F32), k_ref[...].astype(F32), mb_ref[...]
    qs[0] = jnp.where(head0, q, jnp.where(lane == 64, 1.0, 0.0)).astype(BF16)
    qs[1] = jnp.where(head0, jnp.where(lane == 0, 1.0, 0.0), q).astype(BF16)
    qz[0] = jnp.where(head0, q, 0.0).astype(BF16)
    qz[1] = jnp.where(head0, 0.0, q).astype(BF16)
    ks[0] = jnp.where(head0, k, jnp.where(lane == 64, mb, 0.0)).astype(BF16)
    ks[1] = jnp.where(head0, jnp.where(lane == 0, mb, 0.0), k).astype(BF16)
    kt[...] = k_ref[...].T
    dk_acc[...] = jnp.zeros_like(dk_acc)
    dv_acc[...] = jnp.zeros_like(dv_acc)

    def block(j, carry):
        rows = pl.ds(pl.multiple_of(j * QB, QB), QB)
        for head in range(2):
            s_t = lax.dot_general(ks[head], qs[head, rows, :], NT, preferred_element_type=F32)
            p_t = jnp.exp(s_t - lse_ref[0, 4 * head:4 * head + 1, rows])
            do_b = dos[head, rows, :]
            dp_t = lax.dot_general(v_ref[...], do_b, NT, preferred_element_type=F32)
            corr = jnp.sum(p_t * dp_t, axis=0, keepdims=True)
            ds_t = (p_t * (dp_t - corr)).astype(BF16)
            dv_acc[...] += jnp.dot(p_t.astype(BF16), do_b, preferred_element_type=F32)
            dk_acc[...] += jnp.dot(ds_t, qz[head, rows, :], preferred_element_type=F32)
            dqt[64 * head:64 * head + 64, rows] = jnp.dot(kt[64 * head:64 * head + 64, :], ds_t, preferred_element_type=F32)
        return carry

    lax.fori_loop(0, seq // QB, block, 0)
    cos, sin = cos_ref[...], sin_ref[...]
    dq, dk, dv = dqt[...].T, dk_acc[...], dv_acc[...]
    dq = (dq * cos - swap_halves(dq, first_half) * sin) * 0.125
    dk = dk * cos - swap_halves(dk, first_half) * sin
    d_all = jnp.concatenate([dq, dk, dv], axis=1)
    sums = jnp.sum(d_all, axis=0, keepdims=True)
    gb_ref[0] = jnp.concatenate([sums[:, :128], sums[:, 128:256], sums[:, 256:], jnp.zeros((5, 128), F32)], axis=0)
    d_low = d_all.astype(BF16)
    w = pair_rows(w0_ref, w1_ref)
    part = jnp.dot(d_low, w, preferred_element_type=F32)
    gw = jnp.dot(d_low.T, h_ref[...], preferred_element_type=F32)
    for i in range(3):
        gw0_ref[i] = gw[128 * i:128 * i + 64]
        gw1_ref[i] = gw[128 * i + 64:128 * i + 128]

    @pl.when(pl.program_id(0) == 0)
    def _():
        dh_ref[...] = part

    @pl.when(pl.program_id(0) > 0)
    def _():
        dh_ref[...] += part


def attn_bwd(h1, d_x1, w0, w1, wo0, wo1, q, k, v, o, lse, cos_tab, sin_tab, mask_col):
    seq, dim = h1.shape
    heads = w0.shape[1] // 64
    full = lambda i: (0, 0)
    pair = pl.BlockSpec((seq, 128), lambda i: (0, i))
    head_w = pl.BlockSpec((3, 64, dim), lambda i: (0, i, 0))
    head_o = pl.BlockSpec((1, 64, dim), lambda i: (i, 0, 0))
    tab = pl.BlockSpec((seq, 128), full)
    gw = jax.ShapeDtypeStruct((3, heads * 64, dim), F32)
    gwo = jax.ShapeDtypeStruct((heads, 64, dim), F32)
    half = pltpu.VMEM((2, seq, 128), BF16)
    return pl.pallas_call(
        attn_bwd_kernel,
        grid=(heads,),
        in_specs=[pl.BlockSpec((seq, dim), full), pl.BlockSpec((seq, dim), full), head_w, head_w, head_o, head_o, pair, pair, pair, pair,
                  pl.BlockSpec((1, 8, seq), lambda i: (i, 0, 0)), tab, tab, tab],
        out_specs=[pl.BlockSpec((seq, dim), full), head_w, head_w, head_o, head_o, pl.BlockSpec((1, 8, 128), lambda i: (i, 0, 0))],
        out_shape=[jax.ShapeDtypeStruct((seq, dim), F32), gw, gw, gwo, gwo, jax.ShapeDtypeStruct((heads, 8, 128), F32)],
        scratch_shapes=[half, half, half, half, pltpu.VMEM((128, seq), BF16), pltpu.VMEM((128, seq), F32),
                        pltpu.VMEM((seq, 128), F32), pltpu.VMEM((seq, 128), F32)],
        compiler_params=pltpu.CompilerParams(dimension_semantics=("arbitrary",), vmem_limit_bytes=VMEM_LIMIT),
        cost_estimate=pl.CostEstimate(flops=heads * 2 * seq * (dim * 1024 + 10 * seq * 256), bytes_accessed=40_000_000, transcendentals=0),
        name="attn_bwd",
    )(h1, d_x1, w0, w1, wo0, wo1, q, k, v, o, lse, cos_tab, sin_tab, mask_col)


def gelu_terms(pre):
    erf_term = lax.erf(pre * INV_SQRT2)
    act = 0.5 * pre * (1.0 + erf_term)
    slope = 0.5 * (1.0 + erf_term) + pre * jnp.exp(-0.5 * pre * pre) * INV_SQRT_2PI
    return act, slope


def mlp_kernel(tiles, n_w, *refs):
    h_ref, dy_ref, b_ref = refs[:3]
    up_refs, down_refs = refs[3:3 + n_w], refs[3 + n_w:3 + 2 * n_w]
    y_ref, dh_ref, wu, wd, sem = refs[3 + 2 * n_w:]
    seq = h_ref.shape[0]
    width = wu.shape[2]
    copies = []
    for t, (src, part) in enumerate(tiles):
        cols = pl.ds(part * width, width)
        copies.append((pltpu.make_async_copy(up_refs[src].at[:, cols], wu.at[t], sem.at[0, t]),
                       pltpu.make_async_copy(down_refs[src].at[cols, :], wd.at[t], sem.at[1, t])))
    for pair in copies:
        pair[0].start()
        pair[1].start()
    for t in range(len(tiles)):
        copies[t][0].wait()
        copies[t][1].wait()

        def block(j, carry, t=t):
            rows = pl.ds(pl.multiple_of(j * QB, QB), QB)
            pre = jnp.dot(h_ref[rows, :], wu[t], preferred_element_type=F32) + b_ref[t]
            act, slope = gelu_terms(pre)
            d_act = lax.dot_general(dy_ref[rows, :], wd[t], NT, preferred_element_type=F32)
            y_part = jnp.dot(act.astype(BF16), wd[t], preferred_element_type=F32)
            d_pre = (d_act * slope).astype(BF16)
            dh_part = lax.dot_general(d_pre, wu[t], NT, preferred_element_type=F32)
            if t == 0:
                y_ref[rows, :] = y_part
                dh_ref[rows, :] = dh_part
            else:
                y_ref[rows, :] += y_part
                dh_ref[rows, :] += dh_part
            return carry

        lax.fori_loop(0, seq // QB, block, 0)


def mlp_chain(h2, d_y, bias, ups, downs):
    seq, dim = h2.shape
    width = 640
    tiles = [(i, p) for i, w in enumerate(ups) for p in range(w.shape[1] // width)]
    vmem, hbm = pl.BlockSpec(memory_space=pltpu.VMEM), pl.BlockSpec(memory_space=pl.ANY)
    out = jax.ShapeDtypeStruct((seq, dim), F32)
    return pl.pallas_call(
        functools.partial(mlp_kernel, tiles, len(ups)),
        in_specs=[vmem, vmem, vmem] + [hbm] * (2 * len(ups)),
        out_specs=[vmem, vmem],
        out_shape=[out, out],
        scratch_shapes=[pltpu.VMEM((len(tiles), dim, width), BF16), pltpu.VMEM((len(tiles), width, dim), BF16),
                        pltpu.SemaphoreType.DMA((2, len(tiles)))],
        compiler_params=pltpu.CompilerParams(vmem_limit_bytes=VMEM_LIMIT),
        cost_estimate=pl.CostEstimate(flops=len(tiles) * 8 * seq * dim * width, bytes_accessed=30_000_000, transcendentals=0),
        name="mlp_chain",
    )(h2, d_y, bias.reshape(len(tiles), 1, width), *ups, *downs)


def xor_move(value, bits):
    return lax.ppermute(value, 'tp', [(i, i ^ bits) for i in range(4)])


def swap_groups(value):
    return lax.ppermute(value, 'dp', [(0, 1), (1, 0)])


def cross_halves(shard, axis, group):
    size = shard.shape[axis] // 2
    piece = xor_move(lax.dynamic_slice_in_dim(shard, group * size, size, axis), 2)
    return piece, swap_groups(piece)


def cross_ordered(shard, axis, group):
    here, there = cross_halves(shard, axis, group)
    return jnp.concatenate([jnp.where(group == 0, here, there), jnp.where(group == 0, there, here)], axis=axis)


def solution(mesh):
    act_spec = P('dp', 'tp', None)
    rep_vec = P(None)
    part_vec = P('dp')
    in_specs = (act_spec, act_spec, P('dp', None), rep_vec, rep_vec, P(None, None, 'tp', None), P(None, 'tp', None),
                P('tp', None, None), rep_vec, rep_vec, rep_vec, P(None, 'tp'), P('tp'), P('tp', None), rep_vec)
    out_specs = (act_spec, act_spec, part_vec, part_vec, P('dp', None, 'tp', None), P('dp', 'tp', None),
                 P(('dp', 'tp'), None, None), part_vec, part_vec, part_vec, P('dp', 'tp'), P(('dp', 'tp')),
                 P(('dp', 'tp'), None), part_vec)

    def device_step(x_in, grad_y, pad_mask, ln1_gain, ln1_bias, w_qkv, b_qkv, w_out, b_out, ln2_gain, ln2_bias, w_up, b_up, w_down, b_down):
        me = lax.axis_index('tp')
        group = lax.axis_index('dp')
        n_seq, rows, dim = x_in.shape
        seq = pad_mask.shape[1]
        heads = w_out.shape[0]
        cols = w_up.shape[1]
        cos_tab, sin_tab = rope_tables(seq, 64)

        def to_sequence(blocks):
            out = jnp.zeros((seq, dim), blocks.dtype)
            for s in range(4):
                mine = lax.dynamic_index_in_dim(blocks, me ^ s, 0, keepdims=False)
                got = xor_move(mine, s) if s else mine
                out = lax.dynamic_update_slice_in_dim(out, got, (me ^ s) * rows, 0)
            return out

        def to_blocks(value):
            out = jnp.zeros((n_seq, rows, dim), value.dtype)
            for s in range(4):
                mine = lax.dynamic_slice_in_dim(value, (me ^ s) * rows, rows, 0)
                got = xor_move(mine, s) if s else mine
                out = lax.dynamic_update_index_in_dim(out, got, me ^ s, 0)
            return out

        x_seq = to_sequence(x_in)
        wq = [jnp.transpose(w_qkv, (0, 2, 3, 1)).reshape(3, heads * 64, dim)]
        wq.append(xor_move(wq[0], 1))
        wq.append(cross_ordered(wq[0], 1, group))
        wq.append(xor_move(wq[2], 1))
        wo = [w_out]
        wo.append(xor_move(w_out, 1))
        wo.append(cross_ordered(w_out.reshape(heads * 64, dim), 0, group).reshape(heads, 64, dim))
        wo.append(xor_move(wo[2], 1))
        small = jnp.concatenate([b_up, b_qkv.reshape(-1)])
        smalls = [small] + [xor_move(small, s) for s in (1, 2, 3)]
        b_ups = [v[:cols] for v in smalls]
        b_qkvs = [v[cols:].reshape(3, heads, 64) for v in smalls]
        ups = [w_up, xor_move(w_up, 1)]
        downs = [w_down, xor_move(w_down, 1)]
        dy_full = lax.all_gather(grad_y, 'tp', axis=1, tiled=True)
        up_x = cross_halves(w_up, 1, group)
        down_x = cross_halves(w_down, 0, group)
        ups_x = list(up_x) + [xor_move(v, 1) for v in up_x]
        downs_x = list(down_x) + [xor_move(v, 1) for v in down_x]

        def ordered_bias(v):
            return jnp.where(group == 0, v, jnp.concatenate([v[cols // 2:], v[:cols // 2]]))

        my_mask = lax.dynamic_index_in_dim(pad_mask, me, 0, keepdims=False)
        mask_col = jnp.broadcast_to(jnp.where(my_mask > 0, 0.0, NEG_LARGE).astype(F32)[:, None], (seq, 128))
        x_f = x_seq.astype(F32)
        h1_f, x_hat1, inv_std1 = layer_norm(x_f, ln1_gain, ln1_bias)
        h1 = h1_f.astype(BF16)

        def pair_bias(a, b):
            return jnp.transpose(jnp.concatenate([a, b], axis=-1), (1, 0, 2))

        fwd = [attn_fwd(h1, wq[i], wq[i + 1], pair_bias(b_qkvs[i], b_qkvs[i + 1]), cos_tab, sin_tab, mask_col, wo[i], wo[i + 1])
               for i in (0, 2)]
        x1_f = (x_f + ((fwd[0][5] + fwd[1][5]) + b_out)).astype(BF16).astype(F32)
        h2_f, x_hat2, inv_std2 = layer_norm(x1_f, ln2_gain, ln2_bias)
        h2 = h2_f.astype(BF16)

        d_y = lax.dynamic_index_in_dim(dy_full, me, 0, keepdims=False)
        dy_f = d_y.astype(F32)
        y_a, dh2_a = mlp_chain(h2, d_y, jnp.concatenate([b_ups[0], b_ups[1]]), ups, downs)
        y_b, dh2_b = mlp_chain(h2, d_y, jnp.concatenate([ordered_bias(b_ups[2]), ordered_bias(b_ups[3])]), ups_x, downs_x)
        y_seq = (x1_f + ((y_a + y_b) + b_down)).astype(BF16)
        y_out = to_blocks(y_seq)
        d_h2 = dh2_a + dh2_b
        d_x1 = dy_f + layer_norm_grad(d_h2, x_hat2, inv_std2, ln2_gain)
        d_x1_b = d_x1.astype(BF16)

        bwd = {}
        for i in (2, 0):
            q, k, v, o, lse, _ = fwd[i // 2]
            bwd[i] = attn_bwd(h1, d_x1_b, wq[i], wq[i + 1], wo[i], wo[i + 1], q, k, v, o, lse, cos_tab, sin_tab, mask_col)
        far = [(bwd[2][1], bwd[2][2]), (bwd[2][3], bwd[2][4])]
        near = [(bwd[0][1], bwd[0][2]), (bwd[0][3], bwd[0][4])]
        grads = []
        for (far2, far3), (near0, near1) in zip(far, near):
            across = xor_move(far2 + xor_move(far3, 1), 2)
            grads.append((near0 + xor_move(near1, 1)) + across)
        grad_w_qkv = jnp.transpose(grads[0].reshape(3, heads, 64, dim), (0, 3, 1, 2))
        grad_w_out = grads[1]
        d_h1 = bwd[2][0] + bwd[0][0]
        grad_x_seq = (d_x1 + layer_norm_grad(d_h1, x_hat1, inv_std1, ln1_gain)).astype(BF16)
        grad_x = to_blocks(grad_x_seq)
        gb = []
        for i in (0, 2):
            part = jnp.transpose(bwd[i][5][:, :3], (1, 0, 2))
            gb += [part[..., :64], part[..., 64:]]
        grad_b_qkv = (gb[0] + xor_move(gb[1], 1)) + (xor_move(gb[2], 2) + xor_move(gb[3], 3))

        h2_full = lax.all_gather(h2[None], 'tp', axis=0, tiled=True)
        pre_act = jnp.einsum('bsd,df->bsf', h2_full, w_up, preferred_element_type=F32) + b_up
        act, gelu_slope = gelu_terms(pre_act)
        act_b = act.astype(BF16)
        grad_w_down = jnp.einsum('bsf,bsd->fd', act_b, dy_full, preferred_element_type=F32)
        d_act = jnp.einsum('bsd,fd->bsf', dy_full, w_down, preferred_element_type=F32)
        d_pre = d_act * gelu_slope
        grad_b_up = jnp.sum(d_pre, axis=(0, 1))
        grad_w_up = jnp.einsum('bsd,bsf->df', h2_full, d_pre.astype(BF16), preferred_element_type=F32)

        sums = jnp.stack([jnp.sum(dy_f, axis=0), jnp.sum(d_h2 * x_hat2, axis=0), jnp.sum(d_h2, axis=0), jnp.sum(d_x1, axis=0),
                          jnp.sum(d_h1 * x_hat1, axis=0), jnp.sum(d_h1, axis=0)])
        sums = sums + xor_move(sums, 1)
        sums = sums + xor_move(sums, 2)
        return (y_out, grad_x, sums[4], sums[5], grad_w_qkv, grad_b_qkv, grad_w_out, sums[3],
                sums[1], sums[2], grad_w_up, grad_b_up, grad_w_down, sums[0])

    return jax.shard_map(device_step, mesh=mesh, in_specs=in_specs, out_specs=out_specs, check_vma=False)
```

time: 1310 us -> 810 us (0.62)
  waiting for transfers between devices: 694 us -> 256 us
  matrix products: 427 us -> 85.4 us
  Pallas kernels: 0 us -> 328 us
  other arithmetic: 140 us -> 68.5 us
  starting transfers between devices: 1.29 us -> 25.6 us
    reduce_scatter x4 -> x0, waiting for transfers between devices: 482 us -> none  [the longest x1 144 us: device_step(): lax.psum_scatter(attn_part, 'tp', scatter_dimension=1, tiled=True)]
    pallas_call x0 -> x6, Pallas kernels: none -> 328 us  [the longest x2 141 us: attn_bwd(): pl.pallas_call(attn_bwd_kernel, grid=(heads,), in_specs=[pl.BlockSpec((se...]
    dot_general x17 -> x4, matrix products: 352 us -> 85.4 us  [the longest x1 24.2 us: device_step(): jnp.einsum('bsd,fd->bsf', dy_full, w_down, preferred_element_type=F32)]
    ppermute x0 -> x41, waiting for transfers between devices: none -> 256 us  [the longest x37 215 us: xor_move(): return lax.ppermute(value, 'tp', [(i, i ^ bits) for i in range(4)])]
    all_gather x3 -> x1, waiting for transfers between devices: 162 us -> 0.01 us  [device_step(): h2_full = lax.all_gather(h2[None], 'tp', axis=0, tiled=True)]
    convert_element_type x6 -> x4, other arithmetic: 89.1 us -> 12 us  [the longest x1 5.24 us: device_step(): (d_x1 + layer_norm_grad(d_h1, x_hat1, inv_std1, ln1_gain)).astype(BF16)]
    sub x2 -> x0, matrix products: 75.2 us -> none  [device_step(): attn_probs = jax.nn.softmax(jnp.where(key_ok, scores, NEG_LARGE), axis=-1)]
    all_gather x1, waiting for transfers between devices: 49.1 us -> 0.02 us  [device_step(): dy_full = lax.all_gather(grad_y, 'tp', axis=1, tiled=True)]
  transfers between devices with their start and end apart: 8 -> 43, of which waited for: 8 -> 10; matrix products, arithmetic and copies ran while one was open for 12% -> 21% of each run, Pallas kernels for 0% -> 41%
where the time goes in v1:
time: 810 us; the launch traced here: 804 us
  Pallas kernels  328 us (40%)
  waiting for transfers between devices  256 us (32%)
  matrix products  85.4 us (11%)
  other arithmetic  68.5 us (8%)
  starting transfers between devices  25.6 us (3%)
  local copies, waits for them, and re-layouts  24.3 us (3%)
  between operations  15.3 us (2%)
    ppermute x37, waiting for transfers between devices, xor_move(): return lax.ppermute(value, 'tp', [(i, i ^ bits) for i in range(4)])  215 us
    pallas_call x2, Pallas kernels, attn_bwd(): pl.pallas_call(attn_bwd_kernel, grid=(heads,), in_specs=[pl.BlockSpec((se...  141 us
    pallas_call x2, Pallas kernels, attn_fwd(): pl.pallas_call(attn_fwd_kernel, grid=(heads,), in_specs=[pl.BlockSpec((se...  98.7 us
    pallas_call x2, Pallas kernels, mlp_chain(): pl.pallas_call(functools.partial(mlp_kernel, tiles, len(ups)), in_specs=[...  88.9 us
    ppermute x4, waiting for transfers between devices, swap_groups(): return lax.ppermute(value, 'dp', [(0, 1), (1, 0)])  40.8 us
    dot_general x1, matrix products, device_step(): jnp.einsum('bsd,fd->bsf', dy_full, w_down, preferred_element_type=F32)  24.2 us
    dot_general x1, matrix products, device_step(): jnp.einsum('bsf,bsd->fd', act_b, dy_full, preferred_element_type=F32)  23.1 us
    ppermute x37, starting transfers between devices, xor_move(): return lax.ppermute(value, 'tp', [(i, i ^ bits) for i in range(4)])  21.4 us
  transfers between devices with their start and end apart: 43, of which 10 were waited for; matrix products, arithmetic and copies ran while one was open for 21% of the time, Pallas kernels for 41%

profile of v1, /device:TPU:0, one launch (start us, length us, event | category | flops | bytes accessed | tf_op | source)
XLA Modules:
  0.0 803.9 jit_solution(7743577105208003046)
XLA Ops:
  36.7 24.6 %collective-permute-done.1 = bf16[256,1280]{1,0:T(8,128)(2,1)} collective-permute-done((bf16[256,1280]{1,0:T(8,128)(2,1)}, bf16[256,1280]{1,0:T(8,128)(2,1)}, u32[]{:S(2)}, u32[]{:S(2)}) %collective-permute-start.1) | collective-permute-done | bytes 655392 | tf_op jit(solution)/shard_map/ppermute | solution.py:281
  62.4 79.3 %collective-permute-done.11 = bf16[160,1280]{1,0:T(8,128)(2,1)S(1)} collective-permute-done((bf16[160,1280]{1,0:T(8,128)(2,1)}, bf16[160,1280]{1,0:T(8,128)(2,1)S(1)}, u32[]{:S(2)}, u32[]{:S(2)}) %collective-permute-start.11) | collective-permute-done | bytes 409632 | tf_op jit(solution)/shard_map/ppermute | solution.py:281
  146.5 32.8 %collective-permute-done.7 = bf16[3,160,1280]{2,1,0:T(8,128)(2,1)S(1)} collective-permute-done((bf16[3,160,1280]{2,1,0:T(8,128)(2,1)}, bf16[3,160,1280]{2,1,0:T(8,128)(2,1)S(1)}, u32[]{:S(2)}, u32[]{:S(2)}) %collective-permute-start.7) | collective-permute-done | bytes 1228832 | tf_op jit(solution)/shard_map/ppermute | solution.py:285
  188.3 49.5 %attn_fwd.2 = (bf16[1024,640]{1,0:T(8,128)(2,1)}, bf16[1024,640]{1,0:T(8,128)(2,1)}, bf16[1024,640]{1,0:T(8,128)(2,1)}, bf16[1024,640]{1,0:T(8,128)(2,1)}, f32[5,8,1024]{2,1,0:T(8,128)}, /*index=5*/f32[1024,1280]{1,0:T(8,128)}) custom-call(bf16[1024,1280]{1,0:T(8,128)(2,1)} %fusion.32.h_ref, bf16[3,320,1280]{2,1,0:T(8,128)(2,1)} %bitcast.5.w0_ref, ...), custom_call_target="tpu_custom_call" | custom-call | flops 17448304640 | bytes 20000000 | tf_op jit(solution)/shard_map/attn_fwd/pallas_call | solution.py:113
  240.2 49.2 %attn_fwd.3 = (bf16[1024,640]{1,0:T(8,128)(2,1)}, bf16[1024,640]{1,0:T(8,128)(2,1)}, bf16[1024,640]{1,0:T(8,128)(2,1)}, bf16[1024,640]{1,0:T(8,128)(2,1)}, f32[5,8,1024]{2,1,0:T(8,128)}, /*index=5*/f32[1024,1280]{1,0:T(8,128)}) custom-call(bf16[1024,1280]{1,0:T(8,128)(2,1)} %fusion.32.h_ref, bf16[3,320,1280]{2,1,0:T(8,128)(2,1)} %pad_maximum_fusion.w0_ref, ...), custom_call_target="tpu_custom_call" | custom-call | flops 17448304640 | bytes 20000000 | tf_op jit(solution)/shard_map/attn_fwd/pallas_call | solution.py:113
  303.2 8.1 %collective-permute-done.21.refs_8_ = bf16[640,1280]{1,0:T(8,128)(2,1)} collective-permute-done((bf16[640,1280]{1,0:T(8,128)(2,1)}, bf16[640,1280]{1,0:T(8,128)(2,1)}, u32[]{:S(2)}, u32[]{:S(2)}) %collective-permute-start.21) | collective-permute-done | bytes 1638432 | tf_op jit(solution)/shard_map/ppermute | solution.py:285
  311.7 44.3 %mlp_chain.2 = (f32[1024,1280]{1,0:T(8,128)}, f32[1024,1280]{1,0:T(8,128)}) custom-call(bf16[1024,1280]{1,0:T(8,128)(2,1)} %fusion.25.refs_0_, bf16[1024,1280]{1,0:T(8,128)(2,1)} %get-tuple-element.87.refs_1_, f32[4,1,640]{2,1,0:T(1,128)} %pad_maximum_fusion.4.refs_2_, bf16[1280,1280]{1,0:T(8,128)(2,1)} %refs_3_.1, ...), custom_call_target="tpu_custom_call" | custom-call | flops 26843545600 | bytes 30000000 | tf_op jit(solution)/shard_map/mlp_chain/pallas_call | solution.py:267
  356.1 44.6 %mlp_chain.3 = (f32[1024,1280]{1,0:T(8,128)}, f32[1024,1280]{1,0:T(8,128)}) custom-call(bf16[1024,1280]{1,0:T(8,128)(2,1)} %fusion.25.refs_0_, bf16[1024,1280]{1,0:T(8,128)(2,1)} %get-tuple-element.87.refs_1_, f32[4,1,640]{2,1,0:T(1,128)} %pad_maximum_fusion.5.refs_2_, bf16[1280,640]{1,0:T(8,128)(2,1)} %collective-permute-done.16.refs_3_, ...), custom_call_target="tpu_custom_call" | custom-call | flops 26843545600 | bytes 30000000 | tf_op jit(solution)/shard_map/mlp_chain/pallas_call | solution.py:267
  400.8 5.7 fusion.29
  407.1 5.6 fusion.49
  416.8 70.4 %attn_bwd.2 = (f32[1024,1280]{1,0:T(8,128)}, f32[3,320,1280]{2,1,0:T(8,128)}, f32[3,320,1280]{2,1,0:T(8,128)}, f32[5,64,1280]{2,1,0:T(8,128)}, f32[5,64,1280]{2,1,0:T(8,128)}, /*index=5*/f32[5,8,128]{2,1,0:T(8,128)}) custom-call(bf16[1024,1280]{1,0:T(8,128)(2,1)} %fusion.32.h_ref, bf16[1024,1280]{1,0:T(8,128)(2,1)} %convert_element_type.40.dx_ref, ...), custom_call_target="tpu_custom_call" | custom-call | flops 40265318400 | bytes 40000000 | tf_op jit(solution)/shard_map/attn_bwd/pallas_call | solution.py:202
  487.3 70.2 %attn_bwd.3 = (f32[1024,1280]{1,0:T(8,128)}, f32[3,320,1280]{2,1,0:T(8,128)}, f32[3,320,1280]{2,1,0:T(8,128)}, f32[5,64,1280]{2,1,0:T(8,128)}, f32[5,64,1280]{2,1,0:T(8,128)}, /*index=5*/f32[5,8,128]{2,1,0:T(8,128)}) custom-call(bf16[1024,1280]{1,0:T(8,128)(2,1)} %fusion.32.h_ref, bf16[1024,1280]{1,0:T(8,128)(2,1)} %convert_element_type.40.dx_ref, ...), custom_call_target="tpu_custom_call" | custom-call | flops 40265318400 | bytes 40000000 | tf_op jit(solution)/shard_map/attn_bwd/pallas_call | solution.py:202
  558.9 7.0 fusion.38
  580.1 13.8 %collective-permute-done.31 = f32[6,1280]{1,0:T(8,128)S(1)} collective-permute-done((f32[6,1280]{1,0:T(8,128)S(1)}, f32[6,1280]{1,0:T(8,128)S(1)}, u32[]{:S(2)}, u32[]{:S(2)}) %collective-permute-start.31) | collective-permute-done | bytes 30752 | tf_op jit(solution)/shard_map/ppermute | solution.py:281
  598.7 12.2 %collective-permute-done.29 = bf16[256,1280]{1,0:T(8,128)(2,1)S(1)} collective-permute-done((bf16[256,1280]{1,0:T(8,128)(2,1)S(1)}, bf16[256,1280]{1,0:T(8,128)(2,1)S(1)}, u32[]{:S(2)}, u32[]{:S(2)}) %collective-permute-start.29) | collective-permute-done | bytes 655392 | tf_op jit(solution)/shard_map/ppermute | solution.py:281
  613.6 12.7 %collective-permute-done.25 = bf16[256,1280]{1,0:T(8,128)(2,1)S(1)} collective-permute-done((bf16[256,1280]{1,0:T(8,128)(2,1)S(1)}, bf16[256,1280]{1,0:T(8,128)(2,1)S(1)}, u32[]{:S(2)}, u32[]{:S(2)}) %collective-permute-start.25) | collective-permute-done | bytes 655392 | tf_op jit(solution)/shard_map/ppermute | solution.py:281
  626.4 47.7 %collective-permute-done.26 = bf16[256,1280]{1,0:T(8,128)(2,1)S(1)} collective-permute-done((bf16[256,1280]{1,0:T(8,128)(2,1)S(1)}, bf16[256,1280]{1,0:T(8,128)(2,1)S(1)}, u32[]{:S(2)}, u32[]{:S(2)}) %collective-permute-start.26) | collective-permute-done | bytes 655392 | tf_op jit(solution)/shard_map/ppermute | solution.py:281
  675.9 5.2 add.205
  681.6 20.4 %convolution_add_fusion = f32[4,1024,1280]{2,1,0:T(8,128)} fusion(bf16[4,1024,1280]{2,1,0:T(8,128)(2,1)} %bitcast.72, f32[1280]{0:T(1024)S(1)} %copy-done.26, bf16[1280,1280]{1,0:T(8,128)(2,1)} %refs_3_.1), kind=kOutput, calls=%fused_computation.8 | convolution fusion | flops 13427015680 | bytes 34739200 | tf_op jit(solution)/shard_map/bsd,df->bsf/dot_general | solution.py:405
  702.0 24.2 %fusion.54 = (f32[1280]{0:T(1024)}, bf16[4,1024,1280]{2,1,0:T(8,128)(2,1)}) fusion(f32[4,1024,1280]{2,1,0:T(8,128)} %convolution_add_fusion, bf16[4,1024,1280]{2,1,0:T(8,128)(2,1)} %all-gather.4.cloned.1.call-done, bf16[1280,1280]{1,0:T(8,128)(2,1)S(1)} %copy-done.14), kind=kOutput, calls=%fused_computation.131 | convolution fusion | flops 13479443456 | bytes 45224960 | tf_op jit(solution)/shard_map/bsd,fd->bsf/dot_general | solution.py:409
  726.2 17.6 %fusion.8 = f32[1280,1280]{1,0:T(8,128)} fusion(bf16[4,1024,1280]{2,1,0:T(8,128)(2,1)S(1)} %bitcast.75, bf16[4,1024,1280]{2,1,0:T(8,128)(2,1)} %get-tuple-element.116), kind=kOutput, calls=%fused_computation.13 | convolution fusion | flops 13421772800 | bytes 27525120 | tf_op jit(solution)/shard_map/bsd,bsf->df/dot_general | solution.py:412
  743.9 23.1 %fusion.11 = f32[1280,1280]{1,0:T(8,128)} fusion(bf16[4,1024,1280]{2,1,0:T(8,128)(2,1)} %all-gather.4.cloned.1.call-done, f32[4,1024,1280]{2,1,0:T(8,128)} %convolution_add_fusion), kind=kOutput, calls=%fused_computation.14 | convolution fusion | flops 13447987200 | bytes 38010880 | tf_op jit(solution)/shard_map/bsf,bsd->fd/dot_general | solution.py:408
  767.0 22.6 %collective-permute-done.34 = f32[3,320,1280]{2,1,0:T(8,128)} collective-permute-done((f32[3,320,1280]{2,1,0:T(8,128)}, f32[3,320,1280]{2,1,0:T(8,128)}, u32[]{:S(2)}, u32[]{:S(2)}) %collective-permute-start.34) | collective-permute-done | bytes 4915232 | tf_op jit(solution)/shard_map/ppermute | solution.py:281
  789.6 7.1 add_add_fusion
  (261 shorter events, 90.6 us)
Async XLA Ops:
  7.2 291.4 %all-gather.4.cloned.1.call-start = ((), (), s32[]{:S(2)}) async-start(), calls=%async_computation | async-start | bytes 13107200 | tf_op jit(solution)/shard_map/all_gather | solution.py:349
  7.9 673.7 %all-gather.6.cloned.1.call-start = ((), (), s32[]{:S(2)}) async-start(), calls=%async_computation.1 | async-start | bytes 13107200 | tf_op jit(solution)/shard_map/all_gather | solution.py:404
  16.1 170.9 %collective-permute-start.3 = (bf16[3,320,1280]{2,1,0:T(8,128)(2,1)}, bf16[3,320,1280]{2,1,0:T(8,128)(2,1)}, u32[]{:S(2)}, u32[]{:S(2)}) collective-permute-start(bf16[3,320,1280]{2,1,0:T(8,128)(2,1)} %bitcast.5.w0_ref), channel_id=1, source_target_pairs={{0,1},{1,0},{2,3},{3,2},{4,5},{5,4},{6,7},{7,6}} | collective-permute-start | bytes 7372808 | tf_op jit(solution)/shard_map/ppermute | solution.py:281
  31.6 112.1 %collective-permute-start.6 = (bf16[3,160,1280]{2,1,0:T(8,128)(2,1)}, bf16[3,160,1280]{2,1,0:T(8,128)(2,1)}, u32[]{:S(2)}, u32[]{:S(2)}) collective-permute-start(bf16[3,160,1280]{2,1,0:T(8,128)(2,1)} %constant_dynamic-slice_fusion.9), channel_id=1, source_target_pairs={{0,2},{1,3},{2,0},{3,1},{4,6},{5,7},{6,4},{7,5}} | collective-permute-start | bytes 3686408 | tf_op jit(solution)/shard_map/ppermute | solution.py:281
  31.8 110.2 %collective-permute-start.2 = (bf16[256,1280]{1,0:T(8,128)(2,1)}, bf16[256,1280]{1,0:T(8,128)(2,1)}, u32[]{:S(2)}, u32[]{:S(2)}) collective-permute-start(bf16[256,1280]{1,0:T(8,128)(2,1)} %get-tuple-element.99), channel_id=1, source_target_pairs={{0,3},{1,2},{2,1},{3,0},{4,7},{5,6},{6,5},{7,4}} | collective-permute-start | bytes 1966088 | tf_op jit(solution)/shard_map/ppermute | solution.py:281
  35.6 106.0 %collective-permute-start.11 = (bf16[160,1280]{1,0:T(8,128)(2,1)}, bf16[160,1280]{1,0:T(8,128)(2,1)S(1)}, u32[]{:S(2)}, u32[]{:S(2)}) collective-permute-start(bf16[160,1280]{1,0:T(8,128)(2,1)} %constant_dynamic-slice_fusion.8), channel_id=1, source_target_pairs={{0,2},{1,3},{2,0},{3,1},{4,6},{5,7},{6,4},{7,5}} | collective-permute-start | bytes 1228808 | tf_op jit(solution)/shard_map/ppermute | solution.py:281
  61.3 125.5 %collective-permute-start.5 = (bf16[5,64,1280]{2,1,0:T(8,128)(2,1)}, bf16[5,64,1280]{2,1,0:T(8,128)(2,1)S(1)}, u32[]{:S(2)}, u32[]{:S(2)}) collective-permute-start(bf16[5,64,1280]{2,1,0:T(8,128)(2,1)} %wo0_ref.3), channel_id=1, source_target_pairs={{0,1},{1,0},{2,3},{3,2},{4,5},{5,4},{6,7},{7,6}} | collective-permute-start | bytes 2457608 | tf_op jit(solution)/shard_map/ppermute | solution.py:281
  141.7 96.5 %collective-permute-start.16 = (bf16[1280,640]{1,0:T(8,128)(2,1)}, bf16[1280,640]{1,0:T(8,128)(2,1)}, u32[]{:S(2)}, u32[]{:S(2)}) collective-permute-start(bf16[1280,640]{1,0:T(8,128)(2,1)} %constant_dynamic-slice_fusion.7), channel_id=1, source_target_pairs={{0,2},{1,3},{2,0},{3,1},{4,6},{5,7},{6,4},{7,5}} | collective-permute-start | bytes 4915208 | tf_op jit(solution)/shard_map/ppermute | solution.py:281
  182.3 57.2 %collective-permute-start.8 = (bf16[3,320,1280]{2,1,0:T(8,128)(2,1)}, bf16[3,320,1280]{2,1,0:T(8,128)(2,1)}, u32[]{:S(2)}, u32[]{:S(2)}) collective-permute-start(bf16[3,320,1280]{2,1,0:T(8,128)(2,1)} %pad_maximum_fusion.w0_ref), channel_id=1, source_target_pairs={{0,1},{1,0},{2,3},{3,2},{4,5},{5,4},{6,7},{7,6}} | collective-permute-start | bytes 7372808 | tf_op jit(solution)/shard_map/ppermute | solution.py:281
  184.9 54.6 %collective-permute-start.20 = (bf16[640,1280]{1,0:T(8,128)(2,1)}, bf16[640,1280]{1,0:T(8,128)(2,1)}, u32[]{:S(2)}, u32[]{:S(2)}) collective-permute-start(bf16[640,1280]{1,0:T(8,128)(2,1)} %constant_dynamic-slice_fusion.6), channel_id=1, source_target_pairs={{0,2},{1,3},{2,0},{3,1},{4,6},{5,7},{6,4},{7,5}} | collective-permute-start | bytes 4915208 | tf_op jit(solution)/shard_map/ppermute | solution.py:281
  186.8 124.5 %collective-permute-start.14 = (bf16[1280,1280]{1,0:T(8,128)(2,1)}, bf16[1280,1280]{1,0:T(8,128)(2,1)}, u32[]{:S(2)}, u32[]{:S(2)}) collective-permute-start(bf16[1280,1280]{1,0:T(8,128)(2,1)} %refs_3_.1), channel_id=1, source_target_pairs={{0,1},{1,0},{2,3},{3,2},{4,5},{5,4},{6,7},{7,6}} | collective-permute-start | bytes 9830408 | tf_op jit(solution)/shard_map/ppermute | solution.py:281
  187.0 50.9 %collective-permute-start.13 = (bf16[5,64,1280]{2,1,0:T(8,128)(2,1)S(1)}, bf16[5,64,1280]{2,1,0:T(8,128)(2,1)}, u32[]{:S(2)}, u32[]{:S(2)}) collective-permute-start(bf16[5,64,1280]{2,1,0:T(8,128)(2,1)S(1)} %bitcast.67), channel_id=1, source_target_pairs={{0,1},{1,0},{2,3},{3,2},{4,5},{5,4},{6,7},{7,6}} | collective-permute-start | bytes 2457608 | tf_op jit(solution)/shard_map/ppermute | solution.py:281
  237.9 73.9 %collective-permute-start.15 = (bf16[1280,1280]{1,0:T(8,128)(2,1)}, bf16[1280,1280]{1,0:T(8,128)(2,1)}, u32[]{:S(2)}, u32[]{:S(2)}) collective-permute-start(bf16[1280,1280]{1,0:T(8,128)(2,1)} %refs_5_.1), channel_id=1, source_target_pairs={{0,1},{1,0},{2,3},{3,2},{4,5},{5,4},{6,7},{7,6}} | collective-permute-start | bytes 9830408 | tf_op jit(solution)/shard_map/ppermute | solution.py:281
  238.2 64.8 %collective-permute-start.17 = (bf16[1280,640]{1,0:T(8,128)(2,1)}, bf16[1280,640]{1,0:T(8,128)(2,1)}, u32[]{:S(2)}, u32[]{:S(2)}) collective-permute-start(bf16[1280,640]{1,0:T(8,128)(2,1)} %collective-permute-done.16.refs_3_), channel_id=1, source_target_pairs={{0,4},{4,0},{1,5},{5,1},{2,6},{6,2},{3,7},{7,3}} | collective-permute-start | bytes 4915208 | tf_op jit(solution)/shard_map/ppermute | solution.py:285
  239.5 116.6 %collective-permute-start.18 = (bf16[1280,640]{1,0:T(8,128)(2,1)}, bf16[1280,640]{1,0:T(8,128)(2,1)}, u32[]{:S(2)}, u32[]{:S(2)}) collective-permute-start(bf16[1280,640]{1,0:T(8,128)(2,1)} %collective-permute-done.16.refs_3_), channel_id=1, source_target_pairs={{0,1},{1,0},{2,3},{3,2},{4,5},{5,4},{6,7},{7,6}} | collective-permute-start | bytes 4915208 | tf_op jit(solution)/shard_map/ppermute | solution.py:281
  239.5 71.7 %collective-permute-start.21 = (bf16[640,1280]{1,0:T(8,128)(2,1)}, bf16[640,1280]{1,0:T(8,128)(2,1)}, u32[]{:S(2)}, u32[]{:S(2)}) collective-permute-start(bf16[640,1280]{1,0:T(8,128)(2,1)} %collective-permute-done.20.refs_7_), channel_id=1, source_target_pairs={{0,4},{4,0},{1,5},{5,1},{2,6},{6,2},{3,7},{7,3}} | collective-permute-start | bytes 4915208 | tf_op jit(solution)/shard_map/ppermute | solution.py:285
  303.0 53.1 %collective-permute-start.22 = (bf16[640,1280]{1,0:T(8,128)(2,1)}, bf16[640,1280]{1,0:T(8,128)(2,1)}, u32[]{:S(2)}, u32[]{:S(2)}) collective-permute-start(bf16[640,1280]{1,0:T(8,128)(2,1)} %collective-permute-done.20.refs_7_), channel_id=1, source_target_pairs={{0,1},{1,0},{2,3},{3,2},{4,5},{5,4},{6,7},{7,6}} | collective-permute-start | bytes 4915208 | tf_op jit(solution)/shard_map/ppermute | solution.py:281
  487.3 107.9 %collective-permute-start.39 = (f32[5,64,1280]{2,1,0:T(8,128)}, f32[5,64,1280]{2,1,0:T(8,128)}, u32[]{:S(2)}, u32[]{:S(2)}) collective-permute-start(f32[5,64,1280]{2,1,0:T(8,128)} %get-tuple-element.69), channel_id=1, source_target_pairs={{0,1},{1,0},{2,3},{3,2},{4,5},{5,4},{6,7},{7,6}} | collective-permute-start | bytes 4915208 | tf_op jit(solution)/shard_map/ppermute | solution.py:281
  558.8 117.0 %collective-permute-start.33 = (f32[3,320,1280]{2,1,0:T(8,128)}, f32[3,320,1280]{2,1,0:T(8,128)}, u32[]{:S(2)}, u32[]{:S(2)}) collective-permute-start(f32[3,320,1280]{2,1,0:T(8,128)} %get-tuple-element.63), channel_id=1, source_target_pairs={{0,1},{1,0},{2,3},{3,2},{4,5},{5,4},{6,7},{7,6}} | collective-permute-start | bytes 14745608 | tf_op jit(solution)/shard_map/ppermute | solution.py:281
  593.8 80.3 %collective-permute-start.38 = (f32[5,64,1280]{2,1,0:T(8,128)S(1)}, f32[5,64,1280]{2,1,0:T(8,128)S(1)}, u32[]{:S(2)}, u32[]{:S(2)}) collective-permute-start(f32[5,64,1280]{2,1,0:T(8,128)S(1)} %copy-done.32), channel_id=1, source_target_pairs={{0,1},{1,0},{2,3},{3,2},{4,5},{5,4},{6,7},{7,6}} | collective-permute-start | bytes 4915208 | tf_op jit(solution)/shard_map/ppermute | solution.py:281
  610.9 63.3 %collective-permute-start.40 = (f32[5,64,1280]{2,1,0:T(8,128)S(1)}, f32[5,64,1280]{2,1,0:T(8,128)S(1)}, u32[]{:S(2)}, u32[]{:S(2)}) collective-permute-start(f32[5,64,1280]{2,1,0:T(8,128)S(1)} %add.211), channel_id=1, source_target_pairs={{0,2},{1,3},{2,0},{3,1},{4,6},{5,7},{6,4},{7,5}} | collective-permute-start | bytes 4915208 | tf_op jit(solution)/shard_map/ppermute | solution.py:281
  611.9 62.2 %collective-permute-start.26 = (bf16[256,1280]{1,0:T(8,128)(2,1)S(1)}, bf16[256,1280]{1,0:T(8,128)(2,1)S(1)}, u32[]{:S(2)}, u32[]{:S(2)}) collective-permute-start(bf16[256,1280]{1,0:T(8,128)(2,1)S(1)} %get-tuple-element.96), channel_id=1, source_target_pairs={{0,3},{1,2},{2,1},{3,0},{4,7},{5,6},{6,5},{7,4}} | collective-permute-start | bytes 1966088 | tf_op jit(solution)/shard_map/ppermute | solution.py:281
  626.3 140.7 %collective-permute-start.32 = (f32[3,320,1280]{2,1,0:T(8,128)}, f32[3,320,1280]{2,1,0:T(8,128)}, u32[]{:S(2)}, u32[]{:S(2)}) collective-permute-start(f32[3,320,1280]{2,1,0:T(8,128)} %get-tuple-element.61), channel_id=1, source_target_pairs={{0,1},{1,0},{2,3},{3,2},{4,5},{5,4},{6,7},{7,6}} | collective-permute-start | bytes 14745608 | tf_op jit(solution)/shard_map/ppermute | solution.py:281
  681.1 108.4 %collective-permute-start.34 = (f32[3,320,1280]{2,1,0:T(8,128)}, f32[3,320,1280]{2,1,0:T(8,128)}, u32[]{:S(2)}, u32[]{:S(2)}) collective-permute-start(f32[3,320,1280]{2,1,0:T(8,128)} %add.205), channel_id=1, source_target_pairs={{0,2},{1,3},{2,0},{3,1},{4,6},{5,7},{6,4},{7,5}} | collective-permute-start | bytes 14745608 | tf_op jit(solution)/shard_map/ppermute | solution.py:281
  (60 other events, 1902.9 us)
Sparse Core Ops, SparseCore 0:
  9.5 116.8 all-gather.3
  298.7 67.6 all-gather.5

commit v2 on v1

--- a/solution.py
+++ b/solution.py
@@ -6,6 +6,7 @@
 from jax.experimental import pallas as pl
 from jax.experimental.pallas import tpu as pltpu
 from jax.sharding import PartitionSpec as P
+
 
 LN_EPS = 1e-5
 ROPE_BASE = 10000.0
@@ -126,7 +127,7 @@
 
 def attn_bwd_kernel(h_ref, dx_ref, w0_ref, w1_ref, wo0_ref, wo1_ref, q_ref, k_ref, v_ref, o_ref, lse_ref, cos_ref, sin_ref, mb_ref,
                     dh_ref, gw0_ref, gw1_ref, gwo0_ref, gwo1_ref, gb_ref, qs, qz, ks, dos, kt, dqt, dk_acc, dv_acc):
-    seq, dim = h_ref.shape
+    seq, _ = h_ref.shape
     lane = lax.broadcasted_iota(jnp.int32, (1, 128), 1)
     first_half = (lane % 64) < 32
     head0 = lane < 64
@@ -285,15 +286,8 @@
     return lax.ppermute(value, 'dp', [(0, 1), (1, 0)])
 
 
-def cross_halves(shard, axis, group):
-    size = shard.shape[axis] // 2
-    piece = xor_move(lax.dynamic_slice_in_dim(shard, group * size, size, axis), 2)
-    return piece, swap_groups(piece)
-
-
-def cross_ordered(shard, axis, group):
-    here, there = cross_halves(shard, axis, group)
-    return jnp.concatenate([jnp.where(group == 0, here, there), jnp.where(group == 0, there, here)], axis=axis)
+def after(value, *others):
+    return lax.optimization_barrier((value,) + others)[0]
 
 
 def solution(mesh):
@@ -306,54 +300,46 @@
                  P(('dp', 'tp'), None, None), part_vec, part_vec, part_vec, P('dp', 'tp'), P(('dp', 'tp')),
                  P(('dp', 'tp'), None), part_vec)
 
-    def device_step(x_in, grad_y, pad_mask, ln1_gain, ln1_bias, w_qkv, b_qkv, w_out, b_out, ln2_gain, ln2_bias, w_up, b_up, w_down, b_down):
+    def layer(x_in, grad_y, pad_mask, ln1_gain, ln1_bias, w_qkv, b_qkv, w_out, b_out, ln2_gain, ln2_bias, w_up, b_up, w_down, b_down):
         me = lax.axis_index('tp')
         group = lax.axis_index('dp')
+        core, far_chip = me % 2, 1 - me // 2
         n_seq, rows, dim = x_in.shape
         seq = pad_mask.shape[1]
         heads = w_out.shape[0]
         cols = w_up.shape[1]
-        cos_tab, sin_tab = rope_tables(seq, 64)
-
-        def to_sequence(blocks):
-            out = jnp.zeros((seq, dim), blocks.dtype)
-            for s in range(4):
-                mine = lax.dynamic_index_in_dim(blocks, me ^ s, 0, keepdims=False)
-                got = xor_move(mine, s) if s else mine
-                out = lax.dynamic_update_slice_in_dim(out, got, (me ^ s) * rows, 0)
-            return out
+        half = cols // 2
 
         def to_blocks(value):
             out = jnp.zeros((n_seq, rows, dim), value.dtype)
-            for s in range(4):
+            for s in (0, 2, 3, 1):
                 mine = lax.dynamic_slice_in_dim(value, (me ^ s) * rows, rows, 0)
                 got = xor_move(mine, s) if s else mine
                 out = lax.dynamic_update_index_in_dim(out, got, me ^ s, 0)
             return out
 
-        x_seq = to_sequence(x_in)
-        wq = [jnp.transpose(w_qkv, (0, 2, 3, 1)).reshape(3, heads * 64, dim)]
-        wq.append(xor_move(wq[0], 1))
-        wq.append(cross_ordered(wq[0], 1, group))
-        wq.append(xor_move(wq[2], 1))
-        wo = [w_out]
-        wo.append(xor_move(w_out, 1))
-        wo.append(cross_ordered(w_out.reshape(heads * 64, dim), 0, group).reshape(heads, 64, dim))
-        wo.append(xor_move(wo[2], 1))
+        x_seq = jnp.zeros((seq, dim), x_in.dtype)
+        for s in (0, 1, 2, 3):
+            mine = lax.dynamic_index_in_dim(x_in, me ^ s, 0, keepdims=False)
+            got = xor_move(mine, s) if s else mine
+            x_seq = lax.dynamic_update_slice_in_dim(x_seq, got, (me ^ s) * rows, 0)
+        cos_tab, sin_tab = rope_tables(seq, 64)
         small = jnp.concatenate([b_up, b_qkv.reshape(-1)])
         smalls = [small] + [xor_move(small, s) for s in (1, 2, 3)]
         b_ups = [v[:cols] for v in smalls]
         b_qkvs = [v[cols:].reshape(3, heads, 64) for v in smalls]
+        w_heads = jnp.transpose(w_qkv, (0, 2, 3, 1)).reshape(3, heads * 64, dim)
+        wq = [w_heads, xor_move(w_heads, 1), xor_move(w_heads, 2)]
+        wo = [w_out, xor_move(w_out, 1), xor_move(w_out, 2)]
+        dy_far_part = xor_move(lax.dynamic_slice_in_dim(grad_y, far_chip * 2, 2, 0), 2)
+        dy_next = xor_move(grad_y, 1)
+        up2 = xor_move(lax.dynamic_slice_in_dim(w_up, group * half, half, 1), 2)
+        down2 = xor_move(lax.dynamic_slice_in_dim(w_down, group * half, half, 0), 2)
         ups = [w_up, xor_move(w_up, 1)]
         downs = [w_down, xor_move(w_down, 1)]
-        dy_full = lax.all_gather(grad_y, 'tp', axis=1, tiled=True)
-        up_x = cross_halves(w_up, 1, group)
-        down_x = cross_halves(w_down, 0, group)
-        ups_x = list(up_x) + [xor_move(v, 1) for v in up_x]
-        downs_x = list(down_x) + [xor_move(v, 1) for v in down_x]
 
         def ordered_bias(v):
-            return jnp.where(group == 0, v, jnp.concatenate([v[cols // 2:], v[:cols // 2]]))
+            return jnp.where(group == 0, v, jnp.concatenate([v[half:], v[:half]]))
 
         my_mask = lax.dynamic_index_in_dim(pad_mask, me, 0, keepdims=False)
         mask_col = jnp.broadcast_to(jnp.where(my_mask > 0, 0.0, NEG_LARGE).astype(F32)[:, None], (seq, 128))
@@ -364,52 +350,82 @@
         def pair_bias(a, b):
             return jnp.transpose(jnp.concatenate([a, b], axis=-1), (1, 0, 2))
 
-        fwd = [attn_fwd(h1, wq[i], wq[i + 1], pair_bias(b_qkvs[i], b_qkvs[i + 1]), cos_tab, sin_tab, mask_col, wo[i], wo[i + 1])
-               for i in (0, 2)]
-        x1_f = (x_f + ((fwd[0][5] + fwd[1][5]) + b_out)).astype(BF16).astype(F32)
+        fwd_a = attn_fwd(h1, wq[0], wq[1], pair_bias(b_qkvs[0], b_qkvs[1]), cos_tab, sin_tab, mask_col, wo[0], wo[1])
+        wq.append(xor_move(wq[2], 1))
+        wo.append(xor_move(wo[2], 1))
+        fwd_b = attn_fwd(h1, wq[2], wq[3], pair_bias(b_qkvs[2], b_qkvs[3]), cos_tab, sin_tab, mask_col, wo[2], wo[3])
+
+        def chip_rows(own, beside, across, diagonal):
+            out = jnp.zeros((2, seq, dim), own.dtype)
+            for s, value in enumerate((own, beside, across, diagonal)):
+                out = lax.dynamic_update_slice_in_dim(out, value, (me ^ s) * rows, 1)
+            return out
+
+        near = lambda v: lax.dynamic_slice_in_dim(v, (1 - far_chip) * 2, 2, 0)
+        far = lambda v: lax.dynamic_slice_in_dim(v, far_chip * 2, 2, 0)
+        dy_near = chip_rows(near(grad_y), near(dy_next), dy_far_part, xor_move(dy_far_part, 1))
+        d_y = lax.dynamic_index_in_dim(dy_near, core, 0, keepdims=False)
+        dy_f = d_y.astype(F32)
+        x1_f = (x_f + ((fwd_a[5] + fwd_b[5]) + b_out)).astype(BF16).astype(F32)
         h2_f, x_hat2, inv_std2 = layer_norm(x1_f, ln2_gain, ln2_bias)
         h2 = h2_f.astype(BF16)
-
-        d_y = lax.dynamic_index_in_dim(dy_full, me, 0, keepdims=False)
-        dy_f = d_y.astype(F32)
+        h2_next = xor_move(h2, 1)
+        h2_far = xor_move(after(h2, up2, down2), 2)
+        dy_far_rest = xor_move(after(near(grad_y), up2, down2), 2)
+
+        def by_core(mine, other):
+            out = jnp.zeros((2, seq, dim), mine.dtype)
+            out = lax.dynamic_update_index_in_dim(out, mine, core, 0)
+            return lax.dynamic_update_index_in_dim(out, other, 1 - core, 0)
+
+        def mlp_weight_grads(h2_two, dy_two):
+            pre_act = jnp.einsum('bsd,df->bsf', h2_two, w_up, preferred_element_type=F32) + b_up
+            act, gelu_slope = gelu_terms(pre_act)
+            g_down = jnp.einsum('bsf,bsd->fd', act.astype(BF16), dy_two, preferred_element_type=F32)
+            d_act = jnp.einsum('bsd,fd->bsf', dy_two, w_down, preferred_element_type=F32)
+            d_pre = d_act * gelu_slope
+            g_up = jnp.einsum('bsd,bsf->df', h2_two, d_pre.astype(BF16), preferred_element_type=F32)
+            return g_up, g_down, jnp.sum(d_pre, axis=(0, 1))
+
         y_a, dh2_a = mlp_chain(h2, d_y, jnp.concatenate([b_ups[0], b_ups[1]]), ups, downs)
-        y_b, dh2_b = mlp_chain(h2, d_y, jnp.concatenate([ordered_bias(b_ups[2]), ordered_bias(b_ups[3])]), ups_x, downs_x)
+        ups_far = [up2, swap_groups(after(up2, y_a))]
+        downs_far = [down2, swap_groups(after(down2, y_a))]
+        near_grads = mlp_weight_grads(by_core(after(h2, y_a), h2_next), dy_near)
+        ups_far += [xor_move(after(v, *near_grads), 1) for v in ups_far]
+        downs_far += [xor_move(after(v, *near_grads), 1) for v in downs_far]
+        y_b, dh2_b = mlp_chain(h2, d_y, jnp.concatenate([ordered_bias(b_ups[2]), ordered_bias(b_ups[3])]), ups_far, downs_far)
         y_seq = (x1_f + ((y_a + y_b) + b_down)).astype(BF16)
         y_out = to_blocks(y_seq)
         d_h2 = dh2_a + dh2_b
         d_x1 = dy_f + layer_norm_grad(d_h2, x_hat2, inv_std2, ln2_gain)
         d_x1_b = d_x1.astype(BF16)
 
-        bwd = {}
-        for i in (2, 0):
-            q, k, v, o, lse, _ = fwd[i // 2]
-            bwd[i] = attn_bwd(h1, d_x1_b, wq[i], wq[i + 1], wo[i], wo[i + 1], q, k, v, o, lse, cos_tab, sin_tab, mask_col)
-        far = [(bwd[2][1], bwd[2][2]), (bwd[2][3], bwd[2][4])]
-        near = [(bwd[0][1], bwd[0][2]), (bwd[0][3], bwd[0][4])]
-        grads = []
-        for (far2, far3), (near0, near1) in zip(far, near):
-            across = xor_move(far2 + xor_move(far3, 1), 2)
-            grads.append((near0 + xor_move(near1, 1)) + across)
-        grad_w_qkv = jnp.transpose(grads[0].reshape(3, heads, 64, dim), (0, 3, 1, 2))
-        grad_w_out = grads[1]
-        d_h1 = bwd[2][0] + bwd[0][0]
+        def backward(i, fwd, d_mid):
+            q, k, v, o, lse, _ = fwd
+            return attn_bwd(h1, d_mid, wq[i], wq[i + 1], wo[i], wo[i + 1], q, k, v, o, lse, cos_tab, sin_tab, mask_col)
+
+        bwd_b = backward(2, fwd_b, d_x1_b)
+        gq_far = bwd_b[1] + xor_move(bwd_b[2], 1)
+        go_far = bwd_b[3] + xor_move(bwd_b[4], 1)
+        gq_across = xor_move(gq_far, 2)
+        go_across = xor_move(go_far, 2)
+        bwd_a = backward(0, fwd_a, after(d_x1_b, gq_far, go_far))
+        d_h1 = bwd_b[0] + bwd_a[0]
         grad_x_seq = (d_x1 + layer_norm_grad(d_h1, x_hat1, inv_std1, ln1_gain)).astype(BF16)
         grad_x = to_blocks(grad_x_seq)
+        grads_q = (bwd_a[1] + xor_move(bwd_a[2], 1)) + gq_across
+        grad_w_qkv = jnp.transpose(grads_q.reshape(3, heads, 64, dim), (0, 3, 1, 2))
+        grad_w_out = (bwd_a[3] + xor_move(bwd_a[4], 1)) + go_across
         gb = []
-        for i in (0, 2):
-            part = jnp.transpose(bwd[i][5][:, :3], (1, 0, 2))
+        for part in (bwd_a[5], bwd_b[5]):
+            part = jnp.transpose(part[:, :3], (1, 0, 2))
             gb += [part[..., :64], part[..., 64:]]
         grad_b_qkv = (gb[0] + xor_move(gb[1], 1)) + (xor_move(gb[2], 2) + xor_move(gb[3], 3))
 
-        h2_full = lax.all_gather(h2[None], 'tp', axis=0, tiled=True)
-        pre_act = jnp.einsum('bsd,df->bsf', h2_full, w_up, preferred_element_type=F32) + b_up
-        act, gelu_slope = gelu_terms(pre_act)
-        act_b = act.astype(BF16)
-        grad_w_down = jnp.einsum('bsf,bsd->fd', act_b, dy_full, preferred_element_type=F32)
-        d_act = jnp.einsum('bsd,fd->bsf', dy_full, w_down, preferred_element_type=F32)
-        d_pre = d_act * gelu_slope
-        grad_b_up = jnp.sum(d_pre, axis=(0, 1))
-        grad_w_up = jnp.einsum('bsd,bsf->df', h2_full, d_pre.astype(BF16), preferred_element_type=F32)
+        dy_far = chip_rows(far(grad_y), far(dy_next), dy_far_rest, xor_move(after(dy_far_rest, bwd_b[0]), 1))
+        h2_far_next = xor_move(after(h2_far, bwd_b[0]), 1)
+        far_grads = mlp_weight_grads(by_core(after(h2_far, grad_x_seq), h2_far_next), dy_far)
+        grad_w_up, grad_w_down, grad_b_up = (a + b for a, b in zip(near_grads, far_grads))
 
         sums = jnp.stack([jnp.sum(dy_f, axis=0), jnp.sum(d_h2 * x_hat2, axis=0), jnp.sum(d_h2, axis=0), jnp.sum(d_x1, axis=0),
                           jnp.sum(d_h1 * x_hat1, axis=0), jnp.sum(d_h1, axis=0)])
@@ -418,4 +434,4 @@
         return (y_out, grad_x, sums[4], sums[5], grad_w_qkv, grad_b_qkv, grad_w_out, sums[3],
                 sums[1], sums[2], grad_w_up, grad_b_up, grad_w_down, sums[0])
 
-    return jax.shard_map(device_step, mesh=mesh, in_specs=in_specs, out_specs=out_specs, check_vma=False)
+    return jax.shard_map(layer, mesh=mesh, in_specs=in_specs, out_specs=out_specs, check_vma=False)

time: 810 us -> 898 us (1.11)
  waiting for transfers between devices: 256 us -> 327 us
  local copies, waits for them, and re-layouts: 24.3 us -> 50.2 us
  between operations: 15.3 us -> 2 us
  matrix products: 85.4 us -> 96.2 us
  other arithmetic: 68.5 us -> 58.5 us
    ppermute x37 -> x45, waiting for transfers between devices: 215 us -> 302 us  [xor_move(): return lax.ppermute(value, 'tp', [(i, i ^ bits) for i in range(4)])]
    dynamic_update_slice x4 -> x15, local copies, waits for them, and re-layouts: 3.62 us -> 24.5 us  [the longest x7 13.8 us: chip_rows(): out = lax.dynamic_update_slice_in_dim(out, value, (me ^ s) * rows, 1)]
    ppermute x4 -> x2, waiting for transfers between devices: 40.8 us -> 25 us  [swap_groups(): return lax.ppermute(value, 'dp', [(0, 1), (1, 0)])]
    dot_general x4 -> x8, matrix products: 85.4 us -> 96.2 us  [the longest x2 27 us: mlp_weight_grads(): jnp.einsum('bsd,fd->bsf', dy_two, w_down, preferred_element_type=F32)]
    ppermute x37 -> x45, starting transfers between devices: 21.4 us -> 24.7 us  [xor_move(): return lax.ppermute(value, 'tp', [(i, i ^ bits) for i in range(4)])]
  transfers between devices with their start and end apart: 43 -> 47, of which waited for: 10 -> 11; matrix products, arithmetic and copies ran while one was open for 21% -> 21% of each run, Pallas kernels for 41% -> 37%
where the time goes in v2:
time: 898 us; the launch traced here: 889 us
  Pallas kernels  328 us (37%)
  waiting for transfers between devices  327 us (36%)
  matrix products  96.2 us (11%)
  other arithmetic  58.5 us (7%)
  local copies, waits for them, and re-layouts  50.2 us (6%)
  starting transfers between devices  26.7 us (3%)
    ppermute x45, waiting for transfers between devices, xor_move(): return lax.ppermute(value, 'tp', [(i, i ^ bits) for i in range(4)])  302 us
    pallas_call x2, Pallas kernels, attn_bwd(): pl.pallas_call(attn_bwd_kernel, grid=(heads,), in_specs=[pl.BlockSpec((se...  141 us
    pallas_call x2, Pallas kernels, attn_fwd(): pl.pallas_call(attn_fwd_kernel, grid=(heads,), in_specs=[pl.BlockSpec((se...  98.4 us
    pallas_call x2, Pallas kernels, mlp_chain(): pl.pallas_call(functools.partial(mlp_kernel, tiles, len(ups)), in_specs=[...  88.8 us
    dot_general x2, matrix products, mlp_weight_grads(): jnp.einsum('bsd,fd->bsf', dy_two, w_down, preferred_element_type=F32)  27 us
    ppermute x2, waiting for transfers between devices, swap_groups(): return lax.ppermute(value, 'dp', [(0, 1), (1, 0)])  25 us
    dot_general x2, matrix products, mlp_weight_grads(): jnp.einsum('bsd,bsf->df', h2_two, d_pre.astype(BF16), preferred_element_t...  24.9 us
    ppermute x45, starting transfers between devices, xor_move(): return lax.ppermute(value, 'tp', [(i, i ^ bits) for i in range(4)])  24.7 us
  transfers between devices with their start and end apart: 47, of which 11 were waited for; matrix products, arithmetic and copies ran while one was open for 21% of the time, Pallas kernels for 37%

profile of v2, /device:TPU:0, one launch (start us, length us, event | category | flops | bytes accessed | tf_op | source)
XLA Modules:
  0.0 888.6 jit_solution(1501842856421896017)
XLA Ops:
  36.4 61.9 %collective-permute-done.2 = bf16[256,1280]{1,0:T(8,128)(2,1)S(1)} collective-permute-done((bf16[256,1280]{1,0:T(8,128)(2,1)}, bf16[256,1280]{1,0:T(8,128)(2,1)S(1)}, u32[]{:S(2)}, u32[]{:S(2)}) %collective-permute-start.2) | collective-permute-done | bytes 655392 | tf_op jit(solution)/shard_map/ppermute | solution.py:282
  104.0 24.1 %collective-permute-done.13 = bf16[2,256,1280]{2,1,0:T(8,128)(2,1)} collective-permute-done((bf16[2,256,1280]{2,1,0:T(8,128)(2,1)}, bf16[2,256,1280]{2,1,0:T(8,128)(2,1)}, u32[]{:S(2)}, u32[]{:S(2)}) %collective-permute-start.13) | collective-permute-done | bytes 1310752 | tf_op jit(solution)/shard_map/ppermute | solution.py:282
  129.6 49.1 %attn_fwd.2 = (bf16[1024,640]{1,0:T(8,128)(2,1)}, bf16[1024,640]{1,0:T(8,128)(2,1)}, bf16[1024,640]{1,0:T(8,128)(2,1)}, bf16[1024,640]{1,0:T(8,128)(2,1)}, f32[5,8,1024]{2,1,0:T(8,128)}, /*index=5*/f32[1024,1280]{1,0:T(8,128)}) custom-call(bf16[1024,1280]{1,0:T(8,128)(2,1)} %fusion.32.h_ref, bf16[3,320,1280]{2,1,0:T(8,128)(2,1)} %bitcast.96, ...), custom_call_target="tpu_custom_call" | custom-call | flops 17448304640 | bytes 20000000 | tf_op jit(solution)/shard_map/attn_fwd/pallas_call | solution.py:114
  194.1 49.3 %attn_fwd.3 = (bf16[1024,640]{1,0:T(8,128)(2,1)}, bf16[1024,640]{1,0:T(8,128)(2,1)}, bf16[1024,640]{1,0:T(8,128)(2,1)}, bf16[1024,640]{1,0:T(8,128)(2,1)}, f32[5,8,1024]{2,1,0:T(8,128)}, /*index=5*/f32[1024,1280]{1,0:T(8,128)}) custom-call(bf16[1024,1280]{1,0:T(8,128)(2,1)} %fusion.32.h_ref, bf16[3,320,1280]{2,1,0:T(8,128)(2,1)} %collective-permute-done.6.w0_ref, ...), custom_call_target="tpu_custom_call" | custom-call | flops 17448304640 | bytes 20000000 | tf_op jit(solution)/shard_map/attn_fwd/pallas_call | solution.py:114
  252.5 44.5 %mlp_chain.2 = (f32[1024,1280]{1,0:T(8,128)}, f32[1024,1280]{1,0:T(8,128)}) custom-call(bf16[1024,1280]{1,0:T(8,128)(2,1)} %copy-done.7, bf16[1024,1280]{1,0:T(8,128)(2,1)} %get-tuple-element.115.refs_1_, f32[4,1,640]{2,1,0:T(1,128)} %pad_maximum_fusion.2.refs_2_, bf16[1280,1280]{1,0:T(8,128)(2,1)} %refs_3_.1, ...), custom_call_target="tpu_custom_call" | custom-call | flops 26843545600 | bytes 30000000 | tf_op jit(solution)/shard_map/mlp_chain/pallas_call | solution.py:268
  301.9 9.1 %fusion.50 = f32[2,1024,1280]{2,1,0:T(8,128)S(1)} fusion(bf16[2,1024,1280]{2,1,0:T(8,128)(2,1)S(1)} %bitcast_dynamic-update-slice_fusion.2, bf16[1280,1280]{1,0:T(8,128)(2,1)} %refs_3_.1), kind=kOutput, calls=%fused_computation.71 | convolution fusion | flops 6710886400 | bytes 19005440 | tf_op jit(solution)/shard_map/bsd,df->bsf/dot_general | solution.py:382
  311.0 9.5 %convolution_bitcast_fusion.2 = f32[1280,1280]{1,0:T(8,128)} fusion(bf16[2,1024,1280]{2,1,0:T(8,128)(2,1)S(1)} %bitcast.87, f32[2,1024,1280]{2,1,0:T(8,128)S(1)} %fusion.50, f32[1280]{0:T(1024)S(1)} %copy-done.33), kind=kOutput, calls=%fused_computation.20 | convolution fusion | flops 6726615040 | bytes 22287360 | tf_op jit(solution)/shard_map/bsf,bsd->fd/dot_general | solution.py:384
  320.6 12.3 %fusion.65 = (f32[1280]{0:T(1024)}, bf16[2,1024,1280]{2,1,0:T(8,128)(2,1)}) fusion(f32[2,1024,1280]{2,1,0:T(8,128)S(1)} %fusion.50, f32[1280]{0:T(1024)S(1)} %copy-done.33, bf16[2,1024,1280]{2,1,0:T(8,128)(2,1)S(1)} %bitcast.87, bf16[1280,1280]{1,0:T(8,128)(2,1)S(1)} %copy-done.22), kind=kOutput, calls=%fused_computation.155 | convolution fusion | flops 6742342656 | bytes 24258560 | tf_op jit(solution)/shard_map/bsd,fd->bsf/dot_general | solution.py:385
  332.9 11.5 %convolution_bitcast_fusion.3 = f32[1280,1280]{1,0:T(8,128)} fusion(bf16[2,1024,1280]{2,1,0:T(8,128)(2,1)S(1)} %bitcast_dynamic-update-slice_fusion.2, bf16[2,1024,1280]{2,1,0:T(8,128)(2,1)} %get-tuple-element.144), kind=kOutput, calls=%fused_computation.21 | convolution fusion | flops 6710886400 | bytes 17039360 | tf_op jit(solution)/shard_map/bsd,bsf->df/dot_general | solution.py:387
  344.9 25.0 %collective-permute-done.18.refs_4_ = bf16[1280,640]{1,0:T(8,128)(2,1)} collective-permute-done((bf16[1280,640]{1,0:T(8,128)(2,1)}, bf16[1280,640]{1,0:T(8,128)(2,1)}, u32[]{:S(2)}, u32[]{:S(2)}) %collective-permute-start.18) | collective-permute-done | bytes 1638432 | tf_op jit(solution)/shard_map/ppermute | solution.py:286
  376.1 44.3 %mlp_chain.3 = (f32[1024,1280]{1,0:T(8,128)}, f32[1024,1280]{1,0:T(8,128)}) custom-call(bf16[1024,1280]{1,0:T(8,128)(2,1)} %copy-done.7, bf16[1024,1280]{1,0:T(8,128)(2,1)} %get-tuple-element.115.refs_1_, f32[4,1,640]{2,1,0:T(1,128)} %pad_maximum_fusion.3.refs_2_, bf16[1280,640]{1,0:T(8,128)(2,1)} %collective-permute-done.17.refs_3_, ...), custom_call_target="tpu_custom_call" | custom-call | flops 26843545600 | bytes 30000000 | tf_op jit(solution)/shard_map/mlp_chain/pallas_call | solution.py:268
  420.5 5.7 fusion.29
  436.5 70.6 %attn_bwd.2 = (f32[1024,1280]{1,0:T(8,128)}, f32[3,320,1280]{2,1,0:T(8,128)}, f32[3,320,1280]{2,1,0:T(8,128)}, f32[5,64,1280]{2,1,0:T(8,128)}, f32[5,64,1280]{2,1,0:T(8,128)}, /*index=5*/f32[5,8,128]{2,1,0:T(8,128)}) custom-call(bf16[1024,1280]{1,0:T(8,128)(2,1)} %fusion.32.h_ref, bf16[1024,1280]{1,0:T(8,128)(2,1)} %convert_element_type.48.dx_ref, ...), custom_call_target="tpu_custom_call" | custom-call | flops 40265318400 | bytes 40000000 | tf_op jit(solution)/shard_map/attn_bwd/pallas_call | solution.py:203
  507.8 30.6 %collective-permute-done.45 = bf16[2,256,1280]{2,1,0:T(8,128)(2,1)S(1)} collective-permute-done((bf16[2,256,1280]{2,1,0:T(8,128)(2,1)S(1)}, bf16[2,256,1280]{2,1,0:T(8,128)(2,1)S(1)}, u32[]{:S(2)}, u32[]{:S(2)}) %collective-permute-start.45) | collective-permute-done | bytes 1310752 | tf_op jit(solution)/shard_map/ppermute | solution.py:282
  542.0 15.9 %collective-permute-done.26 = bf16[256,1280]{1,0:T(8,128)(2,1)S(1)} collective-permute-done((bf16[256,1280]{1,0:T(8,128)(2,1)S(1)}, bf16[256,1280]{1,0:T(8,128)(2,1)S(1)}, u32[]{:S(2)}, u32[]{:S(2)}) %collective-permute-start.26) | collective-permute-done | bytes 655392 | tf_op jit(solution)/shard_map/ppermute | solution.py:282
  557.9 12.1 %collective-permute-done.27 = bf16[256,1280]{1,0:T(8,128)(2,1)S(1)} collective-permute-done((bf16[256,1280]{1,0:T(8,128)(2,1)S(1)}, bf16[256,1280]{1,0:T(8,128)(2,1)S(1)}, u32[]{:S(2)}, u32[]{:S(2)}) %collective-permute-start.27) | collective-permute-done | bytes 655392 | tf_op jit(solution)/shard_map/ppermute | solution.py:282
  577.8 70.3 %attn_bwd.3 = (f32[1024,1280]{1,0:T(8,128)}, f32[3,320,1280]{2,1,0:T(8,128)}, f32[3,320,1280]{2,1,0:T(8,128)}, f32[5,64,1280]{2,1,0:T(8,128)}, f32[5,64,1280]{2,1,0:T(8,128)}, /*index=5*/f32[5,8,128]{2,1,0:T(8,128)}) custom-call(bf16[1024,1280]{1,0:T(8,128)(2,1)} %fusion.32.h_ref, bf16[1024,1280]{1,0:T(8,128)(2,1)} %convert_element_type.48.dx_ref, ...), custom_call_target="tpu_custom_call" | custom-call | flops 40265318400 | bytes 40000000 | tf_op jit(solution)/shard_map/attn_bwd/pallas_call | solution.py:203
  648.1 5.8 fusion.38
  665.1 11.9 %fusion.48 = f32[2,1024,1280]{2,1,0:T(8,128)} fusion(bf16[2,1024,1280]{2,1,0:T(8,128)(2,1)S(1)} %bitcast_dynamic-update-slice_fusion, bf16[1280,1280]{1,0:T(8,128)(2,1)} %refs_3_.1), kind=kOutput, calls=%fused_computation.69 | convolution fusion | flops 6710886400 | bytes 19005440 | tf_op jit(solution)/shard_map/bsd,df->bsf/dot_general | solution.py:382
  677.0 13.9 %fusion.10 = f32[1280,1280]{1,0:T(8,128)} fusion(f32[1280,1280]{1,0:T(8,128)S(1)} %bitcast.99, bf16[2,1024,1280]{2,1,0:T(8,128)(2,1)} %constant_dynamic-update-slice_fusion, f32[2,1024,1280]{2,1,0:T(8,128)} %fusion.48, f32[1280]{0:T(1024)S(1)} %copy-done.34), kind=kOutput, calls=%fused_computation.17 | convolution fusion | flops 6728253440 | bytes 28840960 | tf_op jit(solution)/shard_map/bsf,bsd->fd/dot_general | solution.py:384
  690.9 14.7 %fusion.66 = (f32[1280]{0:T(1024)S(1)}, bf16[2,1024,1280]{2,1,0:T(8,128)(2,1)}) fusion(f32[2,1024,1280]{2,1,0:T(8,128)} %fusion.48, f32[1280]{0:T(1024)S(1)} %copy-done.34, bf16[2,1024,1280]{2,1,0:T(8,128)(2,1)} %constant_dynamic-update-slice_fusion, bf16[1280,1280]{1,0:T(8,128)(2,1)S(1)} %copy-done.23), kind=kOutput, calls=%fused_computation.156 | convolution fusion | flops 6742342656 | bytes 24258560 | tf_op jit(solution)/shard_map/bsd,fd->bsf/dot_general | solution.py:385
  709.2 13.4 %fusion.11 = f32[1280,1280]{1,0:T(8,128)} fusion(f32[1280,1280]{1,0:T(8,128)} %convolution_bitcast_fusion.3, bf16[2,1024,1280]{2,1,0:T(8,128)(2,1)} %copy-done.12, bf16[2,1024,1280]{2,1,0:T(8,128)(2,1)} %get-tuple-element.146), kind=kOutput, calls=%fused_computation.19 | convolution fusion | flops 6712524800 | bytes 23592960 | tf_op jit(solution)/shard_map/bsd,bsf->df/dot_general | solution.py:387
  725.8 117.6 %collective-permute-done.35 = f32[6,1280]{1,0:T(8,128)S(1)} collective-permute-done((f32[6,1280]{1,0:T(8,128)S(1)}, f32[6,1280]{1,0:T(8,128)S(1)}, u32[]{:S(2)}, u32[]{:S(2)}) %collective-permute-start.35) | collective-permute-done | bytes 30752 | tf_op jit(solution)/shard_map/ppermute | solution.py:282
  848.5 32.7 %collective-permute-done.42 = f32[5,64,1280]{2,1,0:T(8,128)S(1)} collective-permute-done((f32[5,64,1280]{2,1,0:T(8,128)S(1)}, f32[5,64,1280]{2,1,0:T(8,128)S(1)}, u32[]{:S(2)}, u32[]{:S(2)}) %collective-permute-start.42) | collective-permute-done | bytes 1638432 | tf_op jit(solution)/shard_map/ppermute | solution.py:282
  (304 shorter events, 131.1 us)
Async XLA Ops:
  29.3 98.7 %collective-permute-start.6 = (bf16[3,320,1280]{2,1,0:T(8,128)(2,1)}, bf16[3,320,1280]{2,1,0:T(8,128)(2,1)}, u32[]{:S(2)}, u32[]{:S(2)}) collective-permute-start(bf16[3,320,1280]{2,1,0:T(8,128)(2,1)} %bitcast.94), channel_id=1, source_target_pairs={{0,2},{1,3},{2,0},{3,1},{4,6},{5,7},{6,4},{7,5}} | collective-permute-start | bytes 7372808 | tf_op jit(solution)/shard_map/ppermute | solution.py:282
  29.8 98.7 %collective-permute-start.3 = (bf16[3,320,1280]{2,1,0:T(8,128)(2,1)}, bf16[3,320,1280]{2,1,0:T(8,128)(2,1)}, u32[]{:S(2)}, u32[]{:S(2)}) collective-permute-start(bf16[3,320,1280]{2,1,0:T(8,128)(2,1)} %bitcast.95), channel_id=1, source_target_pairs={{0,1},{1,0},{2,3},{3,2},{4,5},{5,4},{6,7},{7,6}} | collective-permute-start | bytes 7372808 | tf_op jit(solution)/shard_map/ppermute | solution.py:282
  29.9 68.4 %collective-permute-start.2 = (bf16[256,1280]{1,0:T(8,128)(2,1)}, bf16[256,1280]{1,0:T(8,128)(2,1)S(1)}, u32[]{:S(2)}, u32[]{:S(2)}) collective-permute-start(bf16[256,1280]{1,0:T(8,128)(2,1)} %get-tuple-element.131), channel_id=1, source_target_pairs={{0,3},{1,2},{2,1},{3,0},{4,7},{5,6},{6,5},{7,4}} | collective-permute-start | bytes 1966088 | tf_op jit(solution)/shard_map/ppermute | solution.py:282
  33.7 145.5 %collective-permute-start.12 = (bf16[4,256,1280]{2,1,0:T(8,128)(2,1)}, bf16[4,256,1280]{2,1,0:T(8,128)(2,1)}, u32[]{:S(2)}, u32[]{:S(2)}) collective-permute-start(bf16[4,256,1280]{2,1,0:T(8,128)(2,1)} %param.16), channel_id=1, source_target_pairs={{0,1},{1,0},{2,3},{3,2},{4,5},{5,4},{6,7},{7,6}} | collective-permute-start | bytes 7864328 | tf_op jit(solution)/shard_map/ppermute | solution.py:282
  34.9 93.1 %collective-permute-start.13 = (bf16[2,256,1280]{2,1,0:T(8,128)(2,1)}, bf16[2,256,1280]{2,1,0:T(8,128)(2,1)}, u32[]{:S(2)}, u32[]{:S(2)}) collective-permute-start(bf16[2,256,1280]{2,1,0:T(8,128)(2,1)} %get-tuple-element.111), channel_id=1, source_target_pairs={{0,2},{1,3},{2,0},{3,1},{4,6},{5,7},{6,4},{7,5}} | collective-permute-start | bytes 3932168 | tf_op jit(solution)/shard_map/ppermute | solution.py:282
  103.6 75.1 %collective-permute-start.10 = (bf16[5,64,1280]{2,1,0:T(8,128)(2,1)}, bf16[5,64,1280]{2,1,0:T(8,128)(2,1)}, u32[]{:S(2)}, u32[]{:S(2)}) collective-permute-start(bf16[5,64,1280]{2,1,0:T(8,128)(2,1)} %wo0_ref.3), channel_id=1, source_target_pairs={{0,2},{1,3},{2,0},{3,1},{4,6},{5,7},{6,4},{7,5}} | collective-permute-start | bytes 2457608 | tf_op jit(solution)/shard_map/ppermute | solution.py:282
  128.0 123.0 %collective-permute-start.15 = (bf16[1280,1280]{1,0:T(8,128)(2,1)}, bf16[1280,1280]{1,0:T(8,128)(2,1)}, u32[]{:S(2)}, u32[]{:S(2)}) collective-permute-start(bf16[1280,1280]{1,0:T(8,128)(2,1)} %refs_3_.1), channel_id=1, source_target_pairs={{0,1},{1,0},{2,3},{3,2},{4,5},{5,4},{6,7},{7,6}} | collective-permute-start | bytes 9830408 | tf_op jit(solution)/shard_map/ppermute | solution.py:282
  128.0 57.1 %collective-permute-start.14 = (bf16[2,256,1280]{2,1,0:T(8,128)(2,1)}, bf16[2,256,1280]{2,1,0:T(8,128)(2,1)}, u32[]{:S(2)}, u32[]{:S(2)}) collective-permute-start(bf16[2,256,1280]{2,1,0:T(8,128)(2,1)} %collective-permute-done.13), channel_id=1, source_target_pairs={{0,1},{1,0},{2,3},{3,2},{4,5},{5,4},{6,7},{7,6}} | collective-permute-start | bytes 3932168 | tf_op jit(solution)/shard_map/ppermute | solution.py:282
  128.5 65.5 %collective-permute-start.7 = (bf16[3,320,1280]{2,1,0:T(8,128)(2,1)}, bf16[3,320,1280]{2,1,0:T(8,128)(2,1)}, u32[]{:S(2)}, u32[]{:S(2)}) collective-permute-start(bf16[3,320,1280]{2,1,0:T(8,128)(2,1)} %collective-permute-done.6.w0_ref), channel_id=1, source_target_pairs={{0,1},{1,0},{2,3},{3,2},{4,5},{5,4},{6,7},{7,6}} | collective-permute-start | bytes 7372808 | tf_op jit(solution)/shard_map/ppermute | solution.py:282
  178.7 72.4 %collective-permute-start.16 = (bf16[1280,1280]{1,0:T(8,128)(2,1)}, bf16[1280,1280]{1,0:T(8,128)(2,1)}, u32[]{:S(2)}, u32[]{:S(2)}) collective-permute-start(bf16[1280,1280]{1,0:T(8,128)(2,1)} %refs_5_.1), channel_id=1, source_target_pairs={{0,1},{1,0},{2,3},{3,2},{4,5},{5,4},{6,7},{7,6}} | collective-permute-start | bytes 9830408 | tf_op jit(solution)/shard_map/ppermute | solution.py:282
  185.2 111.8 %collective-permute-start.22 = (bf16[640,1280]{1,0:T(8,128)(2,1)}, bf16[640,1280]{1,0:T(8,128)(2,1)}, u32[]{:S(2)}, u32[]{:S(2)}) collective-permute-start(bf16[640,1280]{1,0:T(8,128)(2,1)} %constant_dynamic-slice_fusion.6), channel_id=1, source_target_pairs={{0,2},{1,3},{2,0},{3,1},{4,6},{5,7},{6,4},{7,5}} | collective-permute-start | bytes 4915208 | tf_op jit(solution)/shard_map/ppermute | solution.py:282
  192.3 106.2 %collective-permute-start.17 = (bf16[1280,640]{1,0:T(8,128)(2,1)}, bf16[1280,640]{1,0:T(8,128)(2,1)}, u32[]{:S(2)}, u32[]{:S(2)}) collective-permute-start(bf16[1280,640]{1,0:T(8,128)(2,1)} %constant_dynamic-slice_fusion.7), channel_id=1, source_target_pairs={{0,2},{1,3},{2,0},{3,1},{4,6},{5,7},{6,4},{7,5}} | collective-permute-start | bytes 4915208 | tf_op jit(solution)/shard_map/ppermute | solution.py:282
  251.0 48.7 %collective-permute-start.19 = (bf16[1024,1280]{1,0:T(8,128)(2,1)S(1)}, bf16[1024,1280]{1,0:T(8,128)(2,1)}, u32[]{:S(2)}, u32[]{:S(2)}) collective-permute-start(bf16[1024,1280]{1,0:T(8,128)(2,1)S(1)} %fusion.25.refs_0_), channel_id=1, source_target_pairs={{0,1},{1,0},{2,3},{3,2},{4,5},{5,4},{6,7},{7,6}} | collective-permute-start | bytes 7864328 | tf_op jit(solution)/shard_map/ppermute | solution.py:282
  298.6 71.4 %collective-permute-start.18 = (bf16[1280,640]{1,0:T(8,128)(2,1)}, bf16[1280,640]{1,0:T(8,128)(2,1)}, u32[]{:S(2)}, u32[]{:S(2)}) collective-permute-start(bf16[1280,640]{1,0:T(8,128)(2,1)} %collective-permute-done.17.refs_3_), channel_id=1, source_target_pairs={{0,4},{4,0},{1,5},{5,1},{2,6},{6,2},{3,7},{7,3}} | collective-permute-start | bytes 4915208 | tf_op jit(solution)/shard_map/ppermute | solution.py:286
  371.2 168.4 %collective-permute-start.43 = (bf16[1024,1280]{1,0:T(8,128)(2,1)}, bf16[1024,1280]{1,0:T(8,128)(2,1)}, u32[]{:S(2)}, u32[]{:S(2)}) collective-permute-start(bf16[1024,1280]{1,0:T(8,128)(2,1)} %copy-done.7), channel_id=1, source_target_pairs={{0,2},{1,3},{2,0},{3,1},{4,6},{5,7},{6,4},{7,5}} | collective-permute-start | bytes 7864328 | tf_op jit(solution)/shard_map/ppermute | solution.py:282
  507.1 67.7 %collective-permute-start.29 = (f32[3,320,1280]{2,1,0:T(8,128)}, f32[3,320,1280]{2,1,0:T(8,128)S(1)}, u32[]{:S(2)}, u32[]{:S(2)}) collective-permute-start(f32[3,320,1280]{2,1,0:T(8,128)} %get-tuple-element.75), channel_id=1, source_target_pairs={{0,1},{1,0},{2,3},{3,2},{4,5},{5,4},{6,7},{7,6}} | collective-permute-start | bytes 14745608 | tf_op jit(solution)/shard_map/ppermute | solution.py:282
  570.0 90.6 %collective-permute-start.44 = (bf16[1024,1280]{1,0:T(8,128)(2,1)}, bf16[1024,1280]{1,0:T(8,128)(2,1)}, u32[]{:S(2)}, u32[]{:S(2)}) collective-permute-start(bf16[1024,1280]{1,0:T(8,128)(2,1)} %collective-permute-done.43), channel_id=1, source_target_pairs={{0,1},{1,0},{2,3},{3,2},{4,5},{5,4},{6,7},{7,6}} | collective-permute-start | bytes 7864328 | tf_op jit(solution)/shard_map/ppermute | solution.py:282
  570.9 136.4 %collective-permute-start.39 = (f32[3,5,64]{2,0,1:T(4,128)S(1)}, f32[3,5,64]{2,0,1:T(4,128)S(1)}, u32[]{:S(2)}, u32[]{:S(2)}) collective-permute-start(f32[3,5,64]{2,0,1:T(4,128)S(1)} %get-tuple-element.139), channel_id=1, source_target_pairs={{0,2},{1,3},{2,0},{3,1},{4,6},{5,7},{6,4},{7,5}} | collective-permute-start | bytes 11528 | tf_op jit(solution)/shard_map/ppermute | solution.py:282
  571.5 136.0 %collective-permute-start.40 = (f32[3,5,64]{2,0,1:T(4,128)S(1)}, f32[3,5,64]{2,0,1:T(4,128)S(1)}, u32[]{:S(2)}, u32[]{:S(2)}) collective-permute-start(f32[3,5,64]{2,0,1:T(4,128)S(1)} %get-tuple-element.138), channel_id=1, source_target_pairs={{0,3},{1,2},{2,1},{3,0},{4,7},{5,6},{6,5},{7,4}} | collective-permute-start | bytes 11528 | tf_op jit(solution)/shard_map/ppermute | solution.py:282
  705.5 177.1 %collective-permute-start.37 = (f32[3,320,1280]{2,1,0:T(8,128)}, f32[3,320,1280]{2,1,0:T(8,128)}, u32[]{:S(2)}, u32[]{:S(2)}) collective-permute-start(f32[3,320,1280]{2,1,0:T(8,128)} %add.259), channel_id=1, source_target_pairs={{0,2},{1,3},{2,0},{3,1},{4,6},{5,7},{6,4},{7,5}} | collective-permute-start | bytes 14745608 | tf_op jit(solution)/shard_map/ppermute | solution.py:282
  707.2 175.4 %collective-permute-start.36 = (f32[3,320,1280]{2,1,0:T(8,128)}, f32[3,320,1280]{2,1,0:T(8,128)S(1)}, u32[]{:S(2)}, u32[]{:S(2)}) collective-permute-start(f32[3,320,1280]{2,1,0:T(8,128)} %get-tuple-element.86), channel_id=1, source_target_pairs={{0,1},{1,0},{2,3},{3,2},{4,5},{5,4},{6,7},{7,6}} | collective-permute-start | bytes 14745608 | tf_op jit(solution)/shard_map/ppermute | solution.py:282
  707.4 136.5 %collective-permute-start.31 = (bf16[256,1280]{1,0:T(8,128)(2,1)S(1)}, bf16[256,1280]{1,0:T(8,128)(2,1)S(1)}, u32[]{:S(2)}, u32[]{:S(2)}) collective-permute-start(bf16[256,1280]{1,0:T(8,128)(2,1)S(1)} %get-tuple-element.126), channel_id=1, source_target_pairs={{0,2},{1,3},{2,0},{3,1},{4,6},{5,7},{6,4},{7,5}} | collective-permute-start | bytes 1966088 | tf_op jit(solution)/shard_map/ppermute | solution.py:282
  709.0 136.3 %collective-permute-start.32 = (bf16[256,1280]{1,0:T(8,128)(2,1)S(1)}, bf16[256,1280]{1,0:T(8,128)(2,1)S(1)}, u32[]{:S(2)}, u32[]{:S(2)}) collective-permute-start(bf16[256,1280]{1,0:T(8,128)(2,1)S(1)} %get-tuple-element.125), channel_id=1, source_target_pairs={{0,3},{1,2},{2,1},{3,0},{4,7},{5,6},{6,5},{7,4}} | collective-permute-start | bytes 1966088 | tf_op jit(solution)/shard_map/ppermute | solution.py:282
  722.6 120.9 %collective-permute-start.35 = (f32[6,1280]{1,0:T(8,128)S(1)}, f32[6,1280]{1,0:T(8,128)S(1)}, u32[]{:S(2)}, u32[]{:S(2)}) collective-permute-start(f32[6,1280]{1,0:T(8,128)S(1)} %add.263), channel_id=1, source_target_pairs={{0,2},{1,3},{2,0},{3,1},{4,6},{5,7},{6,4},{7,5}} | collective-permute-start | bytes 92168 | tf_op jit(solution)/shard_map/ppermute | solution.py:282
  (75 other events, 2541.9 us)

commit v3 on v2

--- a/solution.py
+++ b/solution.py
@@ -32,10 +32,10 @@
     return inv_std * (d_hat - jnp.mean(d_hat, axis=-1, keepdims=True) - x_hat * jnp.mean(d_hat * x_hat, axis=-1, keepdims=True))
 
 
-def rope_tables(seq_len, head_dim):
+def rope_tables(positions, head_dim):
     half_dim = head_dim // 2
     inv_freq = ROPE_BASE ** (-2.0 * jnp.arange(half_dim, dtype=F32) / head_dim)
-    angles = jnp.arange(seq_len, dtype=F32)[:, None] * inv_freq[None, :]
+    angles = positions.astype(F32)[:, None] * inv_freq[None, :]
     cos_half, sin_half = jnp.cos(angles), jnp.sin(angles)
     cos_tab = jnp.concatenate([cos_half] * 4, axis=-1)
     sin_tab = jnp.concatenate([-sin_half, sin_half, -sin_half, sin_half], axis=-1)
@@ -126,7 +126,7 @@
 
 
 def attn_bwd_kernel(h_ref, dx_ref, w0_ref, w1_ref, wo0_ref, wo1_ref, q_ref, k_ref, v_ref, o_ref, lse_ref, cos_ref, sin_ref, mb_ref,
-                    dh_ref, gw0_ref, gw1_ref, gwo0_ref, gwo1_ref, gb_ref, qs, qz, ks, dos, kt, dqt, dk_acc, dv_acc):
+                    dh_ref, gw0_ref, gw1_ref, gb_ref, qs, qz, ks, dos, kt, dqt, dk_acc, dv_acc):
     seq, _ = h_ref.shape
     lane = lax.broadcasted_iota(jnp.int32, (1, 128), 1)
     first_half = (lane % 64) < 32
@@ -137,8 +137,8 @@
     dos[0] = jnp.where(head0, d_o, 0.0).astype(BF16)
     dos[1] = jnp.where(head0, 0.0, d_o).astype(BF16)
     gwo = jnp.dot(o_ref[...].T, dx, preferred_element_type=F32)
-    gwo0_ref[0] = gwo[:64]
-    gwo1_ref[0] = gwo[64:]
+    gw0_ref[3] = gwo[:64]
+    gw1_ref[3] = gwo[64:]
     q, k, mb = q_ref[...].astype(F32), k_ref[...].astype(F32), mb_ref[...]
     qs[0] = jnp.where(head0, q, jnp.where(lane == 64, 1.0, 0.0)).astype(BF16)
     qs[1] = jnp.where(head0, jnp.where(lane == 0, 1.0, 0.0), q).astype(BF16)
@@ -197,16 +197,16 @@
     head_w = pl.BlockSpec((3, 64, dim), lambda i: (0, i, 0))
     head_o = pl.BlockSpec((1, 64, dim), lambda i: (i, 0, 0))
     tab = pl.BlockSpec((seq, 128), full)
-    gw = jax.ShapeDtypeStruct((3, heads * 64, dim), F32)
-    gwo = jax.ShapeDtypeStruct((heads, 64, dim), F32)
+    gw = jax.ShapeDtypeStruct((4, heads * 64, dim), F32)
+    head_g = pl.BlockSpec((4, 64, dim), lambda i: (0, i, 0))
     half = pltpu.VMEM((2, seq, 128), BF16)
     return pl.pallas_call(
         attn_bwd_kernel,
         grid=(heads,),
         in_specs=[pl.BlockSpec((seq, dim), full), pl.BlockSpec((seq, dim), full), head_w, head_w, head_o, head_o, pair, pair, pair, pair,
                   pl.BlockSpec((1, 8, seq), lambda i: (i, 0, 0)), tab, tab, tab],
-        out_specs=[pl.BlockSpec((seq, dim), full), head_w, head_w, head_o, head_o, pl.BlockSpec((1, 8, 128), lambda i: (i, 0, 0))],
-        out_shape=[jax.ShapeDtypeStruct((seq, dim), F32), gw, gw, gwo, gwo, jax.ShapeDtypeStruct((heads, 8, 128), F32)],
+        out_specs=[pl.BlockSpec((seq, dim), full), head_g, head_g, pl.BlockSpec((1, 8, 128), lambda i: (i, 0, 0))],
+        out_shape=[jax.ShapeDtypeStruct((seq, dim), F32), gw, gw, jax.ShapeDtypeStruct((heads, 8, 128), F32)],
         scratch_shapes=[half, half, half, half, pltpu.VMEM((128, seq), BF16), pltpu.VMEM((128, seq), F32),
                         pltpu.VMEM((seq, 128), F32), pltpu.VMEM((seq, 128), F32)],
         compiler_params=pltpu.CompilerParams(dimension_semantics=("arbitrary",), vmem_limit_bytes=VMEM_LIMIT),
@@ -303,97 +303,90 @@
     def layer(x_in, grad_y, pad_mask, ln1_gain, ln1_bias, w_qkv, b_qkv, w_out, b_out, ln2_gain, ln2_bias, w_up, b_up, w_down, b_down):
         me = lax.axis_index('tp')
         group = lax.axis_index('dp')
-        core, far_chip = me % 2, 1 - me // 2
-        n_seq, rows, dim = x_in.shape
-        seq = pad_mask.shape[1]
+        core, chip = me % 2, me // 2
+        _, rows, dim = x_in.shape
         heads = w_out.shape[0]
         cols = w_up.shape[1]
         half = cols // 2
 
+        def pick(blocks, index):
+            return lax.dynamic_index_in_dim(blocks, index, 0, keepdims=False)
+
         def to_blocks(value):
-            out = jnp.zeros((n_seq, rows, dim), value.dtype)
-            for s in (0, 2, 3, 1):
-                mine = lax.dynamic_slice_in_dim(value, (me ^ s) * rows, rows, 0)
-                got = xor_move(mine, s) if s else mine
-                out = lax.dynamic_update_index_in_dim(out, got, me ^ s, 0)
-            return out
-
-        x_seq = jnp.zeros((seq, dim), x_in.dtype)
-        for s in (0, 1, 2, 3):
-            mine = lax.dynamic_index_in_dim(x_in, me ^ s, 0, keepdims=False)
-            got = xor_move(mine, s) if s else mine
-            x_seq = lax.dynamic_update_slice_in_dim(x_seq, got, (me ^ s) * rows, 0)
-        cos_tab, sin_tab = rope_tables(seq, 64)
-        small = jnp.concatenate([b_up, b_qkv.reshape(-1)])
+            v = [value[s * rows:(s + 1) * rows] for s in range(4)]
+            v = [v[0]] + [xor_move(v[s], s) for s in (1, 2, 3)]
+            low = [jnp.where(core == 1, a, b) for a, b in ((v[1], v[0]), (v[0], v[1]))]
+            high = [jnp.where(core == 1, a, b) for a, b in ((v[3], v[2]), (v[2], v[3]))]
+            first = [jnp.where(chip == 1, b, a) for a, b in zip(low, high)]
+            last = [jnp.where(chip == 1, a, b) for a, b in zip(low, high)]
+            return jnp.stack(first + last)
+
+        x_slots = [pick(x_in, me ^ s) for s in range(4)]
+        x_seq = jnp.concatenate([x_slots[0]] + [xor_move(x_slots[s], s) for s in (1, 2, 3)])
+        small = jnp.concatenate([b_up, jnp.transpose(b_qkv, (1, 0, 2)).reshape(-1)])
         smalls = [small] + [xor_move(small, s) for s in (1, 2, 3)]
-        b_ups = [v[:cols] for v in smalls]
-        b_qkvs = [v[cols:].reshape(3, heads, 64) for v in smalls]
+        b_ups = [v[:cols].reshape(2, 1, half) for v in smalls]
+        b_qkvs = [v[cols:].reshape(heads, 3, 64) for v in smalls]
         w_heads = jnp.transpose(w_qkv, (0, 2, 3, 1)).reshape(3, heads * 64, dim)
         wq = [w_heads, xor_move(w_heads, 1), xor_move(w_heads, 2)]
         wo = [w_out, xor_move(w_out, 1), xor_move(w_out, 2)]
-        dy_far_part = xor_move(lax.dynamic_slice_in_dim(grad_y, far_chip * 2, 2, 0), 2)
-        dy_next = xor_move(grad_y, 1)
+        dya2 = xor_move(lax.dynamic_slice_in_dim(grad_y, (1 - chip) * 2, 2, 0), 2)
+        dy1 = xor_move(grad_y, 1)
         up2 = xor_move(lax.dynamic_slice_in_dim(w_up, group * half, half, 1), 2)
         down2 = xor_move(lax.dynamic_slice_in_dim(w_down, group * half, half, 0), 2)
         ups = [w_up, xor_move(w_up, 1)]
         downs = [w_down, xor_move(w_down, 1)]
 
-        def ordered_bias(v):
-            return jnp.where(group == 0, v, jnp.concatenate([v[half:], v[:half]]))
-
-        my_mask = lax.dynamic_index_in_dim(pad_mask, me, 0, keepdims=False)
-        mask_col = jnp.broadcast_to(jnp.where(my_mask > 0, 0.0, NEG_LARGE).astype(F32)[:, None], (seq, 128))
+        positions = jnp.concatenate([(me ^ s) * rows + jnp.arange(rows) for s in range(4)])
+        cos_tab, sin_tab = rope_tables(positions, 64)
+        length = jnp.sum((pick(pad_mask, me) > 0).astype(jnp.int32))
+        mask_col = jnp.broadcast_to(jnp.where(positions < length, 0.0, NEG_LARGE).astype(F32)[:, None], (4 * rows, 128))
         x_f = x_seq.astype(F32)
         h1_f, x_hat1, inv_std1 = layer_norm(x_f, ln1_gain, ln1_bias)
         h1 = h1_f.astype(BF16)
 
         def pair_bias(a, b):
-            return jnp.transpose(jnp.concatenate([a, b], axis=-1), (1, 0, 2))
+            return jnp.concatenate([a, b], axis=-1)
 
         fwd_a = attn_fwd(h1, wq[0], wq[1], pair_bias(b_qkvs[0], b_qkvs[1]), cos_tab, sin_tab, mask_col, wo[0], wo[1])
         wq.append(xor_move(wq[2], 1))
         wo.append(xor_move(wo[2], 1))
         fwd_b = attn_fwd(h1, wq[2], wq[3], pair_bias(b_qkvs[2], b_qkvs[3]), cos_tab, sin_tab, mask_col, wo[2], wo[3])
 
-        def chip_rows(own, beside, across, diagonal):
-            out = jnp.zeros((2, seq, dim), own.dtype)
-            for s, value in enumerate((own, beside, across, diagonal)):
-                out = lax.dynamic_update_slice_in_dim(out, value, (me ^ s) * rows, 1)
-            return out
-
-        near = lambda v: lax.dynamic_slice_in_dim(v, (1 - far_chip) * 2, 2, 0)
-        far = lambda v: lax.dynamic_slice_in_dim(v, far_chip * 2, 2, 0)
-        dy_near = chip_rows(near(grad_y), near(dy_next), dy_far_part, xor_move(dy_far_part, 1))
-        d_y = lax.dynamic_index_in_dim(dy_near, core, 0, keepdims=False)
-        dy_f = d_y.astype(F32)
         x1_f = (x_f + ((fwd_a[5] + fwd_b[5]) + b_out)).astype(BF16).astype(F32)
         h2_f, x_hat2, inv_std2 = layer_norm(x1_f, ln2_gain, ln2_bias)
         h2 = h2_f.astype(BF16)
+        dya3 = xor_move(dya2, 1)
         h2_next = xor_move(h2, 1)
-        h2_far = xor_move(after(h2, up2, down2), 2)
-        dy_far_rest = xor_move(after(near(grad_y), up2, down2), 2)
-
-        def by_core(mine, other):
-            out = jnp.zeros((2, seq, dim), mine.dtype)
-            out = lax.dynamic_update_index_in_dim(out, mine, core, 0)
-            return lax.dynamic_update_index_in_dim(out, other, 1 - core, 0)
-
-        def mlp_weight_grads(h2_two, dy_two):
-            pre_act = jnp.einsum('bsd,df->bsf', h2_two, w_up, preferred_element_type=F32) + b_up
+        d_y = jnp.concatenate([pick(grad_y, me), pick(dy1, me), pick(dya2, core), pick(dya3, core)])
+        d_y_next = jnp.concatenate([pick(dy1, me ^ 1), pick(grad_y, me ^ 1), pick(dya3, 1 - core), pick(dya2, 1 - core)])
+        dy_f = d_y.astype(F32)
+
+        def up_part(h2_two):
+            return jnp.dot(h2_two, w_up, preferred_element_type=F32) + b_up
+
+        def mlp_weight_grads(h2_two, pre_act, dy_two):
             act, gelu_slope = gelu_terms(pre_act)
-            g_down = jnp.einsum('bsf,bsd->fd', act.astype(BF16), dy_two, preferred_element_type=F32)
-            d_act = jnp.einsum('bsd,fd->bsf', dy_two, w_down, preferred_element_type=F32)
+            g_down = jnp.einsum('sf,sd->fd', act.astype(BF16), dy_two, preferred_element_type=F32)
+            d_act = jnp.einsum('sd,fd->sf', dy_two, w_down, preferred_element_type=F32)
             d_pre = d_act * gelu_slope
-            g_up = jnp.einsum('bsd,bsf->df', h2_two, d_pre.astype(BF16), preferred_element_type=F32)
-            return g_up, g_down, jnp.sum(d_pre, axis=(0, 1))
-
-        y_a, dh2_a = mlp_chain(h2, d_y, jnp.concatenate([b_ups[0], b_ups[1]]), ups, downs)
-        ups_far = [up2, swap_groups(after(up2, y_a))]
-        downs_far = [down2, swap_groups(after(down2, y_a))]
-        near_grads = mlp_weight_grads(by_core(after(h2, y_a), h2_next), dy_near)
-        ups_far += [xor_move(after(v, *near_grads), 1) for v in ups_far]
-        downs_far += [xor_move(after(v, *near_grads), 1) for v in downs_far]
-        y_b, dh2_b = mlp_chain(h2, d_y, jnp.concatenate([ordered_bias(b_ups[2]), ordered_bias(b_ups[3])]), ups_far, downs_far)
+            g_up = jnp.einsum('sd,sf->df', h2_two, d_pre.astype(BF16), preferred_element_type=F32)
+            return g_up, g_down, jnp.sum(d_pre, axis=0)
+
+        h2_near = jnp.concatenate([h2, h2_next])
+        pre_near = up_part(h2_near)
+
+        up_y = swap_groups(after(up2, pre_near))
+        y_a, dh2_a = mlp_chain(after(h2, pre_near), d_y, jnp.concatenate([b_ups[0], b_ups[1]]), ups, downs)
+        down_y = swap_groups(after(down2, y_a))
+        near_grads = mlp_weight_grads(h2_near, after(pre_near, y_a), jnp.concatenate([d_y, d_y_next]))
+        h2_far = xor_move(after(h2, down2), 2)
+        dyb2 = xor_move(after(lax.dynamic_slice_in_dim(grad_y, chip * 2, 2, 0), down2), 2)
+        ups_far, downs_far = [up2, up_y], [down2, down_y]
+        ups_far += [xor_move(after(v, y_a), 1) for v in ups_far]
+        downs_far += [xor_move(after(v, near_grads[0]), 1) for v in downs_far]
+        far_bias = [jnp.where(group == 0, v, v[::-1]) for v in b_ups[2:]]
+        y_b, dh2_b = mlp_chain(after(h2, *near_grads), d_y, jnp.concatenate(far_bias), ups_far, downs_far)
         y_seq = (x1_f + ((y_a + y_b) + b_down)).astype(BF16)
         y_out = to_blocks(y_seq)
         d_h2 = dh2_a + dh2_b
@@ -405,32 +398,32 @@
             return attn_bwd(h1, d_mid, wq[i], wq[i + 1], wo[i], wo[i + 1], q, k, v, o, lse, cos_tab, sin_tab, mask_col)
 
         bwd_b = backward(2, fwd_b, d_x1_b)
-        gq_far = bwd_b[1] + xor_move(bwd_b[2], 1)
-        go_far = bwd_b[3] + xor_move(bwd_b[4], 1)
-        gq_across = xor_move(gq_far, 2)
-        go_across = xor_move(go_far, 2)
-        bwd_a = backward(0, fwd_a, after(d_x1_b, gq_far, go_far))
+        g_far = bwd_b[1] + xor_move(bwd_b[2], 1)
+        g_across = xor_move(g_far, 2)
+        dyb3 = xor_move(after(dyb2, bwd_b[0]), 1)
+        h2_far_next = xor_move(after(h2_far, bwd_b[0]), 1)
+        bwd_a = backward(0, fwd_a, after(d_x1_b, g_far))
         d_h1 = bwd_b[0] + bwd_a[0]
         grad_x_seq = (d_x1 + layer_norm_grad(d_h1, x_hat1, inv_std1, ln1_gain)).astype(BF16)
+        sums = jnp.concatenate([jnp.sum(v, axis=0) for v in (dy_f, d_h2 * x_hat2, d_h2, d_x1, d_h1 * x_hat1, d_h1)])
+        gb = []
+        for part in (bwd_a[3], bwd_b[3]):
+            part = jnp.transpose(part[:, :3], (1, 0, 2))
+            gb += [part[..., :64].reshape(-1), part[..., 64:].reshape(-1)]
+        packs = [jnp.concatenate([sums, v]) for v in gb]
+        packs = [packs[0]] + [xor_move(packs[s], s) for s in (1, 2, 3)]
+        totals = (packs[0] + packs[1]) + (packs[2] + packs[3])
+        sums, grad_b_qkv = totals[:6 * dim].reshape(6, dim), totals[6 * dim:].reshape(3, heads, 64)
         grad_x = to_blocks(grad_x_seq)
-        grads_q = (bwd_a[1] + xor_move(bwd_a[2], 1)) + gq_across
-        grad_w_qkv = jnp.transpose(grads_q.reshape(3, heads, 64, dim), (0, 3, 1, 2))
-        grad_w_out = (bwd_a[3] + xor_move(bwd_a[4], 1)) + go_across
-        gb = []
-        for part in (bwd_a[5], bwd_b[5]):
-            part = jnp.transpose(part[:, :3], (1, 0, 2))
-            gb += [part[..., :64], part[..., 64:]]
-        grad_b_qkv = (gb[0] + xor_move(gb[1], 1)) + (xor_move(gb[2], 2) + xor_move(gb[3], 3))
-
-        dy_far = chip_rows(far(grad_y), far(dy_next), dy_far_rest, xor_move(after(dy_far_rest, bwd_b[0]), 1))
-        h2_far_next = xor_move(after(h2_far, bwd_b[0]), 1)
-        far_grads = mlp_weight_grads(by_core(after(h2_far, grad_x_seq), h2_far_next), dy_far)
+        g_all = (bwd_a[1] + xor_move(bwd_a[2], 1)) + g_across
+        grad_w_qkv = jnp.transpose(g_all[:3].reshape(3, heads, 64, dim), (0, 3, 1, 2))
+        grad_w_out = g_all[3].reshape(heads, 64, dim)
+
+        dy_far = jnp.concatenate([pick(dyb2, core), pick(dyb3, core), pick(grad_y, me ^ 2), pick(dy1, me ^ 2),
+                                  pick(dyb3, 1 - core), pick(dyb2, 1 - core), pick(dy1, me ^ 3), pick(grad_y, me ^ 3)])
+        h2_other = jnp.concatenate([after(h2_far, grad_x_seq), h2_far_next])
+        far_grads = mlp_weight_grads(h2_other, up_part(h2_other), dy_far)
         grad_w_up, grad_w_down, grad_b_up = (a + b for a, b in zip(near_grads, far_grads))
-
-        sums = jnp.stack([jnp.sum(dy_f, axis=0), jnp.sum(d_h2 * x_hat2, axis=0), jnp.sum(d_h2, axis=0), jnp.sum(d_x1, axis=0),
-                          jnp.sum(d_h1 * x_hat1, axis=0), jnp.sum(d_h1, axis=0)])
-        sums = sums + xor_move(sums, 1)
-        sums = sums + xor_move(sums, 2)
         return (y_out, grad_x, sums[4], sums[5], grad_w_qkv, grad_b_qkv, grad_w_out, sums[3],
                 sums[1], sums[2], grad_w_up, grad_b_up, grad_w_down, sums[0])
 

time: 898 us -> 863 us (0.961)
  waiting for transfers between devices: 327 us -> 256 us
  other arithmetic: 58.5 us -> 81.6 us
  local copies, waits for them, and re-layouts: 50.2 us -> 60.6 us
    ppermute x45 -> x40, waiting for transfers between devices: 302 us -> 210 us  [xor_move(): return lax.ppermute(value, 'tp', [(i, i ^ bits) for i in range(4)])]
    dynamic_update_slice x23 -> x0, local copies, waits for them, and re-layouts: 26.2 us -> none  [the longest x7 13.8 us: chip_rows(): out = lax.dynamic_update_slice_in_dim(out, value, (me ^ s) * rows, 1)]
    unnamed x106 -> x127, local copies, waits for them, and re-layouts: 8.9 us -> 34 us
    ppermute x2, waiting for transfers between devices: 25 us -> 45.7 us  [swap_groups(): return lax.ppermute(value, 'dp', [(0, 1), (1, 0)])]
    slice x12 -> x18, local copies, waits for them, and re-layouts: 0.2 us -> 9.36 us  [the longest x1 4.96 us: layer(): g_all[:3].reshape(3, heads, 64, dim)]
    add x7 -> x5, other arithmetic: 11.9 us -> 18.8 us  [the longest x1 10.5 us: layer(): g_all = bwd_a[1] + xor_move(bwd_a[2], 1) + g_across]
    reduce_sum x4 -> x5, other arithmetic: 21.4 us -> 23.9 us  [the longest x4 22.5 us: layer(): jnp.sum(v, axis=0)]
    ppermute x45 -> x40, starting transfers between devices: 24.7 us -> 23.7 us  [xor_move(): return lax.ppermute(value, 'tp', [(i, i ^ bits) for i in range(4)])]
  transfers between devices with their start and end apart: 47 -> 42, of which waited for: 11 -> 12; matrix products, arithmetic and copies ran while one was open for 21% -> 24% of each run, Pallas kernels for 37% -> 25%
where the time goes in v3:
time: 863 us; the launch traced here: 855 us
  Pallas kernels  329 us (38%)
  waiting for transfers between devices  256 us (30%)
  matrix products  101 us (12%)
  other arithmetic  81.6 us (9%)
  local copies, waits for them, and re-layouts  60.6 us (7%)
  starting transfers between devices  25.8 us (3%)
    ppermute x40, waiting for transfers between devices, xor_move(): return lax.ppermute(value, 'tp', [(i, i ^ bits) for i in range(4)])  210 us
    pallas_call x2, Pallas kernels, attn_bwd(): pl.pallas_call(attn_bwd_kernel, grid=(heads,), in_specs=[pl.BlockSpec((se...  141 us
    pallas_call x2, Pallas kernels, attn_fwd(): pl.pallas_call(attn_fwd_kernel, grid=(heads,), in_specs=[pl.BlockSpec((se...  98.4 us
    pallas_call x2, Pallas kernels, mlp_chain(): pl.pallas_call(functools.partial(mlp_kernel, tiles, len(ups)), in_specs=[...  89.1 us
    ppermute x2, waiting for transfers between devices, swap_groups(): return lax.ppermute(value, 'dp', [(0, 1), (1, 0)])  45.7 us
    unnamed x127, local copies, waits for them, and re-layouts  34 us
    dot_general x2, matrix products, mlp_weight_grads(): d_act = jnp.einsum('sd,fd->sf', dy_two, w_down, preferred_element_type=F32)  27.1 us
    dot_general x2, matrix products, mlp_weight_grads(): jnp.einsum('sf,sd->fd', act.astype(BF16), dy_two, preferred_element_type=...  25.8 us
  transfers between devices with their start and end apart: 42, of which 12 were waited for; matrix products, arithmetic and copies ran while one was open for 24% of the time, Pallas kernels for 25%

profile of v3, /device:TPU:0, one launch (start us, length us, event | category | flops | bytes accessed | tf_op | source)
XLA Modules:
  0.0 854.8 jit_solution(8182081174303154293)
XLA Ops:
  21.5 36.8 %collective-permute-done.9 = f32[2240]{0:T(1024)S(1)} collective-permute-done((f32[2240]{0:T(1024)S(1)}, f32[2240]{0:T(1024)S(1)}, u32[]{:S(2)}, u32[]{:S(2)}) %collective-permute-start.9) | collective-permute-done | bytes 8992 | tf_op jit(solution)/shard_map/ppermute | solution.py:282
  72.8 14.0 %collective-permute-done.1 = bf16[256,1280]{1,0:T(8,128)(2,1)S(1)} collective-permute-done((bf16[256,1280]{1,0:T(8,128)(2,1)}, bf16[256,1280]{1,0:T(8,128)(2,1)S(1)}, u32[]{:S(2)}, u32[]{:S(2)}) %collective-permute-start.1) | collective-permute-done | bytes 655392 | tf_op jit(solution)/shard_map/ppermute | solution.py:282
  109.7 49.1 %attn_fwd.2 = (bf16[1024,640]{1,0:T(8,128)(2,1)}, bf16[1024,640]{1,0:T(8,128)(2,1)}, bf16[1024,640]{1,0:T(8,128)(2,1)}, bf16[1024,640]{1,0:T(8,128)(2,1)}, f32[5,8,1024]{2,1,0:T(8,128)}, /*index=5*/f32[1024,1280]{1,0:T(8,128)}) custom-call(bf16[1024,1280]{1,0:T(8,128)(2,1)} %fusion.30.h_ref, bf16[3,320,1280]{2,1,0:T(8,128)(2,1)} %bitcast.94, ...), custom_call_target="tpu_custom_call" | custom-call | flops 17448304640 | bytes 20000000 | tf_op jit(solution)/shard_map/attn_fwd/pallas_call | solution.py:114
  160.2 49.3 %attn_fwd.3 = (bf16[1024,640]{1,0:T(8,128)(2,1)}, bf16[1024,640]{1,0:T(8,128)(2,1)}, bf16[1024,640]{1,0:T(8,128)(2,1)}, bf16[1024,640]{1,0:T(8,128)(2,1)}, f32[5,8,1024]{2,1,0:T(8,128)}, /*index=5*/f32[1024,1280]{1,0:T(8,128)}) custom-call(bf16[1024,1280]{1,0:T(8,128)(2,1)} %fusion.30.h_ref, bf16[3,320,1280]{2,1,0:T(8,128)(2,1)} %collective-permute-done.6.w0_ref, ...), custom_call_target="tpu_custom_call" | custom-call | flops 17448304640 | bytes 20000000 | tf_op jit(solution)/shard_map/attn_fwd/pallas_call | solution.py:114
  239.8 13.1 %convolution_add_fusion.2 = f32[2048,1280]{1,0:T(8,128)} fusion(bf16[1280,1280]{1,0:T(8,128)(2,1)} %refs_3_.1, f32[1280]{0:T(1024)S(1)} %copy-done.29, bf16[1024,1280]{1,0:T(8,128)(2,1)} %collective-permute-done.12, bf16[1024,1280]{1,0:T(8,128)(2,1)} %fusion.23.refs_0_), kind=kOutput, calls=%fused_computation.18 | convolution fusion | flops 6723993600 | bytes 19010560 | tf_op jit(solution)/shard_map/dot_general | solution.py:366
  253.0 44.6 %mlp_chain.2 = (f32[1024,1280]{1,0:T(8,128)}, f32[1024,1280]{1,0:T(8,128)}) custom-call(bf16[1024,1280]{1,0:T(8,128)(2,1)} %fusion.23.refs_0_, bf16[1024,1280]{1,0:T(8,128)(2,1)} %get-tuple-element.131.refs_1_, f32[4,1,640]{2,1,0:T(1,128)} %pad_maximum_fusion.11.refs_2_, bf16[1280,1280]{1,0:T(8,128)(2,1)} %refs_3_.1, ...), custom_call_target="tpu_custom_call" | custom-call | flops 26843545600 | bytes 30000000 | tf_op jit(solution)/shard_map/mlp_chain/pallas_call | solution.py:268
  299.7 13.8 %fusion.61 = (f32[1280]{0:T(1024)}, bf16[2048,1280]{1,0:T(8,128)(2,1)S(1)}) fusion(f32[2048,1280]{1,0:T(8,128)} %convolution_add_fusion.2, bf16[2048,1280]{1,0:T(8,128)(2,1)} %bitcast_dynamic-update-slice_fusion.8, bf16[1280,1280]{1,0:T(8,128)(2,1)} %refs_5_.1), kind=kOutput, calls=%fused_computation.191 | convolution fusion | flops 6739721216 | bytes 24253440 | tf_op jit(solution)/shard_map/sd,fd->sf/dot_general | solution.py:371
  313.5 11.1 %fusion.42 = f32[1280,1280]{1,0:T(8,128)} fusion(bf16[2048,1280]{1,0:T(8,128)(2,1)S(1)} %get-tuple-element.203, bf16[1024,1280]{1,0:T(8,128)(2,1)} %collective-permute-done.12, bf16[1024,1280]{1,0:T(8,128)(2,1)} %fusion.23.refs_0_), kind=kOutput, calls=%fused_computation.61 | convolution fusion | flops 6721372160 | bytes 17039360 | tf_op jit(solution)/shard_map/sd,sf->df/dot_general | solution.py:373
  324.8 11.7 %collective-permute-done.19.refs_4_ = bf16[1280,640]{1,0:T(8,128)(2,1)S(1)} collective-permute-done((bf16[1280,640]{1,0:T(8,128)(2,1)}, bf16[1280,640]{1,0:T(8,128)(2,1)S(1)}, u32[]{:S(2)}, u32[]{:S(2)}) %collective-permute-start.19) | collective-permute-done | bytes 1638432 | tf_op jit(solution)/shard_map/ppermute | solution.py:286
  336.5 34.1 %collective-permute-done.23.refs_8_ = bf16[640,1280]{1,0:T(8,128)(2,1)S(1)} collective-permute-done((bf16[640,1280]{1,0:T(8,128)(2,1)}, bf16[640,1280]{1,0:T(8,128)(2,1)S(1)}, u32[]{:S(2)}, u32[]{:S(2)}) %collective-permute-start.23) | collective-permute-done | bytes 1638432 | tf_op jit(solution)/shard_map/ppermute | solution.py:286
  370.6 12.5 %fusion.40 = f32[1280,1280]{1,0:T(8,128)} fusion(bf16[2048,1280]{1,0:T(8,128)(2,1)} %bitcast_dynamic-update-slice_fusion.8, f32[2048,1280]{1,0:T(8,128)S(1)} %copy-done.45), kind=kOutput, calls=%fused_computation.58 | convolution fusion | flops 6723993600 | bytes 22282240 | tf_op jit(solution)/shard_map/sf,sd->fd/dot_general | solution.py:370
  386.0 44.5 %mlp_chain.3 = (f32[1024,1280]{1,0:T(8,128)}, f32[1024,1280]{1,0:T(8,128)}) custom-call(bf16[1024,1280]{1,0:T(8,128)(2,1)} %fusion.23.refs_0_, bf16[1024,1280]{1,0:T(8,128)(2,1)} %get-tuple-element.131.refs_1_, f32[4,1,640]{2,1,0:T(1,128)} %pad_maximum_fusion.12.refs_2_, bf16[1280,640]{1,0:T(8,128)(2,1)} %collective-permute-done.18.refs_3_, ...), custom_call_target="tpu_custom_call" | custom-call | flops 26843545600 | bytes 30000000 | tf_op jit(solution)/shard_map/mlp_chain/pallas_call | solution.py:268
  446.5 70.7 %attn_bwd.2 = (f32[1024,1280]{1,0:T(8,128)}, f32[4,320,1280]{2,1,0:T(8,128)}, f32[4,320,1280]{2,1,0:T(8,128)}, f32[5,8,128]{2,1,0:T(8,128)}) custom-call(bf16[1024,1280]{1,0:T(8,128)(2,1)} %fusion.30.h_ref, bf16[1024,1280]{1,0:T(8,128)(2,1)} %convert_element_type.61.dx_ref, bf16[3,320,1280]{2,1,0:T(8,128)(2,1)} %collective-permute-done.6.w0_ref, ...), custom_call_target="tpu_custom_call" | custom-call | flops 40265318400 | bytes 40000000 | tf_op jit(solution)/shard_map/attn_bwd/pallas_call | solution.py:203
  519.2 85.6 %collective-permute-done.40 = bf16[2,256,1280]{2,1,0:T(8,128)(2,1)} collective-permute-done((bf16[2,256,1280]{2,1,0:T(8,128)(2,1)}, bf16[2,256,1280]{2,1,0:T(8,128)(2,1)}, u32[]{:S(2)}, u32[]{:S(2)}) %collective-permute-start.40) | collective-permute-done | bytes 1310752 | tf_op jit(solution)/shard_map/ppermute | solution.py:282
  610.3 15.1 %collective-permute-done.26 = bf16[256,1280]{1,0:T(8,128)(2,1)S(1)} collective-permute-done((bf16[256,1280]{1,0:T(8,128)(2,1)}, bf16[256,1280]{1,0:T(8,128)(2,1)S(1)}, u32[]{:S(2)}, u32[]{:S(2)}) %collective-permute-start.26) | collective-permute-done | bytes 655392 | tf_op jit(solution)/shard_map/ppermute | solution.py:282
  625.4 13.7 %collective-permute-done.27 = bf16[256,1280]{1,0:T(8,128)(2,1)} collective-permute-done((bf16[256,1280]{1,0:T(8,128)(2,1)}, bf16[256,1280]{1,0:T(8,128)(2,1)}, u32[]{:S(2)}, u32[]{:S(2)}) %collective-permute-start.27) | collective-permute-done | bytes 655392 | tf_op jit(solution)/shard_map/ppermute | solution.py:282
  658.2 70.4 %attn_bwd.3 = (f32[1024,1280]{1,0:T(8,128)}, f32[4,320,1280]{2,1,0:T(8,128)}, f32[4,320,1280]{2,1,0:T(8,128)}, f32[5,8,128]{2,1,0:T(8,128)}) custom-call(bf16[1024,1280]{1,0:T(8,128)(2,1)} %fusion.30.h_ref, bf16[1024,1280]{1,0:T(8,128)(2,1)} %convert_element_type.61.dx_ref, bf16[3,320,1280]{2,1,0:T(8,128)(2,1)} %bitcast.95, ...), custom_call_target="tpu_custom_call" | custom-call | flops 40265318400 | bytes 40000000 | tf_op jit(solution)/shard_map/attn_bwd/pallas_call | solution.py:203
  750.8 11.8 %fusion.63 = f32[2048,1280]{1,0:T(8,128)} fusion(bf16[2048,1280]{1,0:T(8,128)(2,1)S(1)} %constant_dynamic-update-slice_fusion.9, bf16[1280,1280]{1,0:T(8,128)(2,1)} %refs_3_.1), kind=kOutput, calls=%fused_computation.193 | convolution fusion | flops 6710886400 | bytes 19005440 | tf_op jit(solution)/shard_map/dot_general | solution.py:366
  762.7 13.3 %fusion.62 = (f32[1280]{0:T(1024)S(1)}, bf16[2048,1280]{1,0:T(8,128)(2,1)}) fusion(f32[2048,1280]{1,0:T(8,128)} %fusion.63, f32[1280]{0:T(1024)S(1)} %copy-done.30, bf16[2048,1280]{1,0:T(8,128)(2,1)S(1)} %bitcast.89, bf16[1280,1280]{1,0:T(8,128)(2,1)S(1)} %copy-done.17), kind=kOutput, calls=%fused_computation.192 | convolution fusion | flops 6742342656 | bytes 24258560 | tf_op jit(solution)/shard_map/sd,fd->sf/dot_general | solution.py:371
  776.0 11.7 %convolution_add_fusion.1 = f32[1280,1280]{1,0:T(8,128)} fusion(f32[1280,1280]{1,0:T(8,128)S(1)} %bitcast.97, bf16[2048,1280]{1,0:T(8,128)(2,1)S(1)} %constant_dynamic-update-slice_fusion.9, bf16[2048,1280]{1,0:T(8,128)(2,1)} %get-tuple-element.205), kind=kOutput, calls=%fused_computation.17 | convolution fusion | flops 6712524800 | bytes 23592960 | tf_op jit(solution)/shard_map/sd,sf->df/dot_general | solution.py:373
  787.7 13.3 %convolution_add_fusion = f32[1280,1280]{1,0:T(8,128)} fusion(f32[1280,1280]{1,0:T(8,128)} %fusion.40, bf16[2048,1280]{1,0:T(8,128)(2,1)S(1)} %bitcast.89, f32[2048,1280]{1,0:T(8,128)} %fusion.63, f32[1280]{0:T(1024)S(1)} %copy-done.30), kind=kOutput, calls=%fused_computation.16 | convolution fusion | flops 6728253440 | bytes 28840960 | tf_op jit(solution)/shard_map/sf,sd->fd/dot_general | solution.py:370
  805.0 13.2 %collective-permute-done.30 = bf16[256,1280]{1,0:T(8,128)(2,1)S(1)} collective-permute-done((bf16[256,1280]{1,0:T(8,128)(2,1)S(1)}, bf16[256,1280]{1,0:T(8,128)(2,1)S(1)}, u32[]{:S(2)}, u32[]{:S(2)}) %collective-permute-start.30) | collective-permute-done | bytes 655392 | tf_op jit(solution)/shard_map/ppermute | solution.py:282
  818.2 14.6 %collective-permute-done.31 = bf16[256,1280]{1,0:T(8,128)(2,1)S(1)} collective-permute-done((bf16[256,1280]{1,0:T(8,128)(2,1)S(1)}, bf16[256,1280]{1,0:T(8,128)(2,1)S(1)}, u32[]{:S(2)}, u32[]{:S(2)}) %collective-permute-start.31) | collective-permute-done | bytes 655392 | tf_op jit(solution)/shard_map/ppermute | solution.py:282
  836.1 10.5 %add_add_fusion = f32[4,320,1280]{2,1,0:T(8,128)} fusion(f32[4,320,1280]{2,1,0:T(8,128)} %collective-permute-done.37, f32[4,320,1280]{2,1,0:T(8,128)} %get-tuple-element.85, f32[4,320,1280]{2,1,0:T(8,128)} %collective-permute-done.36), kind=kLoop, calls=%fused_computation.25 | loop fusion | flops 3276800 | bytes 26214400 | tf_op jit(solution)/shard_map/add | solution.py:418
  (297 shorter events, 174.3 us)
Async XLA Ops:
  0.7 108.0 %collective-permute-start.3 = (bf16[3,320,1280]{2,1,0:T(8,128)(2,1)}, bf16[3,320,1280]{2,1,0:T(8,128)(2,1)}, u32[]{:S(2)}, u32[]{:S(2)}) collective-permute-start(bf16[3,320,1280]{2,1,0:T(8,128)(2,1)} %bitcast.92), channel_id=1, source_target_pairs={{0,1},{1,0},{2,3},{3,2},{4,5},{5,4},{6,7},{7,6}} | collective-permute-start | bytes 7372808 | tf_op jit(solution)/shard_map/ppermute | solution.py:282
  1.5 90.2 %collective-permute-start.6 = (bf16[3,320,1280]{2,1,0:T(8,128)(2,1)}, bf16[3,320,1280]{2,1,0:T(8,128)(2,1)}, u32[]{:S(2)}, u32[]{:S(2)}) collective-permute-start(bf16[3,320,1280]{2,1,0:T(8,128)(2,1)} %bitcast.93), channel_id=1, source_target_pairs={{0,2},{1,3},{2,0},{3,1},{4,6},{5,7},{6,4},{7,5}} | collective-permute-start | bytes 7372808 | tf_op jit(solution)/shard_map/ppermute | solution.py:282
  5.7 52.6 %collective-permute-start.9 = (f32[2240]{0:T(1024)S(1)}, f32[2240]{0:T(1024)S(1)}, u32[]{:S(2)}, u32[]{:S(2)}) collective-permute-start(f32[2240]{0:T(1024)S(1)} %constant_dynamic-update-slice_fusion.11), channel_id=1, source_target_pairs={{0,3},{1,2},{2,1},{3,0},{4,7},{5,6},{6,5},{7,4}} | collective-permute-start | bytes 26888 | tf_op jit(solution)/shard_map/ppermute | solution.py:282
  5.8 53.9 %collective-permute-start.8 = (f32[2240]{0:T(1024)S(1)}, f32[2240]{0:T(1024)S(1)}, u32[]{:S(2)}, u32[]{:S(2)}) collective-permute-start(f32[2240]{0:T(1024)S(1)} %constant_dynamic-update-slice_fusion.11), channel_id=1, source_target_pairs={{0,2},{1,3},{2,0},{3,1},{4,6},{5,7},{6,4},{7,5}} | collective-permute-start | bytes 26888 | tf_op jit(solution)/shard_map/ppermute | solution.py:282
  88.6 132.9 %collective-permute-start.13 = (bf16[4,256,1280]{2,1,0:T(8,128)(2,1)}, bf16[4,256,1280]{2,1,0:T(8,128)(2,1)}, u32[]{:S(2)}, u32[]{:S(2)}) collective-permute-start(bf16[4,256,1280]{2,1,0:T(8,128)(2,1)} %param.16), channel_id=1, source_target_pairs={{0,1},{1,0},{2,3},{3,2},{4,5},{5,4},{6,7},{7,6}} | collective-permute-start | bytes 7864328 | tf_op jit(solution)/shard_map/ppermute | solution.py:282
  91.7 67.7 %collective-permute-start.7 = (bf16[3,320,1280]{2,1,0:T(8,128)(2,1)}, bf16[3,320,1280]{2,1,0:T(8,128)(2,1)}, u32[]{:S(2)}, u32[]{:S(2)}) collective-permute-start(bf16[3,320,1280]{2,1,0:T(8,128)(2,1)} %collective-permute-done.6.w0_ref), channel_id=1, source_target_pairs={{0,1},{1,0},{2,3},{3,2},{4,5},{5,4},{6,7},{7,6}} | collective-permute-start | bytes 7372808 | tf_op jit(solution)/shard_map/ppermute | solution.py:282
  96.8 156.1 %collective-permute-start.16 = (bf16[1280,1280]{1,0:T(8,128)(2,1)}, bf16[1280,1280]{1,0:T(8,128)(2,1)}, u32[]{:S(2)}, u32[]{:S(2)}) collective-permute-start(bf16[1280,1280]{1,0:T(8,128)(2,1)} %refs_3_.1), channel_id=1, source_target_pairs={{0,1},{1,0},{2,3},{3,2},{4,5},{5,4},{6,7},{7,6}} | collective-permute-start | bytes 9830408 | tf_op jit(solution)/shard_map/ppermute | solution.py:282
  107.2 51.6 %collective-permute-start.14 = (bf16[2,256,1280]{2,1,0:T(8,128)(2,1)}, bf16[2,256,1280]{2,1,0:T(8,128)(2,1)}, u32[]{:S(2)}, u32[]{:S(2)}) collective-permute-start(bf16[2,256,1280]{2,1,0:T(8,128)(2,1)} %get-tuple-element.153), channel_id=1, source_target_pairs={{0,2},{1,3},{2,0},{3,1},{4,6},{5,7},{6,4},{7,5}} | collective-permute-start | bytes 3932168 | tf_op jit(solution)/shard_map/ppermute | solution.py:282
  158.8 94.2 %collective-permute-start.17 = (bf16[1280,1280]{1,0:T(8,128)(2,1)}, bf16[1280,1280]{1,0:T(8,128)(2,1)}, u32[]{:S(2)}, u32[]{:S(2)}) collective-permute-start(bf16[1280,1280]{1,0:T(8,128)(2,1)} %refs_5_.1), channel_id=1, source_target_pairs={{0,1},{1,0},{2,3},{3,2},{4,5},{5,4},{6,7},{7,6}} | collective-permute-start | bytes 9830408 | tf_op jit(solution)/shard_map/ppermute | solution.py:282
  159.3 66.7 %collective-permute-start.15 = (bf16[2,256,1280]{2,1,0:T(8,128)(2,1)}, bf16[2,256,1280]{2,1,0:T(8,128)(2,1)}, u32[]{:S(2)}, u32[]{:S(2)}) collective-permute-start(bf16[2,256,1280]{2,1,0:T(8,128)(2,1)} %collective-permute-done.14), channel_id=1, source_target_pairs={{0,1},{1,0},{2,3},{3,2},{4,5},{5,4},{6,7},{7,6}} | collective-permute-start | bytes 3932168 | tf_op jit(solution)/shard_map/ppermute | solution.py:282
  221.5 76.1 %collective-permute-start.18 = (bf16[1280,640]{1,0:T(8,128)(2,1)}, bf16[1280,640]{1,0:T(8,128)(2,1)}, u32[]{:S(2)}, u32[]{:S(2)}) collective-permute-start(bf16[1280,640]{1,0:T(8,128)(2,1)} %constant_dynamic-slice_fusion.2), channel_id=1, source_target_pairs={{0,2},{1,3},{2,0},{3,1},{4,6},{5,7},{6,4},{7,5}} | collective-permute-start | bytes 4915208 | tf_op jit(solution)/shard_map/ppermute | solution.py:282
  226.0 73.1 %collective-permute-start.22 = (bf16[640,1280]{1,0:T(8,128)(2,1)}, bf16[640,1280]{1,0:T(8,128)(2,1)}, u32[]{:S(2)}, u32[]{:S(2)}) collective-permute-start(bf16[640,1280]{1,0:T(8,128)(2,1)} %constant_dynamic-slice_fusion.1), channel_id=1, source_target_pairs={{0,2},{1,3},{2,0},{3,1},{4,6},{5,7},{6,4},{7,5}} | collective-permute-start | bytes 4915208 | tf_op jit(solution)/shard_map/ppermute | solution.py:282
  299.2 84.0 %collective-permute-start.20 = (bf16[1280,640]{1,0:T(8,128)(2,1)}, bf16[1280,640]{1,0:T(8,128)(2,1)S(1)}, u32[]{:S(2)}, u32[]{:S(2)}) collective-permute-start(bf16[1280,640]{1,0:T(8,128)(2,1)} %collective-permute-done.18.refs_3_), channel_id=1, source_target_pairs={{0,1},{1,0},{2,3},{3,2},{4,5},{5,4},{6,7},{7,6}} | collective-permute-start | bytes 4915208 | tf_op jit(solution)/shard_map/ppermute | solution.py:282
  299.2 71.4 %collective-permute-start.23 = (bf16[640,1280]{1,0:T(8,128)(2,1)}, bf16[640,1280]{1,0:T(8,128)(2,1)S(1)}, u32[]{:S(2)}, u32[]{:S(2)}) collective-permute-start(bf16[640,1280]{1,0:T(8,128)(2,1)} %collective-permute-done.22.refs_7_), channel_id=1, source_target_pairs={{0,4},{4,0},{1,5},{5,1},{2,6},{6,2},{3,7},{7,3}} | collective-permute-start | bytes 4915208 | tf_op jit(solution)/shard_map/ppermute | solution.py:286
  324.6 58.6 %collective-permute-start.24 = (bf16[640,1280]{1,0:T(8,128)(2,1)}, bf16[640,1280]{1,0:T(8,128)(2,1)S(1)}, u32[]{:S(2)}, u32[]{:S(2)}) collective-permute-start(bf16[640,1280]{1,0:T(8,128)(2,1)} %collective-permute-done.22.refs_7_), channel_id=1, source_target_pairs={{0,1},{1,0},{2,3},{3,2},{4,5},{5,4},{6,7},{7,6}} | collective-permute-start | bytes 4915208 | tf_op jit(solution)/shard_map/ppermute | solution.py:282
  517.1 131.7 %collective-permute-start.29 = (f32[4,320,1280]{2,1,0:T(8,128)}, f32[4,320,1280]{2,1,0:T(8,128)}, u32[]{:S(2)}, u32[]{:S(2)}) collective-permute-start(f32[4,320,1280]{2,1,0:T(8,128)} %get-tuple-element.75), channel_id=1, source_target_pairs={{0,1},{1,0},{2,3},{3,2},{4,5},{5,4},{6,7},{7,6}} | collective-permute-start | bytes 19660808 | tf_op jit(solution)/shard_map/ppermute | solution.py:282
  517.2 92.9 %collective-permute-start.38 = (bf16[1024,1280]{1,0:T(8,128)(2,1)}, bf16[1024,1280]{1,0:T(8,128)(2,1)}, u32[]{:S(2)}, u32[]{:S(2)}) collective-permute-start(bf16[1024,1280]{1,0:T(8,128)(2,1)} %fusion.23.refs_0_), channel_id=1, source_target_pairs={{0,2},{1,3},{2,0},{3,1},{4,6},{5,7},{6,4},{7,5}} | collective-permute-start | bytes 7864328 | tf_op jit(solution)/shard_map/ppermute | solution.py:282
  517.8 87.1 %collective-permute-start.40 = (bf16[2,256,1280]{2,1,0:T(8,128)(2,1)}, bf16[2,256,1280]{2,1,0:T(8,128)(2,1)}, u32[]{:S(2)}, u32[]{:S(2)}) collective-permute-start(bf16[2,256,1280]{2,1,0:T(8,128)(2,1)} %get-tuple-element.90), channel_id=1, source_target_pairs={{0,2},{1,3},{2,0},{3,1},{4,6},{5,7},{6,4},{7,5}} | collective-permute-start | bytes 3932168 | tf_op jit(solution)/shard_map/ppermute | solution.py:282
  625.4 123.2 %collective-permute-start.39 = (bf16[1024,1280]{1,0:T(8,128)(2,1)}, bf16[1024,1280]{1,0:T(8,128)(2,1)}, u32[]{:S(2)}, u32[]{:S(2)}) collective-permute-start(bf16[1024,1280]{1,0:T(8,128)(2,1)} %collective-permute-done.38), channel_id=1, source_target_pairs={{0,1},{1,0},{2,3},{3,2},{4,5},{5,4},{6,7},{7,6}} | collective-permute-start | bytes 7864328 | tf_op jit(solution)/shard_map/ppermute | solution.py:282
  657.2 179.0 %collective-permute-start.37 = (f32[4,320,1280]{2,1,0:T(8,128)}, f32[4,320,1280]{2,1,0:T(8,128)}, u32[]{:S(2)}, u32[]{:S(2)}) collective-permute-start(f32[4,320,1280]{2,1,0:T(8,128)} %add.252), channel_id=1, source_target_pairs={{0,2},{1,3},{2,0},{3,1},{4,6},{5,7},{6,4},{7,5}} | collective-permute-start | bytes 19660808 | tf_op jit(solution)/shard_map/ppermute | solution.py:282
  737.4 64.3 %collective-permute-start.34 = (f32[8640]{0:T(1024)S(1)}, f32[8640]{0:T(1024)S(1)}, u32[]{:S(2)}, u32[]{:S(2)}) collective-permute-start(f32[8640]{0:T(1024)S(1)} %constant_dynamic-update-slice_fusion.18), channel_id=1, source_target_pairs={{0,2},{1,3},{2,0},{3,1},{4,6},{5,7},{6,4},{7,5}} | collective-permute-start | bytes 103688 | tf_op jit(solution)/shard_map/ppermute | solution.py:282
  738.5 64.2 %collective-permute-start.35 = (f32[8640]{0:T(1024)S(1)}, f32[8640]{0:T(1024)S(1)}, u32[]{:S(2)}, u32[]{:S(2)}) collective-permute-start(f32[8640]{0:T(1024)S(1)} %constant_dynamic-update-slice_fusion.19), channel_id=1, source_target_pairs={{0,3},{1,2},{2,1},{3,0},{4,7},{5,6},{6,5},{7,4}} | collective-permute-start | bytes 103688 | tf_op jit(solution)/shard_map/ppermute | solution.py:282
  738.9 64.8 %collective-permute-start.33 = (f32[8640]{0:T(1024)S(1)}, f32[8640]{0:T(1024)S(1)}, u32[]{:S(2)}, u32[]{:S(2)}) collective-permute-start(f32[8640]{0:T(1024)S(1)} %constant_dynamic-update-slice_fusion.17), channel_id=1, source_target_pairs={{0,1},{1,0},{2,3},{3,2},{4,5},{5,4},{6,7},{7,6}} | collective-permute-start | bytes 103688 | tf_op jit(solution)/shard_map/ppermute | solution.py:282
  748.6 87.5 %collective-permute-start.36 = (f32[4,320,1280]{2,1,0:T(8,128)}, f32[4,320,1280]{2,1,0:T(8,128)}, u32[]{:S(2)}, u32[]{:S(2)}) collective-permute-start(f32[4,320,1280]{2,1,0:T(8,128)} %get-tuple-element.86), channel_id=1, source_target_pairs={{0,1},{1,0},{2,3},{3,2},{4,5},{5,4},{6,7},{7,6}} | collective-permute-start | bytes 19660808 | tf_op jit(solution)/shard_map/ppermute | solution.py:282
  (70 other events, 2264.9 us)

commit v4 on v3

v4 whole, which is shorter than its diff:
```python
import functools

import jax
import jax.numpy as jnp
from jax import lax
from jax.experimental import pallas as pl
from jax.experimental.pallas import tpu as pltpu
from jax.sharding import PartitionSpec as P


LN_EPS = 1e-5
ROPE_BASE = 10000.0
INV_SQRT2 = 0.7071067811865476
INV_SQRT_2PI = 0.3989422804014327
NEG_LARGE = -1e30
F32 = jnp.float32
BF16 = jnp.bfloat16
NT = (((1,), (1,)), ((), ()))
VMEM_LIMIT = 60 << 20
LANES = 128
HD = 64
QB = 256


def layer_norm(values, ln_gain, ln_bias):
    centered = values - jnp.mean(values, axis=-1, keepdims=True)
    inv_std = lax.rsqrt(jnp.mean(centered * centered, axis=-1, keepdims=True) + LN_EPS)
    x_hat = centered * inv_std
    return x_hat * ln_gain + ln_bias, x_hat, inv_std


def layer_norm_grad(d_out, x_hat, inv_std, ln_gain):
    d_hat = d_out * ln_gain
    return inv_std * (d_hat - jnp.mean(d_hat, axis=-1, keepdims=True) - x_hat * jnp.mean(d_hat * x_hat, axis=-1, keepdims=True))


def rope_tables(positions, head_dim):
    half_dim = head_dim // 2
    inv_freq = ROPE_BASE ** (-2.0 * jnp.arange(half_dim, dtype=F32) / head_dim)
    angles = positions.astype(F32)[:, None] * inv_freq[None, :]
    cos_half, sin_half = jnp.cos(angles), jnp.sin(angles)
    cos_tab = jnp.concatenate([cos_half] * 4, axis=-1)
    sin_tab = jnp.concatenate([-sin_half, sin_half, -sin_half, sin_half], axis=-1)
    return cos_tab, sin_tab


def swap_halves(t, first_half):
    return jnp.where(first_half, pltpu.roll(t, 96, 1), pltpu.roll(t, 32, 1))


def pair_rows(ref0, ref1):
    return jnp.concatenate([r[i] for i in range(3) for r in (ref0, ref1)], axis=0)


def attn_fwd_kernel(h_ref, w0_ref, w1_ref, b_ref, cos_ref, sin_ref, mb_ref, q_ref, k_ref, v_ref, o_ref, lse_ref, qs, ks, st):
    seq = h_ref.shape[0]
    lane = lax.broadcasted_iota(jnp.int32, (1, LANES), 1)
    first_half = (lane % HD) < 32
    head0 = lane < HD
    w = pair_rows(w0_ref, w1_ref)
    t = lax.dot_general(h_ref[...], w, NT, preferred_element_type=F32)
    cos, sin = cos_ref[...], sin_ref[...]
    tq = (t[:, :LANES] + b_ref[0, 0:1]) * 0.125
    tk = t[:, LANES:256] + b_ref[0, 1:2]
    q = (tq * cos + swap_halves(tq, first_half) * sin).astype(BF16)
    k = (tk * cos + swap_halves(tk, first_half) * sin).astype(BF16)
    v_ref[...] = (t[:, 256:] + b_ref[0, 2:3]).astype(BF16)
    q_ref[...] = q
    k_ref[...] = k
    q, k = q.astype(F32), k.astype(F32)
    mb = mb_ref[...]
    qs[0] = jnp.where(head0, q, jnp.where(lane == HD, 1.0, 0.0)).astype(BF16)
    qs[1] = jnp.where(head0, jnp.where(lane == 0, 1.0, 0.0), q).astype(BF16)
    ks[0] = jnp.where(head0, k, jnp.where(lane == HD, mb, 0.0)).astype(BF16)
    ks[1] = jnp.where(head0, jnp.where(lane == 0, mb, 0.0), k).astype(BF16)

    def block(j, carry):
        rows = pl.ds(pl.multiple_of(j * QB, QB), QB)
        outs, stats = [], []
        for head in range(2):
            s = lax.dot_general(qs[head, rows, :], ks[head], NT, preferred_element_type=F32)
            m = jnp.max(s, axis=-1, keepdims=True)
            e = jnp.exp(s - m)
            total = jnp.sum(e, axis=-1, keepdims=True)
            p = (e * (1.0 / total)).astype(BF16)
            outs.append(jnp.dot(p, v_ref[...], preferred_element_type=F32))
            stats.append(m + jnp.log(total))
        o_ref[rows, :] = jnp.where(head0, outs[0], outs[1]).astype(BF16)
        st[rows, :] = jnp.where(head0, stats[0], stats[1])
        return carry

    lax.fori_loop(0, seq // QB, block, 0)
    st_t = st[...].T
    lse_ref[0] = jnp.concatenate([st_t[0:1]] * 4 + [st_t[HD:65]] * 4, axis=0)


def whole(*shape):
    return pl.BlockSpec(shape, lambda *i: (0,) * len(shape))


def head_blocks(parts, dim, first=0):
    return pl.BlockSpec((parts, HD, dim), lambda i: (0, i + first, 0))


def compiler_params():
    return pltpu.CompilerParams(dimension_semantics=("arbitrary",), vmem_limit_bytes=VMEM_LIMIT)


def cost(flops):
    return pl.CostEstimate(flops=flops, bytes_accessed=20_000_000, transcendentals=0)


def attn_fwd(h1, w0, w1, bias, cos_tab, sin_tab, mask_col):
    seq, dim = h1.shape
    heads = w0.shape[1] // HD
    pair = pl.BlockSpec((seq, LANES), lambda i: (0, i))
    head_w = head_blocks(3, dim)
    tab = whole(seq, LANES)
    act = jax.ShapeDtypeStruct((seq, heads * LANES), BF16)
    both = pltpu.VMEM((2, seq, LANES), BF16)
    return pl.pallas_call(
        attn_fwd_kernel,
        grid=(heads,),
        in_specs=[whole(seq, dim), head_w, head_w, pl.BlockSpec((1, 3, LANES), lambda i: (i, 0, 0)), tab, tab, tab],
        out_specs=[pair, pair, pair, pair, pl.BlockSpec((1, 8, seq), lambda i: (i, 0, 0))],
        out_shape=[act, act, act, act, jax.ShapeDtypeStruct((heads, 8, seq), F32)],
        scratch_shapes=[both, both, pltpu.VMEM((seq, LANES), F32)],
        compiler_params=compiler_params(),
        cost_estimate=cost(heads * seq * (dim + seq) * 1024),
        name="attn_fwd",
    )(h1, w0, w1, bias, cos_tab, sin_tab, mask_col)


def attn_bwd_kernel(h_ref, dx_ref, w0_ref, w1_ref, wo0_ref, wo1_ref, q_ref, k_ref, v_ref, o_ref, lse_ref, cos_ref, sin_ref, mb_ref,
                    dh_ref, gw0_ref, gw1_ref, gb_ref, qs, qz, ks, dos, kt, dqt, dk_acc, dv_acc):
    seq, _ = h_ref.shape
    lane = lax.broadcasted_iota(jnp.int32, (1, LANES), 1)
    first_half = (lane % HD) < 32
    head0 = lane < HD
    dx = dx_ref[...]
    wo = jnp.concatenate([wo0_ref[0], wo1_ref[0]], axis=0)
    d_o = lax.dot_general(dx, wo, NT, preferred_element_type=F32)
    dos[0] = jnp.where(head0, d_o, 0.0).astype(BF16)
    dos[1] = jnp.where(head0, 0.0, d_o).astype(BF16)
    gwo = jnp.dot(o_ref[...].T, dx, preferred_element_type=F32)
    gw0_ref[3] = gwo[:HD]
    gw1_ref[3] = gwo[HD:]
    q, k, mb = q_ref[...].astype(F32), k_ref[...].astype(F32), mb_ref[...]
    qs[0] = jnp.where(head0, q, jnp.where(lane == HD, 1.0, 0.0)).astype(BF16)
    qs[1] = jnp.where(head0, jnp.where(lane == 0, 1.0, 0.0), q).astype(BF16)
    qz[0] = jnp.where(head0, q, 0.0).astype(BF16)
    qz[1] = jnp.where(head0, 0.0, q).astype(BF16)
    ks[0] = jnp.where(head0, k, jnp.where(lane == HD, mb, 0.0)).astype(BF16)
    ks[1] = jnp.where(head0, jnp.where(lane == 0, mb, 0.0), k).astype(BF16)
    kt[...] = k_ref[...].T
    dk_acc[...] = jnp.zeros_like(dk_acc)
    dv_acc[...] = jnp.zeros_like(dv_acc)

    def block(j, carry):
        rows = pl.ds(pl.multiple_of(j * QB, QB), QB)
        for head in range(2):
            s_t = lax.dot_general(ks[head], qs[head, rows, :], NT, preferred_element_type=F32)
            p_t = jnp.exp(s_t - lse_ref[0, 4 * head:4 * head + 1, rows])
            do_b = dos[head, rows, :]
            dp_t = lax.dot_general(v_ref[...], do_b, NT, preferred_element_type=F32)
            corr = jnp.sum(p_t * dp_t, axis=0, keepdims=True)
            ds_t = (p_t * (dp_t - corr)).astype(BF16)
            dv_acc[...] += jnp.dot(p_t.astype(BF16), do_b, preferred_element_type=F32)
            dk_acc[...] += jnp.dot(ds_t, qz[head, rows, :], preferred_element_type=F32)
            dqt[HD * head:HD * head + HD, rows] = jnp.dot(kt[HD * head:HD * head + HD, :], ds_t, preferred_element_type=F32)
        return carry

    lax.fori_loop(0, seq // QB, block, 0)
    cos, sin = cos_ref[...], sin_ref[...]
    dq, dk, dv = dqt[...].T, dk_acc[...], dv_acc[...]
    dq = (dq * cos - swap_halves(dq, first_half) * sin) * 0.125
    dk = dk * cos - swap_halves(dk, first_half) * sin
    d_all = jnp.concatenate([dq, dk, dv], axis=1)
    sums = jnp.sum(d_all, axis=0, keepdims=True)
    gb_ref[0] = jnp.concatenate([sums[:, :LANES], sums[:, LANES:256], sums[:, 256:], jnp.zeros((5, LANES), F32)], axis=0)
    d_low = d_all.astype(BF16)
    w = pair_rows(w0_ref, w1_ref)
    part = jnp.dot(d_low, w, preferred_element_type=F32)
    gw = jnp.dot(d_low.T, h_ref[...], preferred_element_type=F32)
    for i in range(3):
        gw0_ref[i] = gw[LANES * i:LANES * i + HD]
        gw1_ref[i] = gw[LANES * i + HD:LANES * i + LANES]

    @pl.when(pl.program_id(0) == 0)
    def _():
        dh_ref[...] = part

    @pl.when(pl.program_id(0) > 0)
    def _():
        dh_ref[...] += part


def attn_bwd(h1, d_x1, w0, w1, wo0, wo1, q, k, v, o, lse, cos_tab, sin_tab, mask_col, first, count):
    seq, dim = h1.shape
    pair = pl.BlockSpec((seq, LANES), lambda i: (0, i + first))
    head_w = head_blocks(3, dim, first)
    head_o = pl.BlockSpec((1, HD, dim), lambda i: (i + first, 0, 0))
    tab = whole(seq, LANES)
    gw = jax.ShapeDtypeStruct((4, count * HD, dim), F32)
    half = pltpu.VMEM((2, seq, LANES), BF16)
    acc = pltpu.VMEM((seq, LANES), F32)
    return pl.pallas_call(
        attn_bwd_kernel,
        grid=(count,),
        in_specs=[whole(seq, dim), whole(seq, dim), head_w, head_w, head_o, head_o, pair, pair, pair, pair,
                  pl.BlockSpec((1, 8, seq), lambda i: (i + first, 0, 0)), tab, tab, tab],
        out_specs=[whole(seq, dim), head_blocks(4, dim), head_blocks(4, dim), pl.BlockSpec((1, 8, LANES), lambda i: (i, 0, 0))],
        out_shape=[jax.ShapeDtypeStruct((seq, dim), F32), gw, gw, jax.ShapeDtypeStruct((count, 8, LANES), F32)],
        scratch_shapes=[half, half, half, half, pltpu.VMEM((LANES, seq), BF16), pltpu.VMEM((LANES, seq), F32), acc, acc],
        compiler_params=compiler_params(),
        cost_estimate=cost(count * seq * (dim + seq) * 2048),
        name="attn_bwd",
    )(h1, d_x1, w0, w1, wo0, wo1, q, k, v, o, lse, cos_tab, sin_tab, mask_col)


def gelu_terms(pre):
    erf_term = lax.erf(pre * INV_SQRT2)
    act = 0.5 * pre * (1.0 + erf_term)
    slope = 0.5 * (1.0 + erf_term) + pre * jnp.exp(-0.5 * pre * pre) * INV_SQRT_2PI
    return act, slope


def mlp_kernel(tiles, n_w, chained, emit, *refs):
    refs = list(refs)
    take = lambda n: [refs.pop(0) for _ in range(n)]
    h_ref, dy_ref, b_ref = take(3)
    ups, downs = take(n_w), take(n_w)
    before = take(2) if chained else None
    y_ref, dh_ref = take(2)
    act_ref, dpre_ref, sum_ref = take(3) if emit else (None,) * 3
    wu, wd, sem = refs
    width = wu.shape[2]
    step = pl.program_id(0)
    copies = []
    for t, (src, part) in enumerate(tiles):
        cols = pl.ds(part * width, width)
        copies.append((pltpu.make_async_copy(ups[src].at[:, cols], wu.at[t], sem.at[0, t]),
                       pltpu.make_async_copy(downs[src].at[cols, :], wd.at[t], sem.at[1, t])))

    @pl.when(step == 0)
    def _():
        for up, down in copies:
            up.start()
            down.start()

    y_sum, dh_sum = (before[0][...], before[1][...]) if chained else (None, None)
    for t in range(len(tiles)):
        @pl.when(step == 0)
        def _(t=t):
            copies[t][0].wait()
            copies[t][1].wait()

        pre = jnp.dot(h_ref[...], wu[t], preferred_element_type=F32) + b_ref[t]
        act, slope = gelu_terms(pre)
        act = act.astype(BF16)
        d_act = lax.dot_general(dy_ref[...], wd[t], NT, preferred_element_type=F32)
        y_part = jnp.dot(act, wd[t], preferred_element_type=F32)
        d_pre = d_act * slope
        d_low = d_pre.astype(BF16)
        dh_part = lax.dot_general(d_low, wu[t], NT, preferred_element_type=F32)
        y_sum = y_part if y_sum is None else y_sum + y_part
        dh_sum = dh_part if dh_sum is None else dh_sum + dh_part
        if emit:
            cols = slice(t * width, (t + 1) * width)
            act_ref[:, cols] = act
            dpre_ref[:, cols] = d_low
            total = jnp.broadcast_to(jnp.sum(d_pre, axis=0, keepdims=True), (8, width))
            sum_ref[:, cols] = total + jnp.where(step == 0, 0.0, sum_ref[:, cols])
    y_ref[...] = y_sum
    dh_ref[...] = dh_sum


def mlp_chain(h2, d_y, bias, ups, downs, before=(), emit=False):
    seq, dim = h2.shape
    width = bias.shape[2]
    tiles = [(i, p) for i, w in enumerate(ups) for p in range(w.shape[1] // width)]
    rows = pl.BlockSpec((QB, dim), lambda j: (j, 0))
    wide = pl.BlockSpec((QB, len(tiles) * width), lambda j: (j, 0))
    hbm = pl.BlockSpec(memory_space=pl.ANY)
    out = jax.ShapeDtypeStruct((seq, dim), F32)
    low = jax.ShapeDtypeStruct((seq, len(tiles) * width), BF16)
    out_specs, out_shape = [rows, rows], [out, out]
    if emit:
        out_specs += [wide, wide, whole(8, len(tiles) * width)]
        out_shape += [low, low, jax.ShapeDtypeStruct((8, len(tiles) * width), F32)]
    return pl.pallas_call(
        functools.partial(mlp_kernel, tiles, len(ups), bool(before), emit),
        grid=(seq // QB,),
        in_specs=[rows, rows, whole(*bias.shape)] + [hbm] * (2 * len(ups)) + [rows] * len(before),
        out_specs=out_specs,
        out_shape=out_shape,
        scratch_shapes=[pltpu.VMEM((len(tiles), dim, width), BF16), pltpu.VMEM((len(tiles), width, dim), BF16),
                        pltpu.SemaphoreType.DMA((2, len(tiles)))],
        compiler_params=compiler_params(),
        cost_estimate=cost(len(tiles) * 8 * seq * dim * width),
        name="mlp_chain",
    )(h2, d_y, bias, *ups, *downs, *before)


def join_kernel(places, n_src, idx_ref, *refs):
    srcs, outs, sem = refs[:n_src], refs[n_src:-1], refs[-1]
    rows = srcs[0].shape[1]
    copies = []
    for p, (src, out, slot) in enumerate(places):
        copies.append(pltpu.make_async_copy(srcs[src].at[idx_ref[p]], outs[out].at[pl.ds(slot * rows, rows)], sem.at[p]))
    for c in copies:
        c.start()
    for c in copies:
        c.wait()


def join(pieces):
    arrays, places, index = [], [], []
    for out, row in enumerate(pieces):
        for slot, (array, i) in enumerate(row):
            at = [k for k, a in enumerate(arrays) if a is array]
            if not at:
                arrays.append(array)
            places.append((at[0] if at else len(arrays) - 1, out, slot))
            index.append(i)
    _, rows, dim = arrays[0].shape
    out = jax.ShapeDtypeStruct((len(pieces[0]) * rows, dim), arrays[0].dtype)
    vmem = pl.BlockSpec(memory_space=pltpu.VMEM)
    return pl.pallas_call(
        functools.partial(join_kernel, places, len(arrays)),
        in_specs=[pl.BlockSpec(memory_space=pltpu.SMEM)] + [pl.BlockSpec(memory_space=pl.ANY)] * len(arrays),
        out_specs=[vmem] * len(pieces),
        out_shape=[out] * len(pieces),
        scratch_shapes=[pltpu.SemaphoreType.DMA((len(places),))],
        cost_estimate=cost(10_000_000),
        name="join_rows",
    )(jnp.stack(index).astype(jnp.int32), *arrays)


def add_kernel(split, a_ref, b_ref, c0_ref, c1_ref, q_ref, o_ref):
    part, head = pl.program_id(0), pl.program_id(1)
    total = (a_ref[0] + b_ref[0]) + jnp.where(head < split, c0_ref[0], c1_ref[0])

    @pl.when(part < 3)
    def _():
        q_ref[0] = total

    @pl.when(part == 3)
    def _():
        o_ref[...] = total


def add_grads(a, b, c0, c1):
    parts, size, dim = a.shape
    heads, split = size // HD, c0.shape[1] // HD
    block = lambda f: pl.BlockSpec((1, HD, dim), f)
    last = parts - 1
    return pl.pallas_call(
        functools.partial(add_kernel, split),
        grid=(parts, heads),
        in_specs=[block(lambda p, i: (p, i, 0)), block(lambda p, i: (p, i, 0)),
                  block(lambda p, i: (p, jnp.minimum(i, split - 1), 0)), block(lambda p, i: (p, jnp.maximum(i - split, 0), 0))],
        out_specs=[block(lambda p, i: (jnp.minimum(p, last - 1), jnp.where(p < last, i, heads - 1), 0)),
                   pl.BlockSpec((HD, dim), lambda p, i: (jnp.where(p < last, 0, i), 0))],
        out_shape=[jax.ShapeDtypeStruct((last, size, dim), F32), jax.ShapeDtypeStruct((size, dim), F32)],
        cost_estimate=cost(10_000_000),
        name="add_grads",
    )(a, b, c0, c1)


def xor_move(value, bits):
    return lax.ppermute(value, 'tp', [(i, i ^ bits) for i in range(4)])


def swap_groups(value):
    return lax.ppermute(value, 'dp', [(0, 1), (1, 0)])


def after(value, *others):
    return lax.optimization_barrier((value,) + others)[0]


def solution(mesh):
    act_spec = P('dp', 'tp', None)
    rep_vec = P(None)
    part_vec = P('dp')
    in_specs = (act_spec, act_spec, P('dp', None), rep_vec, rep_vec, P(None, None, 'tp', None), P(None, 'tp', None),
                P('tp', None, None), rep_vec, rep_vec, rep_vec, P(None, 'tp'), P('tp'), P('tp', None), rep_vec)
    out_specs = (act_spec, act_spec, part_vec, part_vec, P('dp', None, 'tp', None), P('dp', 'tp', None),
                 P(('dp', 'tp'), None, None), part_vec, part_vec, part_vec, P('dp', 'tp'), P(('dp', 'tp')),
                 P(('dp', 'tp'), None), part_vec)

    def layer(x_in, grad_y, pad_mask, ln1_gain, ln1_bias, w_qkv, b_qkv, w_out, b_out, ln2_gain, ln2_bias, w_up, b_up, w_down, b_down):
        me = lax.axis_index('tp')
        group = lax.axis_index('dp')
        core, chip = me % 2, me // 2
        _, rows, dim = x_in.shape
        heads = w_out.shape[0]
        cols = w_up.shape[1]
        half = cols // 2

        def pick(blocks, index):
            return lax.dynamic_index_in_dim(blocks, index, 0, keepdims=False)

        def to_blocks(value):
            v = [value[s * rows:(s + 1) * rows] for s in range(4)]
            v = [v[0]] + [xor_move(v[s], s) for s in (1, 2, 3)]
            low = [jnp.where(core == 1, a, b) for a, b in ((v[1], v[0]), (v[0], v[1]))]
            high = [jnp.where(core == 1, a, b) for a, b in ((v[3], v[2]), (v[2], v[3]))]
            first = [jnp.where(chip == 1, b, a) for a, b in zip(low, high)]
            last = [jnp.where(chip == 1, a, b) for a, b in zip(low, high)]
            return jnp.stack(first + last)

        x_slots = [pick(x_in, me ^ s) for s in range(4)]
        x_seq = jnp.concatenate([x_slots[0]] + [xor_move(x_slots[s], s) for s in (1, 2, 3)])
        small = jnp.concatenate([b_up, jnp.transpose(b_qkv, (1, 0, 2)).reshape(-1)])
        smalls = [small] + [xor_move(small, s) for s in (1, 2, 3)]
        b_ups = [v[:cols].reshape(2, 1, half) for v in smalls]
        b_qkvs = [v[cols:].reshape(heads, 3, HD) for v in smalls]
        w_heads = jnp.transpose(w_qkv, (0, 2, 3, 1)).reshape(3, heads * HD, dim)
        wq = [w_heads, xor_move(w_heads, 1), xor_move(w_heads, 2)]
        wo = [w_out, xor_move(w_out, 1), xor_move(w_out, 2)]
        dya2 = xor_move(lax.dynamic_slice_in_dim(grad_y, (1 - chip) * 2, 2, 0), 2)
        dy1 = xor_move(grad_y, 1)
        up2 = xor_move(lax.dynamic_slice_in_dim(w_up, group * half, half, 1), 2)
        down2 = xor_move(lax.dynamic_slice_in_dim(w_down, group * half, half, 0), 2)
        ups = [w_up, xor_move(w_up, 1)]
        downs = [w_down, xor_move(w_down, 1)]

        positions = jnp.concatenate([(me ^ s) * rows + jnp.arange(rows) for s in range(4)])
        cos_tab, sin_tab = rope_tables(positions, HD)
        length = jnp.sum((pick(pad_mask, me) > 0).astype(jnp.int32))
        mask_col = jnp.broadcast_to(jnp.where(positions < length, 0.0, NEG_LARGE).astype(F32)[:, None], (4 * rows, LANES))
        x_f = x_seq.astype(F32)
        h1_f, x_hat1, inv_std1 = layer_norm(x_f, ln1_gain, ln1_bias)
        h1 = h1_f.astype(BF16)

        def pair_bias(a, b):
            return jnp.concatenate([a, b], axis=-1)

        fwd_a = attn_fwd(h1, wq[0], wq[1], pair_bias(b_qkvs[0], b_qkvs[1]), cos_tab, sin_tab, mask_col)
        wq.append(xor_move(wq[2], 1))
        fwd_b = attn_fwd(h1, wq[2], wq[3], pair_bias(b_qkvs[2], b_qkvs[3]), cos_tab, sin_tab, mask_col)
        wo.append(xor_move(wo[2], 1))

        def pair_out(a, b):
            return jnp.stack([a, b], axis=1).reshape(2 * heads * HD, dim)

        attn_sum = jnp.dot(fwd_a[3], pair_out(wo[0], wo[1]), preferred_element_type=F32)
        attn_sum = attn_sum + jnp.dot(fwd_b[3], pair_out(wo[2], wo[3]), preferred_element_type=F32)
        x1_f = (x_f + (attn_sum + b_out)).astype(BF16).astype(F32)
        h2_f, x_hat2, inv_std2 = layer_norm(x1_f, ln2_gain, ln2_bias)
        h2 = h2_f.astype(BF16)
        dya3 = xor_move(dya2, 1)
        h2_next = xor_move(h2, 1)
        nxt, oth = me ^ 1, 1 - core
        d_y, d_y_next = join([[(grad_y, me), (dy1, me), (dya2, core), (dya3, core)],
                              [(dy1, nxt), (grad_y, nxt), (dya3, oth), (dya2, oth)]])
        dy_f = d_y.astype(F32)

        def grad_dot(a, b):
            return lax.dot_general(a, b, (((0,), (0,)), ((), ())), preferred_element_type=F32)

        y_a, dh2_a, act0, dpre0, sum0 = mlp_chain(h2, d_y, b_ups[0], ups[:1], downs[:1], emit=True)
        up_y = swap_groups(after(up2, y_a))
        y_a, dh2_a, act1, dpre1, sum1 = mlp_chain(h2, d_y, b_ups[1], ups[1:], downs[1:], before=(y_a, dh2_a), emit=True)
        act_next, dpre_next, sum_next = (xor_move(v, 1) for v in (act1, dpre1, sum1))
        h2_far = xor_move(after(h2, down2), 2)
        dyb2 = xor_move(after(lax.dynamic_slice_in_dim(grad_y, chip * 2, 2, 0), down2), 2)
        own_up, own_down = grad_dot(after(h2, y_a), dpre0), grad_dot(act0, after(d_y, y_a))
        down_y = swap_groups(after(down2, y_a))
        up3, down3 = xor_move(after(up2, y_a), 1), xor_move(after(down2, y_a), 1)
        far_bias = [jnp.where(group == 0, v, v[::-1]) for v in b_ups[2:]]
        y_c, dh2_c = mlp_chain(after(h2, own_up, own_down), d_y, jnp.concatenate([v[:1] for v in far_bias]), [up2, up3], [down2, down3],
                               before=(y_a, dh2_a))
        up3_y, down3_y = xor_move(after(up_y, own_up), 1), xor_move(after(down_y, y_c), 1)
        near_up = own_up + grad_dot(after(h2_next, y_c), dpre_next)
        near_down = own_down + grad_dot(act_next, after(d_y_next, y_c))
        y_d, d_h2 = mlp_chain(after(h2, near_up, near_down), d_y, jnp.concatenate([v[1:] for v in far_bias]), [up_y, up3_y], [down_y, down3_y],
                              before=(y_c, dh2_c))
        y_seq = (x1_f + (y_d + b_down)).astype(BF16)
        y_out = to_blocks(y_seq)
        d_x1 = dy_f + layer_norm_grad(d_h2, x_hat2, inv_std2, ln2_gain)
        d_x1_b = d_x1.astype(BF16)

        def backward(i, fwd, d_mid, first, count):
            q, k, v, o, lse = fwd
            return attn_bwd(h1, d_mid, wq[i], wq[i + 1], wo[i], wo[i + 1], q, k, v, o, lse, cos_tab, sin_tab, mask_col, first, count)

        split = 3
        bwd_b = backward(2, fwd_b, d_x1_b, 0, split)
        g_far = bwd_b[1] + xor_move(bwd_b[2], 1)
        g_across = xor_move(g_far, 2)
        bwd_c = backward(2, fwd_b, after(d_x1_b, g_far), split, heads - split)
        g_far_c = bwd_c[1] + xor_move(bwd_c[2], 1)
        g_across_c = xor_move(g_far_c, 2)
        dyb3 = xor_move(after(dyb2, bwd_b[0]), 1)
        h2_far_next = xor_move(after(h2_far, bwd_b[0]), 1)
        bwd_a = backward(0, fwd_a, after(d_x1_b, g_far_c), 0, heads)
        d_h1 = (bwd_b[0] + bwd_c[0]) + bwd_a[0]
        grad_x_seq = (d_x1 + layer_norm_grad(d_h1, x_hat1, inv_std1, ln1_gain)).astype(BF16)
        sums = jnp.concatenate([jnp.sum(v, axis=0) for v in (dy_f, d_h2 * x_hat2, d_h2, d_x1, d_h1 * x_hat1, d_h1)])
        gb = []
        for part in (bwd_a[3], jnp.concatenate([bwd_b[3], bwd_c[3]])):
            part = jnp.transpose(part[:, :3], (1, 0, 2))
            gb += [part[..., :HD].reshape(-1), part[..., HD:].reshape(-1)]
        packs = [jnp.concatenate([sums, v]) for v in gb]
        packs = [packs[0]] + [xor_move(packs[s], s) for s in (1, 2, 3)]
        totals = (packs[0] + packs[1]) + (packs[2] + packs[3])
        sums, grad_b_qkv = totals[:6 * dim].reshape(6, dim), totals[6 * dim:].reshape(3, heads, HD)
        grad_x = to_blocks(grad_x_seq)

        far, diag = me ^ 2, me ^ 3
        dy_far = join([[(dyb2, core), (dyb3, core), (grad_y, far), (dy1, far), (dyb3, oth), (dyb2, oth), (dy1, diag), (grad_y, diag)]])[0]
        h2_other = jnp.concatenate([after(h2_far, grad_x_seq), h2_far_next])
        pre_act = jnp.dot(h2_other, w_up, preferred_element_type=F32) + b_up
        act, gelu_slope = gelu_terms(pre_act)
        grad_w_down = near_down + grad_dot(act.astype(BF16), dy_far)
        d_pre = lax.dot_general(dy_far, w_down, NT, preferred_element_type=F32) * gelu_slope
        grad_w_up = near_up + grad_dot(h2_other, d_pre.astype(BF16))
        grad_b_up = (sum0[0] + sum_next[0]) + jnp.sum(d_pre, axis=0)
        grads_q, grad_w_out = add_grads(bwd_a[1], xor_move(bwd_a[2], 1), g_across, g_across_c)
        grad_w_qkv = jnp.transpose(grads_q.reshape(3, heads, HD, dim), (0, 3, 1, 2))
        grad_w_out = grad_w_out.reshape(heads, HD, dim)
        return (y_out, grad_x, sums[4], sums[5], grad_w_qkv, grad_b_qkv, grad_w_out, sums[3],
                sums[1], sums[2], grad_w_up, grad_b_up, grad_w_down, sums[0])

    return jax.shard_map(layer, mesh=mesh, in_specs=in_specs, out_specs=out_specs, check_vma=False)
```

time: 863 us -> 860 us (level)
  local copies, waits for them, and re-layouts: 60.6 us -> 27.5 us
  Pallas kernels: 329 us -> 358 us
  other arithmetic: 81.6 us -> 66.2 us
  waiting for transfers between devices: 256 us -> 271 us
    ppermute x40 -> x45, waiting for transfers between devices: 210 us -> 243 us  [xor_move(): return lax.ppermute(value, 'tp', [(i, i ^ bits) for i in range(4)])]
    pallas_call x6 -> x12, Pallas kernels: 329 us -> 358 us  [the longest x3 147 us: attn_bwd(): pl.pallas_call(attn_bwd_kernel, grid=(count,), in_specs=[whole(seq, dim),...]
    unnamed x127 -> x87, local copies, waits for them, and re-layouts: 34 us -> 5.1 us
    ppermute x2, waiting for transfers between devices: 45.7 us -> 28.3 us  [swap_groups(): return lax.ppermute(value, 'dp', [(0, 1), (1, 0)])]
    ppermute x40 -> x45, starting transfers between devices: 23.7 us -> 26.6 us  [xor_move(): return lax.ppermute(value, 'tp', [(i, i ^ bits) for i in range(4)])]
    reduce_sum x4 -> x3, other arithmetic: 22.5 us -> 20 us  [layer(): jnp.sum(v, axis=0)]
    dot_general x8 -> x10, matrix products: 101 us -> 101 us  [the longest x6 62.7 us: grad_dot(): lax.dot_general(a, b, (((0,), (0,)), ((), ())), preferred_element_type=F32)]
  transfers between devices with their start and end apart: 42 -> 47, of which waited for: 12 -> 12; matrix products, arithmetic and copies ran while one was open for 24% -> 21% of each run, Pallas kernels for 25% -> 32%
where the time goes in v4:
time: 860 us; the launch traced here: 855 us
  Pallas kernels  358 us (42%)
  waiting for transfers between devices  271 us (32%)
  matrix products  101 us (12%)
  other arithmetic  66.2 us (8%)
  starting transfers between devices  28.6 us (3%)
  local copies, waits for them, and re-layouts  27.5 us (3%)
    ppermute x45, waiting for transfers between devices, xor_move(): return lax.ppermute(value, 'tp', [(i, i ^ bits) for i in range(4)])  243 us
    pallas_call x3, Pallas kernels, attn_bwd(): pl.pallas_call(attn_bwd_kernel, grid=(count,), in_specs=[whole(seq, dim),...  147 us
    pallas_call x4, Pallas kernels, mlp_chain(): pl.pallas_call(functools.partial(mlp_kernel, tiles, len(ups), bool(before...  99.5 us
    pallas_call x2, Pallas kernels, attn_fwd(): pl.pallas_call(attn_fwd_kernel, grid=(heads,), in_specs=[whole(seq, dim),...  84.1 us
    dot_general x6, matrix products, grad_dot(): lax.dot_general(a, b, (((0,), (0,)), ((), ())), preferred_element_type=F32)  62.7 us
    ppermute x2, waiting for transfers between devices, swap_groups(): return lax.ppermute(value, 'dp', [(0, 1), (1, 0)])  28.3 us
    ppermute x45, starting transfers between devices, xor_move(): return lax.ppermute(value, 'tp', [(i, i ^ bits) for i in range(4)])  26.6 us
    reduce_sum x3, other arithmetic, layer(): jnp.sum(v, axis=0)  20 us
  transfers between devices with their start and end apart: 47, of which 12 were waited for; matrix products, arithmetic and copies ran while one was open for 21% of the time, Pallas kernels for 32%

profile of v4, /device:TPU:0, one launch (start us, length us, event | category | flops | bytes accessed | tf_op | source)
XLA Modules:
  0.0 855.2 jit_solution(14954853050660185099)
XLA Ops:
  22.6 67.2 %collective-permute-done.8 = f32[2240]{0:T(1024)S(1)} collective-permute-done((f32[2240]{0:T(1024)S(1)}, f32[2240]{0:T(1024)S(1)}, u32[]{:S(2)}, u32[]{:S(2)}) %collective-permute-start.8) | collective-permute-done | bytes 8992 | tf_op jit(solution)/shard_map/ppermute | solution.py:372
  103.6 13.6 %collective-permute-done.10.wo0_ref = bf16[5,64,1280]{2,1,0:T(8,128)(2,1)S(1)} collective-permute-done((bf16[5,64,1280]{2,1,0:T(8,128)(2,1)}, bf16[5,64,1280]{2,1,0:T(8,128)(2,1)S(1)}, u32[]{:S(2)}, u32[]{:S(2)}) %collective-permute-start.10) | collective-permute-done | bytes 819232 | tf_op jit(solution)/shard_map/ppermute | solution.py:372
  125.3 19.6 %collective-permute-done.13.refs_2_ = bf16[2,256,1280]{2,1,0:T(8,128)(2,1)} collective-permute-done((bf16[2,256,1280]{2,1,0:T(8,128)(2,1)}, bf16[2,256,1280]{2,1,0:T(8,128)(2,1)}, u32[]{:S(2)}, u32[]{:S(2)}) %collective-permute-start.13) | collective-permute-done | bytes 1310752 | tf_op jit(solution)/shard_map/ppermute | solution.py:372
  146.4 41.9 %attn_fwd.2 = (bf16[1024,640]{1,0:T(8,128)(2,1)}, bf16[1024,640]{1,0:T(8,128)(2,1)}, bf16[1024,640]{1,0:T(8,128)(2,1)}, bf16[1024,640]{1,0:T(8,128)(2,1)}, f32[5,8,1024]{2,1,0:T(8,128)}) custom-call(bf16[1024,1280]{1,0:T(8,128)(2,1)} %fusion.25.h_ref, bf16[3,320,1280]{2,1,0:T(8,128)(2,1)} %bitcast.80, bf16[3,320,1280]{2,1,0:T(8,128)(2,1)} %collective-permute-done.3.w1_ref, ...), custom_call_target="tpu_custom_call" | custom-call | flops 12079595520 | bytes 20000000 | tf_op jit(solution)/shard_map/attn_fwd/pallas_call | solution.py:121
  202.3 42.2 %attn_fwd.3 = (bf16[1024,640]{1,0:T(8,128)(2,1)}, bf16[1024,640]{1,0:T(8,128)(2,1)}, bf16[1024,640]{1,0:T(8,128)(2,1)}, bf16[1024,640]{1,0:T(8,128)(2,1)}, f32[5,8,1024]{2,1,0:T(8,128)}) custom-call(bf16[1024,1280]{1,0:T(8,128)(2,1)} %fusion.25.h_ref, bf16[3,320,1280]{2,1,0:T(8,128)(2,1)} %collective-permute-done.6.w0_ref, ...), custom_call_target="tpu_custom_call" | custom-call | flops 12079595520 | bytes 20000000 | tf_op jit(solution)/shard_map/attn_fwd/pallas_call | solution.py:121
  254.2 26.0 %mlp_chain.4 = (f32[1024,1280]{1,0:T(8,128)}, f32[1024,1280]{1,0:T(8,128)}, bf16[1024,1280]{1,0:T(8,128)(2,1)}, bf16[1024,1280]{1,0:T(8,128)(2,1)}, f32[8,1280]{1,0:T(8,128)}) custom-call(bf16[1024,1280]{1,0:T(8,128)(2,1)} %fusion.18.refs_0_, bf16[1024,1280]{1,0:T(8,128)(2,1)} %get-tuple-element.81.refs_1_, f32[2,1,640]{2,1,0:T(1,128)} %reshape.212.refs_2_, ...), custom_call_target="tpu_custom_call" | custom-call | flops 13421772800 | bytes 20000000 | tf_op jit(solution)/shard_map/mlp_chain/pallas_call | solution.py:291
  280.2 25.0 %mlp_chain.5 = (f32[1024,1280]{1,0:T(8,128)}, f32[1024,1280]{1,0:T(8,128)}, bf16[1024,1280]{1,0:T(8,128)(2,1)}, bf16[1024,1280]{1,0:T(8,128)(2,1)}, f32[8,1280]{1,0:T(8,128)}) custom-call(bf16[1024,1280]{1,0:T(8,128)(2,1)} %fusion.18.refs_0_, bf16[1024,1280]{1,0:T(8,128)(2,1)} %get-tuple-element.81.refs_1_, f32[2,1,640]{2,1,0:T(1,128)} %reshape.211.refs_2_, ...), custom_call_target="tpu_custom_call" | custom-call | flops 13421772800 | bytes 20000000 | tf_op jit(solution)/shard_map/mlp_chain/pallas_call | solution.py:291
  327.4 24.4 %mlp_chain.6 = (f32[1024,1280]{1,0:T(8,128)}, f32[1024,1280]{1,0:T(8,128)}) custom-call(bf16[1024,1280]{1,0:T(8,128)(2,1)} %fusion.18.refs_0_, bf16[1024,1280]{1,0:T(8,128)(2,1)} %get-tuple-element.81.refs_1_, f32[2,1,640]{2,1,0:T(1,128)} %pad_maximum_fusion.10.refs_2_, bf16[1280,640]{1,0:T(8,128)(2,1)} %collective-permute-done.18.refs_3_, ...), custom_call_target="tpu_custom_call" | custom-call | flops 13421772800 | bytes 20000000 | tf_op jit(solution)/shard_map/mlp_chain/pallas_call | solution.py:291
  351.8 28.3 %collective-permute-done.24.refs_3_ = bf16[1280,640]{1,0:T(8,128)(2,1)} collective-permute-done((bf16[1280,640]{1,0:T(8,128)(2,1)}, bf16[1280,640]{1,0:T(8,128)(2,1)}, u32[]{:S(2)}, u32[]{:S(2)}) %collective-permute-start.24) | collective-permute-done | bytes 1638432 | tf_op jit(solution)/shard_map/ppermute | solution.py:376
  380.2 10.9 %convolution_add_fusion.2 = f32[1280,1280]{1,0:T(8,128)} fusion(f32[1280,1280]{1,0:T(8,128)} %fusion.55, bf16[1024,1280]{1,0:T(8,128)(2,1)} %collective-permute-done.23, bf16[1024,1280]{1,0:T(8,128)(2,1)} %get-tuple-element.91), kind=kOutput, calls=%fused_computation.10 | convolution fusion | flops 3357081600 | bytes 18350080 | tf_op jit(solution)/shard_map/dot_general | solution.py:462
  400.2 24.2 %mlp_chain.7 = (f32[1024,1280]{1,0:T(8,128)}, f32[1024,1280]{1,0:T(8,128)}) custom-call(bf16[1024,1280]{1,0:T(8,128)(2,1)} %fusion.18.refs_0_, bf16[1024,1280]{1,0:T(8,128)(2,1)} %get-tuple-element.81.refs_1_, f32[2,1,640]{2,1,0:T(1,128)} %pad_maximum_fusion.11.refs_2_, bf16[1280,640]{1,0:T(8,128)(2,1)} %collective-permute-done.24.refs_3_, ...), custom_call_target="tpu_custom_call" | custom-call | flops 13421772800 | bytes 20000000 | tf_op jit(solution)/shard_map/mlp_chain/pallas_call | solution.py:291
  440.0 44.6 %attn_bwd.3 = (f32[1024,1280]{1,0:T(8,128)}, f32[4,192,1280]{2,1,0:T(8,128)}, f32[4,192,1280]{2,1,0:T(8,128)}, f32[3,8,128]{2,1,0:T(8,128)}) custom-call(bf16[1024,1280]{1,0:T(8,128)(2,1)} %fusion.25.h_ref, bf16[1024,1280]{1,0:T(8,128)(2,1)} %convert_element_type.53.dx_ref, bf16[3,320,1280]{2,1,0:T(8,128)(2,1)} %collective-permute-done.6.w0_ref, ...), custom_call_target="tpu_custom_call" | custom-call | flops 14495514624 | bytes 20000000 | tf_op jit(solution)/shard_map/attn_bwd/pallas_call | solution.py:207
  496.5 32.3 %attn_bwd.4 = (f32[1024,1280]{1,0:T(8,128)}, f32[4,128,1280]{2,1,0:T(8,128)}, f32[4,128,1280]{2,1,0:T(8,128)}, f32[2,8,128]{2,1,0:T(8,128)}) custom-call(bf16[1024,1280]{1,0:T(8,128)(2,1)} %fusion.25.h_ref, bf16[1024,1280]{1,0:T(8,128)(2,1)} %convert_element_type.53.dx_ref, bf16[3,320,1280]{2,1,0:T(8,128)(2,1)} %collective-permute-done.6.w0_ref, ...), custom_call_target="tpu_custom_call" | custom-call | flops 9663676416 | bytes 20000000 | tf_op jit(solution)/shard_map/attn_bwd/pallas_call | solution.py:207
  531.7 41.6 %collective-permute-done.44.refs_0_ = bf16[2,256,1280]{2,1,0:T(8,128)(2,1)} collective-permute-done((bf16[2,256,1280]{2,1,0:T(8,128)(2,1)}, bf16[2,256,1280]{2,1,0:T(8,128)(2,1)}, u32[]{:S(2)}, u32[]{:S(2)}) %collective-permute-start.44) | collective-permute-done | bytes 1310752 | tf_op jit(solution)/shard_map/ppermute | solution.py:372
  576.4 9.5 %collective-permute-done.28 = bf16[256,1280]{1,0:T(8,128)(2,1)S(1)} collective-permute-done((bf16[256,1280]{1,0:T(8,128)(2,1)}, bf16[256,1280]{1,0:T(8,128)(2,1)S(1)}, u32[]{:S(2)}, u32[]{:S(2)}) %collective-permute-start.28) | collective-permute-done | bytes 655392 | tf_op jit(solution)/shard_map/ppermute | solution.py:372
  587.1 13.4 %collective-permute-done.29 = bf16[256,1280]{1,0:T(8,128)(2,1)} collective-permute-done((bf16[256,1280]{1,0:T(8,128)(2,1)}, bf16[256,1280]{1,0:T(8,128)(2,1)}, u32[]{:S(2)}, u32[]{:S(2)}) %collective-permute-start.29) | collective-permute-done | bytes 655392 | tf_op jit(solution)/shard_map/ppermute | solution.py:372
  614.3 70.2 %attn_bwd.5 = (f32[1024,1280]{1,0:T(8,128)}, f32[4,320,1280]{2,1,0:T(8,128)}, f32[4,320,1280]{2,1,0:T(8,128)}, f32[5,8,128]{2,1,0:T(8,128)}) custom-call(bf16[1024,1280]{1,0:T(8,128)(2,1)} %fusion.25.h_ref, bf16[1024,1280]{1,0:T(8,128)(2,1)} %convert_element_type.53.dx_ref, bf16[3,320,1280]{2,1,0:T(8,128)(2,1)} %bitcast.81, ...), custom_call_target="tpu_custom_call" | custom-call | flops 24159191040 | bytes 20000000 | tf_op jit(solution)/shard_map/attn_bwd/pallas_call | solution.py:207
  702.2 11.9 %fusion.56 = f32[2048,1280]{1,0:T(8,128)} fusion(bf16[2048,1280]{1,0:T(8,128)(2,1)S(1)} %constant_dynamic-update-slice_fusion.5, bf16[1280,1280]{1,0:T(8,128)(2,1)} %refs_3_.1), kind=kOutput, calls=%fused_computation.165 | convolution fusion | flops 6710886400 | bytes 19005440 | tf_op jit(solution)/shard_map/dot_general | solution.py:516
  714.1 13.9 %fusion.52 = (f32[1280]{0:T(1024)S(1)}, bf16[2048,1280]{1,0:T(8,128)(2,1)}) fusion(f32[2048,1280]{1,0:T(8,128)} %fusion.56, f32[1280]{0:T(1024)S(1)} %copy-done.21, bf16[2048,1280]{1,0:T(8,128)(2,1)S(1)} %bitcast.68, bf16[1280,1280]{1,0:T(8,128)(2,1)} %refs_4_.1), kind=kOutput, calls=%fused_computation.161 | convolution fusion | flops 6742342656 | bytes 24258560 | tf_op jit(solution)/shard_map/dot_general | solution.py:519
  728.0 13.1 %convolution_add_fusion = f32[1280,1280]{1,0:T(8,128)} fusion(f32[1280,1280]{1,0:T(8,128)} %convolution_add_fusion.2, bf16[2048,1280]{1,0:T(8,128)(2,1)S(1)} %bitcast.68, f32[2048,1280]{1,0:T(8,128)} %fusion.56, f32[1280]{0:T(1024)S(1)} %copy-done.21), kind=kOutput, calls=%fused_computation.8 | convolution fusion | flops 6728253440 | bytes 28840960 | tf_op jit(solution)/shard_map/dot_general | solution.py:462
  742.0 11.8 %convolution_add_fusion.1 = f32[1280,1280]{1,0:T(8,128)} fusion(f32[1280,1280]{1,0:T(8,128)S(1)} %bitcast.84, bf16[2048,1280]{1,0:T(8,128)(2,1)S(1)} %constant_dynamic-update-slice_fusion.5, bf16[2048,1280]{1,0:T(8,128)(2,1)} %get-tuple-element.235), kind=kOutput, calls=%fused_computation.9 | convolution fusion | flops 6712524800 | bytes 23592960 | tf_op jit(solution)/shard_map/dot_general | solution.py:462
  758.2 56.3 %collective-permute-done.38 = f32[8640]{0:T(1024)S(1)} collective-permute-done((f32[8640]{0:T(1024)S(1)}, f32[8640]{0:T(1024)S(1)}, u32[]{:S(2)}, u32[]{:S(2)}) %collective-permute-start.38) | collective-permute-done | bytes 34592 | tf_op jit(solution)/shard_map/ppermute | solution.py:372
  820.8 14.0 %collective-permute-done.34 = bf16[256,1280]{1,0:T(8,128)(2,1)} collective-permute-done((bf16[256,1280]{1,0:T(8,128)(2,1)}, bf16[256,1280]{1,0:T(8,128)(2,1)}, u32[]{:S(2)}, u32[]{:S(2)}) %collective-permute-start.34) | collective-permute-done | bytes 655392 | tf_op jit(solution)/shard_map/ppermute | solution.py:372
  838.3 16.5 %add_grads.1 = (f32[3,320,1280]{2,1,0:T(8,128)}, f32[320,1280]{1,0:T(8,128)}) custom-call(f32[4,320,1280]{2,1,0:T(8,128)} %get-tuple-element.119.a_ref, f32[4,320,1280]{2,1,0:T(8,128)} %collective-permute-done.39.b_ref, f32[4,192,1280]{2,1,0:T(8,128)} %collective-permute-done.40.c0_ref, f32[4,128,1280]{2,1,0:T(8,128)} %collective-permute-done.41.c1_ref), custom_call_target="tpu_custom_call" | custom-call | flops 10000000 | bytes 20000000 | tf_op jit(solution)/shard_map/add_grads/pallas_call | solution.py:358
  (278 shorter events, 181.1 us)
Async XLA Ops:
  3.9 91.9 %collective-permute-start = (bf16[256,1280]{1,0:T(8,128)(2,1)}, bf16[256,1280]{1,0:T(8,128)(2,1)}, u32[]{:S(2)}, u32[]{:S(2)}) collective-permute-start(bf16[256,1280]{1,0:T(8,128)(2,1)} %get-tuple-element.188), channel_id=1, source_target_pairs={{0,1},{1,0},{2,3},{3,2},{4,5},{5,4},{6,7},{7,6}} | collective-permute-start | bytes 1966088 | tf_op jit(solution)/shard_map/ppermute | solution.py:372
  4.7 91.1 %collective-permute-start.1 = (bf16[256,1280]{1,0:T(8,128)(2,1)}, bf16[256,1280]{1,0:T(8,128)(2,1)}, u32[]{:S(2)}, u32[]{:S(2)}) collective-permute-start(bf16[256,1280]{1,0:T(8,128)(2,1)} %get-tuple-element.190), channel_id=1, source_target_pairs={{0,2},{1,3},{2,0},{3,1},{4,6},{5,7},{6,4},{7,5}} | collective-permute-start | bytes 1966088 | tf_op jit(solution)/shard_map/ppermute | solution.py:372
  7.2 90.1 %collective-permute-start.2 = (bf16[256,1280]{1,0:T(8,128)(2,1)}, bf16[256,1280]{1,0:T(8,128)(2,1)}, u32[]{:S(2)}, u32[]{:S(2)}) collective-permute-start(bf16[256,1280]{1,0:T(8,128)(2,1)} %get-tuple-element.189), channel_id=1, source_target_pairs={{0,3},{1,2},{2,1},{3,0},{4,7},{5,6},{6,5},{7,4}} | collective-permute-start | bytes 1966088 | tf_op jit(solution)/shard_map/ppermute | solution.py:372
  7.5 109.7 %collective-permute-start.6 = (bf16[3,320,1280]{2,1,0:T(8,128)(2,1)}, bf16[3,320,1280]{2,1,0:T(8,128)(2,1)}, u32[]{:S(2)}, u32[]{:S(2)}) collective-permute-start(bf16[3,320,1280]{2,1,0:T(8,128)(2,1)} %bitcast.78), channel_id=1, source_target_pairs={{0,2},{1,3},{2,0},{3,1},{4,6},{5,7},{6,4},{7,5}} | collective-permute-start | bytes 7372808 | tf_op jit(solution)/shard_map/ppermute | solution.py:372
  19.8 69.9 %collective-permute-start.8 = (f32[2240]{0:T(1024)S(1)}, f32[2240]{0:T(1024)S(1)}, u32[]{:S(2)}, u32[]{:S(2)}) collective-permute-start(f32[2240]{0:T(1024)S(1)} %constant_dynamic-update-slice_fusion.7), channel_id=1, source_target_pairs={{0,2},{1,3},{2,0},{3,1},{4,6},{5,7},{6,4},{7,5}} | collective-permute-start | bytes 26888 | tf_op jit(solution)/shard_map/ppermute | solution.py:372
  103.5 92.2 %collective-permute-start.12 = (bf16[4,256,1280]{2,1,0:T(8,128)(2,1)S(1)}, bf16[4,256,1280]{2,1,0:T(8,128)(2,1)}, u32[]{:S(2)}, u32[]{:S(2)}) collective-permute-start(bf16[4,256,1280]{2,1,0:T(8,128)(2,1)S(1)} %copy-done.3), channel_id=1, source_target_pairs={{0,1},{1,0},{2,3},{3,2},{4,5},{5,4},{6,7},{7,6}} | collective-permute-start | bytes 7864328 | tf_op jit(solution)/shard_map/ppermute | solution.py:372
  117.2 85.1 %collective-permute-start.7 = (bf16[3,320,1280]{2,1,0:T(8,128)(2,1)}, bf16[3,320,1280]{2,1,0:T(8,128)(2,1)}, u32[]{:S(2)}, u32[]{:S(2)}) collective-permute-start(bf16[3,320,1280]{2,1,0:T(8,128)(2,1)} %collective-permute-done.6.w0_ref), channel_id=1, source_target_pairs={{0,1},{1,0},{2,3},{3,2},{4,5},{5,4},{6,7},{7,6}} | collective-permute-start | bytes 7372808 | tf_op jit(solution)/shard_map/ppermute | solution.py:372
  123.8 156.4 %collective-permute-start.15 = (bf16[1280,1280]{1,0:T(8,128)(2,1)}, bf16[1280,1280]{1,0:T(8,128)(2,1)}, u32[]{:S(2)}, u32[]{:S(2)}) collective-permute-start(bf16[1280,1280]{1,0:T(8,128)(2,1)} %refs_3_.1), channel_id=1, source_target_pairs={{0,1},{1,0},{2,3},{3,2},{4,5},{5,4},{6,7},{7,6}} | collective-permute-start | bytes 9830408 | tf_op jit(solution)/shard_map/ppermute | solution.py:372
  144.9 135.3 %collective-permute-start.16 = (bf16[1280,1280]{1,0:T(8,128)(2,1)}, bf16[1280,1280]{1,0:T(8,128)(2,1)}, u32[]{:S(2)}, u32[]{:S(2)}) collective-permute-start(bf16[1280,1280]{1,0:T(8,128)(2,1)} %refs_4_.1), channel_id=1, source_target_pairs={{0,1},{1,0},{2,3},{3,2},{4,5},{5,4},{6,7},{7,6}} | collective-permute-start | bytes 9830408 | tf_op jit(solution)/shard_map/ppermute | solution.py:372
  194.6 110.6 %collective-permute-start.18 = (bf16[1280,640]{1,0:T(8,128)(2,1)}, bf16[1280,640]{1,0:T(8,128)(2,1)}, u32[]{:S(2)}, u32[]{:S(2)}) collective-permute-start(bf16[1280,640]{1,0:T(8,128)(2,1)} %constant_dynamic-slice_fusion.2), channel_id=1, source_target_pairs={{0,2},{1,3},{2,0},{3,1},{4,6},{5,7},{6,4},{7,5}} | collective-permute-start | bytes 4915208 | tf_op jit(solution)/shard_map/ppermute | solution.py:372
  195.7 109.5 %collective-permute-start.20 = (bf16[640,1280]{1,0:T(8,128)(2,1)}, bf16[640,1280]{1,0:T(8,128)(2,1)}, u32[]{:S(2)}, u32[]{:S(2)}) collective-permute-start(bf16[640,1280]{1,0:T(8,128)(2,1)} %constant_dynamic-slice_fusion.1), channel_id=1, source_target_pairs={{0,2},{1,3},{2,0},{3,1},{4,6},{5,7},{6,4},{7,5}} | collective-permute-start | bytes 4915208 | tf_op jit(solution)/shard_map/ppermute | solution.py:372
  308.5 71.7 %collective-permute-start.17 = (bf16[1024,1280]{1,0:T(8,128)(2,1)}, bf16[1024,1280]{1,0:T(8,128)(2,1)}, u32[]{:S(2)}, u32[]{:S(2)}) collective-permute-start(bf16[1024,1280]{1,0:T(8,128)(2,1)} %fusion.18.refs_0_), channel_id=1, source_target_pairs={{0,1},{1,0},{2,3},{3,2},{4,5},{5,4},{6,7},{7,6}} | collective-permute-start | bytes 7864328 | tf_op jit(solution)/shard_map/ppermute | solution.py:372
  308.5 71.7 %collective-permute-start.23 = (bf16[1024,1280]{1,0:T(8,128)(2,1)}, bf16[1024,1280]{1,0:T(8,128)(2,1)}, u32[]{:S(2)}, u32[]{:S(2)}) collective-permute-start(bf16[1024,1280]{1,0:T(8,128)(2,1)} %get-tuple-element.89), channel_id=1, source_target_pairs={{0,1},{1,0},{2,3},{3,2},{4,5},{5,4},{6,7},{7,6}} | collective-permute-start | bytes 7864328 | tf_op jit(solution)/shard_map/ppermute | solution.py:372
  318.1 62.0 %collective-permute-start.24 = (bf16[1280,640]{1,0:T(8,128)(2,1)}, bf16[1280,640]{1,0:T(8,128)(2,1)}, u32[]{:S(2)}, u32[]{:S(2)}) collective-permute-start(bf16[1280,640]{1,0:T(8,128)(2,1)} %collective-permute-done.18.refs_3_), channel_id=1, source_target_pairs={{0,4},{4,0},{1,5},{5,1},{2,6},{6,2},{3,7},{7,3}} | collective-permute-start | bytes 4915208 | tf_op jit(solution)/shard_map/ppermute | solution.py:376
  318.6 72.5 %collective-permute-start.22 = (bf16[1024,1280]{1,0:T(8,128)(2,1)}, bf16[1024,1280]{1,0:T(8,128)(2,1)}, u32[]{:S(2)}, u32[]{:S(2)}) collective-permute-start(bf16[1024,1280]{1,0:T(8,128)(2,1)} %get-tuple-element.88), channel_id=1, source_target_pairs={{0,1},{1,0},{2,3},{3,2},{4,5},{5,4},{6,7},{7,6}} | collective-permute-start | bytes 7864328 | tf_op jit(solution)/shard_map/ppermute | solution.py:372
  485.2 90.7 %collective-permute-start.42 = (bf16[1024,1280]{1,0:T(8,128)(2,1)}, bf16[1024,1280]{1,0:T(8,128)(2,1)}, u32[]{:S(2)}, u32[]{:S(2)}) collective-permute-start(bf16[1024,1280]{1,0:T(8,128)(2,1)} %fusion.18.refs_0_), channel_id=1, source_target_pairs={{0,2},{1,3},{2,0},{3,1},{4,6},{5,7},{6,4},{7,5}} | collective-permute-start | bytes 7864328 | tf_op jit(solution)/shard_map/ppermute | solution.py:372
  486.2 87.1 %collective-permute-start.44 = (bf16[2,256,1280]{2,1,0:T(8,128)(2,1)}, bf16[2,256,1280]{2,1,0:T(8,128)(2,1)}, u32[]{:S(2)}, u32[]{:S(2)}) collective-permute-start(bf16[2,256,1280]{2,1,0:T(8,128)(2,1)} %get-tuple-element.126), channel_id=1, source_target_pairs={{0,2},{1,3},{2,0},{3,1},{4,6},{5,7},{6,4},{7,5}} | collective-permute-start | bytes 3932168 | tf_op jit(solution)/shard_map/ppermute | solution.py:372
  528.8 82.0 %collective-permute-start.32 = (f32[4,128,1280]{2,1,0:T(8,128)}, f32[4,128,1280]{2,1,0:T(8,128)}, u32[]{:S(2)}, u32[]{:S(2)}) collective-permute-start(f32[4,128,1280]{2,1,0:T(8,128)} %get-tuple-element.109), channel_id=1, source_target_pairs={{0,1},{1,0},{2,3},{3,2},{4,5},{5,4},{6,7},{7,6}} | collective-permute-start | bytes 7864328 | tf_op jit(solution)/shard_map/ppermute | solution.py:372
  585.9 114.2 %collective-permute-start.43 = (bf16[1024,1280]{1,0:T(8,128)(2,1)}, bf16[1024,1280]{1,0:T(8,128)(2,1)}, u32[]{:S(2)}, u32[]{:S(2)}) collective-permute-start(bf16[1024,1280]{1,0:T(8,128)(2,1)} %collective-permute-done.42), channel_id=1, source_target_pairs={{0,1},{1,0},{2,3},{3,2},{4,5},{5,4},{6,7},{7,6}} | collective-permute-start | bytes 7864328 | tf_op jit(solution)/shard_map/ppermute | solution.py:372
  609.4 228.9 %collective-permute-start.40 = (f32[4,192,1280]{2,1,0:T(8,128)}, f32[4,192,1280]{2,1,0:T(8,128)}, u32[]{:S(2)}, u32[]{:S(2)}) collective-permute-start(f32[4,192,1280]{2,1,0:T(8,128)} %add.217), channel_id=1, source_target_pairs={{0,2},{1,3},{2,0},{3,1},{4,6},{5,7},{6,4},{7,5}} | collective-permute-start | bytes 11796488 | tf_op jit(solution)/shard_map/ppermute | solution.py:372
  714.1 124.2 %collective-permute-start.39 = (f32[4,320,1280]{2,1,0:T(8,128)}, f32[4,320,1280]{2,1,0:T(8,128)}, u32[]{:S(2)}, u32[]{:S(2)}) collective-permute-start(f32[4,320,1280]{2,1,0:T(8,128)} %get-tuple-element.120), channel_id=1, source_target_pairs={{0,1},{1,0},{2,3},{3,2},{4,5},{5,4},{6,7},{7,6}} | collective-permute-start | bytes 19660808 | tf_op jit(solution)/shard_map/ppermute | solution.py:372
  741.0 97.3 %collective-permute-start.41 = (f32[4,128,1280]{2,1,0:T(8,128)}, f32[4,128,1280]{2,1,0:T(8,128)}, u32[]{:S(2)}, u32[]{:S(2)}) collective-permute-start(f32[4,128,1280]{2,1,0:T(8,128)} %add.219), channel_id=1, source_target_pairs={{0,2},{1,3},{2,0},{3,1},{4,6},{5,7},{6,4},{7,5}} | collective-permute-start | bytes 7864328 | tf_op jit(solution)/shard_map/ppermute | solution.py:372
  755.1 64.4 %collective-permute-start.33 = (bf16[256,1280]{1,0:T(8,128)(2,1)}, bf16[256,1280]{1,0:T(8,128)(2,1)}, u32[]{:S(2)}, u32[]{:S(2)}) collective-permute-start(bf16[256,1280]{1,0:T(8,128)(2,1)} %get-tuple-element.183), channel_id=1, source_target_pairs={{0,3},{1,2},{2,1},{3,0},{4,7},{5,6},{6,5},{7,4}} | collective-permute-start | bytes 1966088 | tf_op jit(solution)/shard_map/ppermute | solution.py:372
  757.2 57.3 %collective-permute-start.38 = (f32[8640]{0:T(1024)S(1)}, f32[8640]{0:T(1024)S(1)}, u32[]{:S(2)}, u32[]{:S(2)}) collective-permute-start(f32[8640]{0:T(1024)S(1)} %constant_dynamic-update-slice_fusion.15), channel_id=1, source_target_pairs={{0,3},{1,2},{2,1},{3,0},{4,7},{5,6},{6,5},{7,4}} | collective-permute-start | bytes 103688 | tf_op jit(solution)/shard_map/ppermute | solution.py:372
  (62 other events, 1740.8 us)

commit v5 on v4

--- a/solution.py
+++ b/solution.py
@@ -225,7 +225,7 @@
     return act, slope
 
 
-def mlp_kernel(tiles, n_w, chained, emit, *refs):
+def mlp_kernel(n_w, chained, emit, *refs):
     refs = list(refs)
     take = lambda n: [refs.pop(0) for _ in range(n)]
     h_ref, dy_ref, b_ref = take(3)
@@ -234,13 +234,12 @@
     y_ref, dh_ref = take(2)
     act_ref, dpre_ref, sum_ref = take(3) if emit else (None,) * 3
     wu, wd, sem = refs
-    width = wu.shape[2]
     step = pl.program_id(0)
+    width = wu.shape[0] // n_w
     copies = []
-    for t, (src, part) in enumerate(tiles):
-        cols = pl.ds(part * width, width)
-        copies.append((pltpu.make_async_copy(ups[src].at[:, cols], wu.at[t], sem.at[0, t]),
-                       pltpu.make_async_copy(downs[src].at[cols, :], wd.at[t], sem.at[1, t])))
+    for t in range(n_w):
+        cols = pl.ds(t * width, width)
+        copies.append((pltpu.make_async_copy(ups[t], wu.at[:, cols], sem.at[0, t]), pltpu.make_async_copy(downs[t], wd.at[cols, :], sem.at[1, t])))
 
     @pl.when(step == 0)
     def _():
@@ -248,56 +247,50 @@
             up.start()
             down.start()
 
-    y_sum, dh_sum = (before[0][...], before[1][...]) if chained else (None, None)
-    for t in range(len(tiles)):
-        @pl.when(step == 0)
-        def _(t=t):
-            copies[t][0].wait()
-            copies[t][1].wait()
-
-        pre = jnp.dot(h_ref[...], wu[t], preferred_element_type=F32) + b_ref[t]
-        act, slope = gelu_terms(pre)
-        act = act.astype(BF16)
-        d_act = lax.dot_general(dy_ref[...], wd[t], NT, preferred_element_type=F32)
-        y_part = jnp.dot(act, wd[t], preferred_element_type=F32)
-        d_pre = d_act * slope
-        d_low = d_pre.astype(BF16)
-        dh_part = lax.dot_general(d_low, wu[t], NT, preferred_element_type=F32)
-        y_sum = y_part if y_sum is None else y_sum + y_part
-        dh_sum = dh_part if dh_sum is None else dh_sum + dh_part
-        if emit:
-            cols = slice(t * width, (t + 1) * width)
-            act_ref[:, cols] = act
-            dpre_ref[:, cols] = d_low
-            total = jnp.broadcast_to(jnp.sum(d_pre, axis=0, keepdims=True), (8, width))
-            sum_ref[:, cols] = total + jnp.where(step == 0, 0.0, sum_ref[:, cols])
-    y_ref[...] = y_sum
-    dh_ref[...] = dh_sum
+    @pl.when(step == 0)
+    def _():
+        for up, down in copies:
+            up.wait()
+            down.wait()
+
+    pre = jnp.dot(h_ref[...], wu[...], preferred_element_type=F32) + b_ref[...]
+    act, slope = gelu_terms(pre)
+    act = act.astype(BF16)
+    d_pre = lax.dot_general(dy_ref[...], wd[...], NT, preferred_element_type=F32) * slope
+    d_low = d_pre.astype(BF16)
+    y_part = jnp.dot(act, wd[...], preferred_element_type=F32)
+    dh_part = lax.dot_general(d_low, wu[...], NT, preferred_element_type=F32)
+    y_ref[...] = before[0][...] + y_part if chained else y_part
+    dh_ref[...] = before[1][...] + dh_part if chained else dh_part
+    if emit:
+        act_ref[...] = act
+        dpre_ref[...] = d_low
+        total = jnp.broadcast_to(jnp.sum(d_pre, axis=0, keepdims=True), sum_ref.shape)
+        sum_ref[...] = total + jnp.where(step == 0, 0.0, sum_ref[...])
 
 
 def mlp_chain(h2, d_y, bias, ups, downs, before=(), emit=False):
     seq, dim = h2.shape
-    width = bias.shape[2]
-    tiles = [(i, p) for i, w in enumerate(ups) for p in range(w.shape[1] // width)]
+    bias = bias.reshape(1, -1)
+    width = bias.shape[1]
     rows = pl.BlockSpec((QB, dim), lambda j: (j, 0))
-    wide = pl.BlockSpec((QB, len(tiles) * width), lambda j: (j, 0))
+    wide = pl.BlockSpec((QB, width), lambda j: (j, 0))
     hbm = pl.BlockSpec(memory_space=pl.ANY)
     out = jax.ShapeDtypeStruct((seq, dim), F32)
-    low = jax.ShapeDtypeStruct((seq, len(tiles) * width), BF16)
+    low = jax.ShapeDtypeStruct((seq, width), BF16)
     out_specs, out_shape = [rows, rows], [out, out]
     if emit:
-        out_specs += [wide, wide, whole(8, len(tiles) * width)]
-        out_shape += [low, low, jax.ShapeDtypeStruct((8, len(tiles) * width), F32)]
+        out_specs += [wide, wide, whole(8, width)]
+        out_shape += [low, low, jax.ShapeDtypeStruct((8, width), F32)]
     return pl.pallas_call(
-        functools.partial(mlp_kernel, tiles, len(ups), bool(before), emit),
+        functools.partial(mlp_kernel, len(ups), bool(before), emit),
         grid=(seq // QB,),
-        in_specs=[rows, rows, whole(*bias.shape)] + [hbm] * (2 * len(ups)) + [rows] * len(before),
+        in_specs=[rows, rows, whole(1, width)] + [hbm] * (2 * len(ups)) + [rows] * len(before),
         out_specs=out_specs,
         out_shape=out_shape,
-        scratch_shapes=[pltpu.VMEM((len(tiles), dim, width), BF16), pltpu.VMEM((len(tiles), width, dim), BF16),
-                        pltpu.SemaphoreType.DMA((2, len(tiles)))],
+        scratch_shapes=[pltpu.VMEM((dim, width), BF16), pltpu.VMEM((width, dim), BF16), pltpu.SemaphoreType.DMA((2, len(ups)))],
         compiler_params=compiler_params(),
-        cost_estimate=cost(len(tiles) * 8 * seq * dim * width),
+        cost_estimate=cost(8 * seq * dim * width),
         name="mlp_chain",
     )(h2, d_y, bias, *ups, *downs, *before)
 
@@ -338,31 +331,32 @@
 
 
 def add_kernel(split, a_ref, b_ref, c0_ref, c1_ref, q_ref, o_ref):
-    part, head = pl.program_id(0), pl.program_id(1)
-    total = (a_ref[0] + b_ref[0]) + jnp.where(head < split, c0_ref[0], c1_ref[0])
+    part = pl.program_id(0)
+
+    def store(dst):
+        dst[:split] = (a_ref[0, :split] + b_ref[0, :split]) + c0_ref[0]
+        dst[split:] = (a_ref[0, split:] + b_ref[0, split:]) + c1_ref[0]
 
     @pl.when(part < 3)
     def _():
-        q_ref[0] = total
+        store(q_ref.at[0])
 
     @pl.when(part == 3)
     def _():
-        o_ref[...] = total
+        store(o_ref)
 
 
 def add_grads(a, b, c0, c1):
     parts, size, dim = a.shape
-    heads, split = size // HD, c0.shape[1] // HD
-    block = lambda f: pl.BlockSpec((1, HD, dim), f)
     last = parts - 1
+    block = lambda v: pl.BlockSpec((1,) + v.shape[1:], lambda p: (p, 0, 0))
     return pl.pallas_call(
-        functools.partial(add_kernel, split),
-        grid=(parts, heads),
-        in_specs=[block(lambda p, i: (p, i, 0)), block(lambda p, i: (p, i, 0)),
-                  block(lambda p, i: (p, jnp.minimum(i, split - 1), 0)), block(lambda p, i: (p, jnp.maximum(i - split, 0), 0))],
-        out_specs=[block(lambda p, i: (jnp.minimum(p, last - 1), jnp.where(p < last, i, heads - 1), 0)),
-                   pl.BlockSpec((HD, dim), lambda p, i: (jnp.where(p < last, 0, i), 0))],
+        functools.partial(add_kernel, c0.shape[1]),
+        grid=(parts,),
+        in_specs=[block(a), block(b), block(c0), block(c1)],
+        out_specs=[pl.BlockSpec((1, size, dim), lambda p: (jnp.minimum(p, last - 1), 0, 0)), whole(size, dim)],
         out_shape=[jax.ShapeDtypeStruct((last, size, dim), F32), jax.ShapeDtypeStruct((size, dim), F32)],
+        compiler_params=compiler_params(),
         cost_estimate=cost(10_000_000),
         name="add_grads",
     )(a, b, c0, c1)

time: 860 us -> 843 us (0.980)
  Pallas kernels: 358 us -> 338 us
    pallas_call x5, Pallas kernels: 116 us -> 95.8 us  [the longest x4 85.9 us: mlp_chain(): pl.pallas_call(functools.partial(mlp_kernel, len(ups), bool(before), emit...]
  transfers between devices with their start and end apart: 47 -> 47, of which waited for: 12 -> 12; matrix products, arithmetic and copies ran while one was open for 21% -> 21% of each run, Pallas kernels for 32% -> 31%
where the time goes in v5:
time: 843 us; the launch traced here: 839 us
  Pallas kernels  338 us (40%)
  waiting for transfers between devices  274 us (33%)
  matrix products  101 us (12%)
  other arithmetic  64.9 us (8%)
  local copies, waits for them, and re-layouts  29.5 us (3%)
  starting transfers between devices  28.6 us (3%)
    ppermute x45, waiting for transfers between devices, xor_move(): return lax.ppermute(value, 'tp', [(i, i ^ bits) for i in range(4)])  243 us
    pallas_call x3, Pallas kernels, attn_bwd(): pl.pallas_call(attn_bwd_kernel, grid=(count,), in_specs=[whole(seq, dim),...  147 us
    pallas_call x4, Pallas kernels, mlp_chain(): pl.pallas_call(functools.partial(mlp_kernel, len(ups), bool(before), emit...  85.9 us
    pallas_call x2, Pallas kernels, attn_fwd(): pl.pallas_call(attn_fwd_kernel, grid=(heads,), in_specs=[whole(seq, dim),...  84.1 us
    dot_general x6, matrix products, grad_dot(): lax.dot_general(a, b, (((0,), (0,)), ((), ())), preferred_element_type=F32)  62.7 us
    ppermute x2, waiting for transfers between devices, swap_groups(): return lax.ppermute(value, 'dp', [(0, 1), (1, 0)])  31 us
    ppermute x45, starting transfers between devices, xor_move(): return lax.ppermute(value, 'tp', [(i, i ^ bits) for i in range(4)])  26.6 us
    reduce_sum x3, other arithmetic, layer(): jnp.sum(v, axis=0)  19.9 us
  transfers between devices with their start and end apart: 47, of which 12 were waited for; matrix products, arithmetic and copies ran while one was open for 21% of the time, Pallas kernels for 31%

profile of v5, /device:TPU:0, one launch (start us, length us, event | category | flops | bytes accessed | tf_op | source)
XLA Modules:
  0.0 838.5 jit_solution(11735545280077956001)
XLA Ops:
  22.6 67.2 %collective-permute-done.8 = f32[2240]{0:T(1024)S(1)} collective-permute-done((f32[2240]{0:T(1024)S(1)}, f32[2240]{0:T(1024)S(1)}, u32[]{:S(2)}, u32[]{:S(2)}) %collective-permute-start.8) | collective-permute-done | bytes 8992 | tf_op jit(solution)/shard_map/ppermute | solution.py:366
  103.9 13.8 %collective-permute-done.10.wo0_ref = bf16[5,64,1280]{2,1,0:T(8,128)(2,1)S(1)} collective-permute-done((bf16[5,64,1280]{2,1,0:T(8,128)(2,1)}, bf16[5,64,1280]{2,1,0:T(8,128)(2,1)S(1)}, u32[]{:S(2)}, u32[]{:S(2)}) %collective-permute-start.10) | collective-permute-done | bytes 819232 | tf_op jit(solution)/shard_map/ppermute | solution.py:366
  125.8 19.6 %collective-permute-done.13.refs_2_ = bf16[2,256,1280]{2,1,0:T(8,128)(2,1)} collective-permute-done((bf16[2,256,1280]{2,1,0:T(8,128)(2,1)}, bf16[2,256,1280]{2,1,0:T(8,128)(2,1)}, u32[]{:S(2)}, u32[]{:S(2)}) %collective-permute-start.13) | collective-permute-done | bytes 1310752 | tf_op jit(solution)/shard_map/ppermute | solution.py:366
  146.9 41.9 %attn_fwd.2 = (bf16[1024,640]{1,0:T(8,128)(2,1)}, bf16[1024,640]{1,0:T(8,128)(2,1)}, bf16[1024,640]{1,0:T(8,128)(2,1)}, bf16[1024,640]{1,0:T(8,128)(2,1)}, f32[5,8,1024]{2,1,0:T(8,128)}) custom-call(bf16[1024,1280]{1,0:T(8,128)(2,1)} %fusion.25.h_ref, bf16[3,320,1280]{2,1,0:T(8,128)(2,1)} %bitcast.90, bf16[3,320,1280]{2,1,0:T(8,128)(2,1)} %collective-permute-done.3.w1_ref, ...), custom_call_target="tpu_custom_call" | custom-call | flops 12079595520 | bytes 20000000 | tf_op jit(solution)/shard_map/attn_fwd/pallas_call | solution.py:121
  202.8 42.2 %attn_fwd.3 = (bf16[1024,640]{1,0:T(8,128)(2,1)}, bf16[1024,640]{1,0:T(8,128)(2,1)}, bf16[1024,640]{1,0:T(8,128)(2,1)}, bf16[1024,640]{1,0:T(8,128)(2,1)}, f32[5,8,1024]{2,1,0:T(8,128)}) custom-call(bf16[1024,1280]{1,0:T(8,128)(2,1)} %fusion.25.h_ref, bf16[3,320,1280]{2,1,0:T(8,128)(2,1)} %collective-permute-done.6.w0_ref, ...), custom_call_target="tpu_custom_call" | custom-call | flops 12079595520 | bytes 20000000 | tf_op jit(solution)/shard_map/attn_fwd/pallas_call | solution.py:121
  254.7 20.7 %mlp_chain.4 = (f32[1024,1280]{1,0:T(8,128)}, f32[1024,1280]{1,0:T(8,128)}, bf16[1024,1280]{1,0:T(8,128)(2,1)}, bf16[1024,1280]{1,0:T(8,128)(2,1)}, f32[8,1280]{1,0:T(8,128)}) custom-call(bf16[1024,1280]{1,0:T(8,128)(2,1)} %fusion.18.refs_0_, bf16[1024,1280]{1,0:T(8,128)(2,1)} %get-tuple-element.81.refs_1_, f32[1,1280]{1,0:T(1,128)} %reshape_reshape.7.refs_2_, ...), custom_call_target="tpu_custom_call" | custom-call | flops 13421772800 | bytes 20000000 | tf_op jit(solution)/shard_map/mlp_chain/pallas_call | solution.py:285
  275.4 22.1 %mlp_chain.5 = (f32[1024,1280]{1,0:T(8,128)}, f32[1024,1280]{1,0:T(8,128)}, bf16[1024,1280]{1,0:T(8,128)(2,1)}, bf16[1024,1280]{1,0:T(8,128)(2,1)}, f32[8,1280]{1,0:T(8,128)}) custom-call(bf16[1024,1280]{1,0:T(8,128)(2,1)} %fusion.18.refs_0_, bf16[1024,1280]{1,0:T(8,128)(2,1)} %get-tuple-element.81.refs_1_, f32[1,1280]{1,0:T(1,128)} %reshape_reshape.6.refs_2_, ...), custom_call_target="tpu_custom_call" | custom-call | flops 13421772800 | bytes 20000000 | tf_op jit(solution)/shard_map/mlp_chain/pallas_call | solution.py:285
  319.7 21.6 %mlp_chain.6 = (f32[1024,1280]{1,0:T(8,128)}, f32[1024,1280]{1,0:T(8,128)}) custom-call(bf16[1024,1280]{1,0:T(8,128)(2,1)} %fusion.18.refs_0_, bf16[1024,1280]{1,0:T(8,128)(2,1)} %get-tuple-element.81.refs_1_, f32[1,1280]{1,0:T(1,128)} %bitcast.86, bf16[1280,640]{1,0:T(8,128)(2,1)} %collective-permute-done.18.refs_3_, bf16[1280,640]{1,0:T(8,128)(2,1)} %copy-done.28, ...), custom_call_target="tpu_custom_call" | custom-call | flops 13421772800 | bytes 20000000 | tf_op jit(solution)/shard_map/mlp_chain/pallas_call | solution.py:285
  341.4 31.0 %collective-permute-done.24.refs_3_ = bf16[1280,640]{1,0:T(8,128)(2,1)} collective-permute-done((bf16[1280,640]{1,0:T(8,128)(2,1)}, bf16[1280,640]{1,0:T(8,128)(2,1)}, u32[]{:S(2)}, u32[]{:S(2)}) %collective-permute-start.24) | collective-permute-done | bytes 1638432 | tf_op jit(solution)/shard_map/ppermute | solution.py:370
  372.5 10.9 %convolution_add_fusion.2 = f32[1280,1280]{1,0:T(8,128)} fusion(f32[1280,1280]{1,0:T(8,128)} %fusion.55, bf16[1024,1280]{1,0:T(8,128)(2,1)} %collective-permute-done.23, bf16[1024,1280]{1,0:T(8,128)(2,1)} %get-tuple-element.91), kind=kOutput, calls=%fused_computation.10 | convolution fusion | flops 3357081600 | bytes 18350080 | tf_op jit(solution)/shard_map/dot_general | solution.py:456
  392.5 21.5 %mlp_chain.7 = (f32[1024,1280]{1,0:T(8,128)}, f32[1024,1280]{1,0:T(8,128)}) custom-call(bf16[1024,1280]{1,0:T(8,128)(2,1)} %fusion.18.refs_0_, bf16[1024,1280]{1,0:T(8,128)(2,1)} %get-tuple-element.81.refs_1_, f32[1,1280]{1,0:T(1,128)} %bitcast.85, bf16[1280,640]{1,0:T(8,128)(2,1)} %collective-permute-done.24.refs_3_, ...), custom_call_target="tpu_custom_call" | custom-call | flops 13421772800 | bytes 20000000 | tf_op jit(solution)/shard_map/mlp_chain/pallas_call | solution.py:285
  429.8 44.6 %attn_bwd.3 = (f32[1024,1280]{1,0:T(8,128)}, f32[4,192,1280]{2,1,0:T(8,128)}, f32[4,192,1280]{2,1,0:T(8,128)}, f32[3,8,128]{2,1,0:T(8,128)}) custom-call(bf16[1024,1280]{1,0:T(8,128)(2,1)} %fusion.25.h_ref, bf16[1024,1280]{1,0:T(8,128)(2,1)} %convert_element_type.53.dx_ref, bf16[3,320,1280]{2,1,0:T(8,128)(2,1)} %collective-permute-done.6.w0_ref, ...), custom_call_target="tpu_custom_call" | custom-call | flops 14495514624 | bytes 20000000 | tf_op jit(solution)/shard_map/attn_bwd/pallas_call | solution.py:207
  486.3 32.3 %attn_bwd.4 = (f32[1024,1280]{1,0:T(8,128)}, f32[4,128,1280]{2,1,0:T(8,128)}, f32[4,128,1280]{2,1,0:T(8,128)}, f32[2,8,128]{2,1,0:T(8,128)}) custom-call(bf16[1024,1280]{1,0:T(8,128)(2,1)} %fusion.25.h_ref, bf16[1024,1280]{1,0:T(8,128)(2,1)} %convert_element_type.53.dx_ref, bf16[3,320,1280]{2,1,0:T(8,128)(2,1)} %collective-permute-done.6.w0_ref, ...), custom_call_target="tpu_custom_call" | custom-call | flops 9663676416 | bytes 20000000 | tf_op jit(solution)/shard_map/attn_bwd/pallas_call | solution.py:207
  521.5 41.6 %collective-permute-done.44.refs_0_ = bf16[2,256,1280]{2,1,0:T(8,128)(2,1)} collective-permute-done((bf16[2,256,1280]{2,1,0:T(8,128)(2,1)}, bf16[2,256,1280]{2,1,0:T(8,128)(2,1)}, u32[]{:S(2)}, u32[]{:S(2)}) %collective-permute-start.44) | collective-permute-done | bytes 1310752 | tf_op jit(solution)/shard_map/ppermute | solution.py:366
  566.2 9.5 %collective-permute-done.28 = bf16[256,1280]{1,0:T(8,128)(2,1)S(1)} collective-permute-done((bf16[256,1280]{1,0:T(8,128)(2,1)}, bf16[256,1280]{1,0:T(8,128)(2,1)S(1)}, u32[]{:S(2)}, u32[]{:S(2)}) %collective-permute-start.28) | collective-permute-done | bytes 655392 | tf_op jit(solution)/shard_map/ppermute | solution.py:366
  576.9 13.4 %collective-permute-done.29 = bf16[256,1280]{1,0:T(8,128)(2,1)} collective-permute-done((bf16[256,1280]{1,0:T(8,128)(2,1)}, bf16[256,1280]{1,0:T(8,128)(2,1)}, u32[]{:S(2)}, u32[]{:S(2)}) %collective-permute-start.29) | collective-permute-done | bytes 655392 | tf_op jit(solution)/shard_map/ppermute | solution.py:366
  604.1 70.2 %attn_bwd.5 = (f32[1024,1280]{1,0:T(8,128)}, f32[4,320,1280]{2,1,0:T(8,128)}, f32[4,320,1280]{2,1,0:T(8,128)}, f32[5,8,128]{2,1,0:T(8,128)}) custom-call(bf16[1024,1280]{1,0:T(8,128)(2,1)} %fusion.25.h_ref, bf16[1024,1280]{1,0:T(8,128)(2,1)} %convert_element_type.53.dx_ref, bf16[3,320,1280]{2,1,0:T(8,128)(2,1)} %bitcast.91, ...), custom_call_target="tpu_custom_call" | custom-call | flops 24159191040 | bytes 20000000 | tf_op jit(solution)/shard_map/attn_bwd/pallas_call | solution.py:207
  692.0 11.9 %fusion.56 = f32[2048,1280]{1,0:T(8,128)} fusion(bf16[2048,1280]{1,0:T(8,128)(2,1)S(1)} %constant_dynamic-update-slice_fusion.5, bf16[1280,1280]{1,0:T(8,128)(2,1)} %refs_3_.1), kind=kOutput, calls=%fused_computation.165 | convolution fusion | flops 6710886400 | bytes 19005440 | tf_op jit(solution)/shard_map/dot_general | solution.py:510
  703.9 13.9 %fusion.52 = (f32[1280]{0:T(1024)S(1)}, bf16[2048,1280]{1,0:T(8,128)(2,1)}) fusion(f32[2048,1280]{1,0:T(8,128)} %fusion.56, f32[1280]{0:T(1024)S(1)} %copy-done.21, bf16[2048,1280]{1,0:T(8,128)(2,1)S(1)} %bitcast.76, bf16[1280,1280]{1,0:T(8,128)(2,1)} %refs_4_.1), kind=kOutput, calls=%fused_computation.161 | convolution fusion | flops 6742342656 | bytes 24258560 | tf_op jit(solution)/shard_map/dot_general | solution.py:513
  717.8 13.1 %convolution_add_fusion = f32[1280,1280]{1,0:T(8,128)} fusion(f32[1280,1280]{1,0:T(8,128)} %convolution_add_fusion.2, bf16[2048,1280]{1,0:T(8,128)(2,1)S(1)} %bitcast.76, f32[2048,1280]{1,0:T(8,128)} %fusion.56, f32[1280]{0:T(1024)S(1)} %copy-done.21), kind=kOutput, calls=%fused_computation.8 | convolution fusion | flops 6728253440 | bytes 28840960 | tf_op jit(solution)/shard_map/dot_general | solution.py:456
  731.8 11.8 %convolution_add_fusion.1 = f32[1280,1280]{1,0:T(8,128)} fusion(f32[1280,1280]{1,0:T(8,128)S(1)} %bitcast.94, bf16[2048,1280]{1,0:T(8,128)(2,1)S(1)} %constant_dynamic-update-slice_fusion.5, bf16[2048,1280]{1,0:T(8,128)(2,1)} %get-tuple-element.235), kind=kOutput, calls=%fused_computation.9 | convolution fusion | flops 6712524800 | bytes 23592960 | tf_op jit(solution)/shard_map/dot_general | solution.py:456
  748.0 56.3 %collective-permute-done.38 = f32[8640]{0:T(1024)S(1)} collective-permute-done((f32[8640]{0:T(1024)S(1)}, f32[8640]{0:T(1024)S(1)}, u32[]{:S(2)}, u32[]{:S(2)}) %collective-permute-start.38) | collective-permute-done | bytes 34592 | tf_op jit(solution)/shard_map/ppermute | solution.py:366
  810.6 14.0 %collective-permute-done.34 = bf16[256,1280]{1,0:T(8,128)(2,1)} collective-permute-done((bf16[256,1280]{1,0:T(8,128)(2,1)}, bf16[256,1280]{1,0:T(8,128)(2,1)}, u32[]{:S(2)}, u32[]{:S(2)}) %collective-permute-start.34) | collective-permute-done | bytes 655392 | tf_op jit(solution)/shard_map/ppermute | solution.py:366
  828.1 10.0 %add_grads.1 = (f32[3,320,1280]{2,1,0:T(8,128)}, f32[320,1280]{1,0:T(8,128)}) custom-call(f32[4,320,1280]{2,1,0:T(8,128)} %get-tuple-element.119.a_ref, f32[4,320,1280]{2,1,0:T(8,128)} %collective-permute-done.39.b_ref, f32[4,192,1280]{2,1,0:T(8,128)} %collective-permute-done.40.c0_ref, f32[4,128,1280]{2,1,0:T(8,128)} %collective-permute-done.41.c1_ref), custom_call_target="tpu_custom_call" | custom-call | flops 10000000 | bytes 20000000 | tf_op jit(solution)/shard_map/add_grads/pallas_call | solution.py:353
  (282 shorter events, 181.7 us)
Async XLA Ops:
  3.9 92.4 %collective-permute-start = (bf16[256,1280]{1,0:T(8,128)(2,1)}, bf16[256,1280]{1,0:T(8,128)(2,1)}, u32[]{:S(2)}, u32[]{:S(2)}) collective-permute-start(bf16[256,1280]{1,0:T(8,128)(2,1)} %get-tuple-element.188), channel_id=1, source_target_pairs={{0,1},{1,0},{2,3},{3,2},{4,5},{5,4},{6,7},{7,6}} | collective-permute-start | bytes 1966088 | tf_op jit(solution)/shard_map/ppermute | solution.py:366
  4.7 91.6 %collective-permute-start.1 = (bf16[256,1280]{1,0:T(8,128)(2,1)}, bf16[256,1280]{1,0:T(8,128)(2,1)}, u32[]{:S(2)}, u32[]{:S(2)}) collective-permute-start(bf16[256,1280]{1,0:T(8,128)(2,1)} %get-tuple-element.190), channel_id=1, source_target_pairs={{0,2},{1,3},{2,0},{3,1},{4,6},{5,7},{6,4},{7,5}} | collective-permute-start | bytes 1966088 | tf_op jit(solution)/shard_map/ppermute | solution.py:366
  7.2 90.7 %collective-permute-start.2 = (bf16[256,1280]{1,0:T(8,128)(2,1)}, bf16[256,1280]{1,0:T(8,128)(2,1)}, u32[]{:S(2)}, u32[]{:S(2)}) collective-permute-start(bf16[256,1280]{1,0:T(8,128)(2,1)} %get-tuple-element.189), channel_id=1, source_target_pairs={{0,3},{1,2},{2,1},{3,0},{4,7},{5,6},{6,5},{7,4}} | collective-permute-start | bytes 1966088 | tf_op jit(solution)/shard_map/ppermute | solution.py:366
  7.5 110.2 %collective-permute-start.6 = (bf16[3,320,1280]{2,1,0:T(8,128)(2,1)}, bf16[3,320,1280]{2,1,0:T(8,128)(2,1)}, u32[]{:S(2)}, u32[]{:S(2)}) collective-permute-start(bf16[3,320,1280]{2,1,0:T(8,128)(2,1)} %bitcast.88), channel_id=1, source_target_pairs={{0,2},{1,3},{2,0},{3,1},{4,6},{5,7},{6,4},{7,5}} | collective-permute-start | bytes 7372808 | tf_op jit(solution)/shard_map/ppermute | solution.py:366
  19.8 69.9 %collective-permute-start.8 = (f32[2240]{0:T(1024)S(1)}, f32[2240]{0:T(1024)S(1)}, u32[]{:S(2)}, u32[]{:S(2)}) collective-permute-start(f32[2240]{0:T(1024)S(1)} %constant_dynamic-update-slice_fusion.7), channel_id=1, source_target_pairs={{0,2},{1,3},{2,0},{3,1},{4,6},{5,7},{6,4},{7,5}} | collective-permute-start | bytes 26888 | tf_op jit(solution)/shard_map/ppermute | solution.py:366
  103.9 92.3 %collective-permute-start.12 = (bf16[4,256,1280]{2,1,0:T(8,128)(2,1)S(1)}, bf16[4,256,1280]{2,1,0:T(8,128)(2,1)}, u32[]{:S(2)}, u32[]{:S(2)}) collective-permute-start(bf16[4,256,1280]{2,1,0:T(8,128)(2,1)S(1)} %copy-done.3), channel_id=1, source_target_pairs={{0,1},{1,0},{2,3},{3,2},{4,5},{5,4},{6,7},{7,6}} | collective-permute-start | bytes 7864328 | tf_op jit(solution)/shard_map/ppermute | solution.py:366
  117.7 85.1 %collective-permute-start.7 = (bf16[3,320,1280]{2,1,0:T(8,128)(2,1)}, bf16[3,320,1280]{2,1,0:T(8,128)(2,1)}, u32[]{:S(2)}, u32[]{:S(2)}) collective-permute-start(bf16[3,320,1280]{2,1,0:T(8,128)(2,1)} %collective-permute-done.6.w0_ref), channel_id=1, source_target_pairs={{0,1},{1,0},{2,3},{3,2},{4,5},{5,4},{6,7},{7,6}} | collective-permute-start | bytes 7372808 | tf_op jit(solution)/shard_map/ppermute | solution.py:366
  124.3 151.1 %collective-permute-start.15 = (bf16[1280,1280]{1,0:T(8,128)(2,1)}, bf16[1280,1280]{1,0:T(8,128)(2,1)}, u32[]{:S(2)}, u32[]{:S(2)}) collective-permute-start(bf16[1280,1280]{1,0:T(8,128)(2,1)} %refs_3_.1), channel_id=1, source_target_pairs={{0,1},{1,0},{2,3},{3,2},{4,5},{5,4},{6,7},{7,6}} | collective-permute-start | bytes 9830408 | tf_op jit(solution)/shard_map/ppermute | solution.py:366
  145.4 130.0 %collective-permute-start.16 = (bf16[1280,1280]{1,0:T(8,128)(2,1)}, bf16[1280,1280]{1,0:T(8,128)(2,1)}, u32[]{:S(2)}, u32[]{:S(2)}) collective-permute-start(bf16[1280,1280]{1,0:T(8,128)(2,1)} %refs_4_.1), channel_id=1, source_target_pairs={{0,1},{1,0},{2,3},{3,2},{4,5},{5,4},{6,7},{7,6}} | collective-permute-start | bytes 9830408 | tf_op jit(solution)/shard_map/ppermute | solution.py:366
  195.1 102.3 %collective-permute-start.18 = (bf16[1280,640]{1,0:T(8,128)(2,1)}, bf16[1280,640]{1,0:T(8,128)(2,1)}, u32[]{:S(2)}, u32[]{:S(2)}) collective-permute-start(bf16[1280,640]{1,0:T(8,128)(2,1)} %constant_dynamic-slice_fusion.2), channel_id=1, source_target_pairs={{0,2},{1,3},{2,0},{3,1},{4,6},{5,7},{6,4},{7,5}} | collective-permute-start | bytes 4915208 | tf_op jit(solution)/shard_map/ppermute | solution.py:366
  196.2 101.3 %collective-permute-start.20 = (bf16[640,1280]{1,0:T(8,128)(2,1)}, bf16[640,1280]{1,0:T(8,128)(2,1)}, u32[]{:S(2)}, u32[]{:S(2)}) collective-permute-start(bf16[640,1280]{1,0:T(8,128)(2,1)} %constant_dynamic-slice_fusion.1), channel_id=1, source_target_pairs={{0,2},{1,3},{2,0},{3,1},{4,6},{5,7},{6,4},{7,5}} | collective-permute-start | bytes 4915208 | tf_op jit(solution)/shard_map/ppermute | solution.py:366
  300.8 71.7 %collective-permute-start.17 = (bf16[1024,1280]{1,0:T(8,128)(2,1)}, bf16[1024,1280]{1,0:T(8,128)(2,1)}, u32[]{:S(2)}, u32[]{:S(2)}) collective-permute-start(bf16[1024,1280]{1,0:T(8,128)(2,1)} %fusion.18.refs_0_), channel_id=1, source_target_pairs={{0,1},{1,0},{2,3},{3,2},{4,5},{5,4},{6,7},{7,6}} | collective-permute-start | bytes 7864328 | tf_op jit(solution)/shard_map/ppermute | solution.py:366
  300.8 71.7 %collective-permute-start.23 = (bf16[1024,1280]{1,0:T(8,128)(2,1)}, bf16[1024,1280]{1,0:T(8,128)(2,1)}, u32[]{:S(2)}, u32[]{:S(2)}) collective-permute-start(bf16[1024,1280]{1,0:T(8,128)(2,1)} %get-tuple-element.89), channel_id=1, source_target_pairs={{0,1},{1,0},{2,3},{3,2},{4,5},{5,4},{6,7},{7,6}} | collective-permute-start | bytes 7864328 | tf_op jit(solution)/shard_map/ppermute | solution.py:366
  310.4 62.1 %collective-permute-start.24 = (bf16[1280,640]{1,0:T(8,128)(2,1)}, bf16[1280,640]{1,0:T(8,128)(2,1)}, u32[]{:S(2)}, u32[]{:S(2)}) collective-permute-start(bf16[1280,640]{1,0:T(8,128)(2,1)} %collective-permute-done.18.refs_3_), channel_id=1, source_target_pairs={{0,4},{4,0},{1,5},{5,1},{2,6},{6,2},{3,7},{7,3}} | collective-permute-start | bytes 4915208 | tf_op jit(solution)/shard_map/ppermute | solution.py:370
  310.9 72.5 %collective-permute-start.22 = (bf16[1024,1280]{1,0:T(8,128)(2,1)}, bf16[1024,1280]{1,0:T(8,128)(2,1)}, u32[]{:S(2)}, u32[]{:S(2)}) collective-permute-start(bf16[1024,1280]{1,0:T(8,128)(2,1)} %get-tuple-element.88), channel_id=1, source_target_pairs={{0,1},{1,0},{2,3},{3,2},{4,5},{5,4},{6,7},{7,6}} | collective-permute-start | bytes 7864328 | tf_op jit(solution)/shard_map/ppermute | solution.py:366
  475.0 90.7 %collective-permute-start.42 = (bf16[1024,1280]{1,0:T(8,128)(2,1)}, bf16[1024,1280]{1,0:T(8,128)(2,1)}, u32[]{:S(2)}, u32[]{:S(2)}) collective-permute-start(bf16[1024,1280]{1,0:T(8,128)(2,1)} %fusion.18.refs_0_), channel_id=1, source_target_pairs={{0,2},{1,3},{2,0},{3,1},{4,6},{5,7},{6,4},{7,5}} | collective-permute-start | bytes 7864328 | tf_op jit(solution)/shard_map/ppermute | solution.py:366
  476.0 87.1 %collective-permute-start.44 = (bf16[2,256,1280]{2,1,0:T(8,128)(2,1)}, bf16[2,256,1280]{2,1,0:T(8,128)(2,1)}, u32[]{:S(2)}, u32[]{:S(2)}) collective-permute-start(bf16[2,256,1280]{2,1,0:T(8,128)(2,1)} %get-tuple-element.126), channel_id=1, source_target_pairs={{0,2},{1,3},{2,0},{3,1},{4,6},{5,7},{6,4},{7,5}} | collective-permute-start | bytes 3932168 | tf_op jit(solution)/shard_map/ppermute | solution.py:366
  518.6 82.0 %collective-permute-start.32 = (f32[4,128,1280]{2,1,0:T(8,128)}, f32[4,128,1280]{2,1,0:T(8,128)}, u32[]{:S(2)}, u32[]{:S(2)}) collective-permute-start(f32[4,128,1280]{2,1,0:T(8,128)} %get-tuple-element.109), channel_id=1, source_target_pairs={{0,1},{1,0},{2,3},{3,2},{4,5},{5,4},{6,7},{7,6}} | collective-permute-start | bytes 7864328 | tf_op jit(solution)/shard_map/ppermute | solution.py:366
  575.7 114.2 %collective-permute-start.43 = (bf16[1024,1280]{1,0:T(8,128)(2,1)}, bf16[1024,1280]{1,0:T(8,128)(2,1)}, u32[]{:S(2)}, u32[]{:S(2)}) collective-permute-start(bf16[1024,1280]{1,0:T(8,128)(2,1)} %collective-permute-done.42), channel_id=1, source_target_pairs={{0,1},{1,0},{2,3},{3,2},{4,5},{5,4},{6,7},{7,6}} | collective-permute-start | bytes 7864328 | tf_op jit(solution)/shard_map/ppermute | solution.py:366
  599.2 228.9 %collective-permute-start.40 = (f32[4,192,1280]{2,1,0:T(8,128)}, f32[4,192,1280]{2,1,0:T(8,128)}, u32[]{:S(2)}, u32[]{:S(2)}) collective-permute-start(f32[4,192,1280]{2,1,0:T(8,128)} %add.217), channel_id=1, source_target_pairs={{0,2},{1,3},{2,0},{3,1},{4,6},{5,7},{6,4},{7,5}} | collective-permute-start | bytes 11796488 | tf_op jit(solution)/shard_map/ppermute | solution.py:366
  703.9 124.2 %collective-permute-start.39 = (f32[4,320,1280]{2,1,0:T(8,128)}, f32[4,320,1280]{2,1,0:T(8,128)}, u32[]{:S(2)}, u32[]{:S(2)}) collective-permute-start(f32[4,320,1280]{2,1,0:T(8,128)} %get-tuple-element.120), channel_id=1, source_target_pairs={{0,1},{1,0},{2,3},{3,2},{4,5},{5,4},{6,7},{7,6}} | collective-permute-start | bytes 19660808 | tf_op jit(solution)/shard_map/ppermute | solution.py:366
  730.9 97.3 %collective-permute-start.41 = (f32[4,128,1280]{2,1,0:T(8,128)}, f32[4,128,1280]{2,1,0:T(8,128)}, u32[]{:S(2)}, u32[]{:S(2)}) collective-permute-start(f32[4,128,1280]{2,1,0:T(8,128)} %add.219), channel_id=1, source_target_pairs={{0,2},{1,3},{2,0},{3,1},{4,6},{5,7},{6,4},{7,5}} | collective-permute-start | bytes 7864328 | tf_op jit(solution)/shard_map/ppermute | solution.py:366
  744.9 64.4 %collective-permute-start.33 = (bf16[256,1280]{1,0:T(8,128)(2,1)}, bf16[256,1280]{1,0:T(8,128)(2,1)}, u32[]{:S(2)}, u32[]{:S(2)}) collective-permute-start(bf16[256,1280]{1,0:T(8,128)(2,1)} %get-tuple-element.183), channel_id=1, source_target_pairs={{0,3},{1,2},{2,1},{3,0},{4,7},{5,6},{6,5},{7,4}} | collective-permute-start | bytes 1966088 | tf_op jit(solution)/shard_map/ppermute | solution.py:366
  747.1 57.3 %collective-permute-start.38 = (f32[8640]{0:T(1024)S(1)}, f32[8640]{0:T(1024)S(1)}, u32[]{:S(2)}, u32[]{:S(2)}) collective-permute-start(f32[8640]{0:T(1024)S(1)} %constant_dynamic-update-slice_fusion.15), channel_id=1, source_target_pairs={{0,3},{1,2},{2,1},{3,0},{4,7},{5,6},{6,5},{7,4}} | collective-permute-start | bytes 103688 | tf_op jit(solution)/shard_map/ppermute | solution.py:366
  (62 other events, 1742.5 us)

commit v6 on v5

--- a/solution.py
+++ b/solution.py
@@ -180,19 +180,16 @@
     gb_ref[0] = jnp.concatenate([sums[:, :LANES], sums[:, LANES:256], sums[:, 256:], jnp.zeros((5, LANES), F32)], axis=0)
     d_low = d_all.astype(BF16)
     w = pair_rows(w0_ref, w1_ref)
-    part = jnp.dot(d_low, w, preferred_element_type=F32)
     gw = jnp.dot(d_low.T, h_ref[...], preferred_element_type=F32)
     for i in range(3):
         gw0_ref[i] = gw[LANES * i:LANES * i + HD]
-        gw1_ref[i] = gw[LANES * i + HD:LANES * i + LANES]
+        gw1_ref[i] = gw[LANES * i + HD:LANES * (i + 1)]
 
     @pl.when(pl.program_id(0) == 0)
     def _():
-        dh_ref[...] = part
-
-    @pl.when(pl.program_id(0) > 0)
-    def _():
-        dh_ref[...] += part
+        dh_ref[...] = jnp.zeros_like(dh_ref)
+
+    dh_ref[...] += jnp.dot(d_low, w, preferred_element_type=F32)
 
 
 def attn_bwd(h1, d_x1, w0, w1, wo0, wo1, q, k, v, o, lse, cos_tab, sin_tab, mask_col, first, count):
@@ -225,13 +222,13 @@
     return act, slope
 
 
-def mlp_kernel(n_w, chained, emit, *refs):
+def mlp_kernel(n_w, chained, emit, chain, *refs):
     refs = list(refs)
     take = lambda n: [refs.pop(0) for _ in range(n)]
     h_ref, dy_ref, b_ref = take(3)
     ups, downs = take(n_w), take(n_w)
     before = take(2) if chained else None
-    y_ref, dh_ref = take(2)
+    y_ref, dh_ref = take(2) if chain else (None, None)
     act_ref, dpre_ref, sum_ref = take(3) if emit else (None,) * 3
     wu, wd, sem = refs
     step = pl.program_id(0)
@@ -258,10 +255,11 @@
     act = act.astype(BF16)
     d_pre = lax.dot_general(dy_ref[...], wd[...], NT, preferred_element_type=F32) * slope
     d_low = d_pre.astype(BF16)
-    y_part = jnp.dot(act, wd[...], preferred_element_type=F32)
-    dh_part = lax.dot_general(d_low, wu[...], NT, preferred_element_type=F32)
-    y_ref[...] = before[0][...] + y_part if chained else y_part
-    dh_ref[...] = before[1][...] + dh_part if chained else dh_part
+    if chain:
+        y_part = jnp.dot(act, wd[...], preferred_element_type=F32)
+        dh_part = lax.dot_general(d_low, wu[...], NT, preferred_element_type=F32)
+        y_ref[...] = before[0][...] + y_part if chained else y_part
+        dh_ref[...] = before[1][...] + dh_part if chained else dh_part
     if emit:
         act_ref[...] = act
         dpre_ref[...] = d_low
@@ -269,7 +267,7 @@
         sum_ref[...] = total + jnp.where(step == 0, 0.0, sum_ref[...])
 
 
-def mlp_chain(h2, d_y, bias, ups, downs, before=(), emit=False):
+def mlp_chain(h2, d_y, bias, ups, downs, before=(), emit=False, chain=True):
     seq, dim = h2.shape
     bias = bias.reshape(1, -1)
     width = bias.shape[1]
@@ -278,12 +276,12 @@
     hbm = pl.BlockSpec(memory_space=pl.ANY)
     out = jax.ShapeDtypeStruct((seq, dim), F32)
     low = jax.ShapeDtypeStruct((seq, width), BF16)
-    out_specs, out_shape = [rows, rows], [out, out]
+    out_specs, out_shape = ([rows, rows], [out, out]) if chain else ([], [])
     if emit:
         out_specs += [wide, wide, whole(8, width)]
         out_shape += [low, low, jax.ShapeDtypeStruct((8, width), F32)]
     return pl.pallas_call(
-        functools.partial(mlp_kernel, len(ups), bool(before), emit),
+        functools.partial(mlp_kernel, len(ups), bool(before), emit, chain),
         grid=(seq // QB,),
         in_specs=[rows, rows, whole(1, width)] + [hbm] * (2 * len(ups)) + [rows] * len(before),
         out_specs=out_specs,
@@ -493,26 +491,24 @@
         bwd_a = backward(0, fwd_a, after(d_x1_b, g_far_c), 0, heads)
         d_h1 = (bwd_b[0] + bwd_c[0]) + bwd_a[0]
         grad_x_seq = (d_x1 + layer_norm_grad(d_h1, x_hat1, inv_std1, ln1_gain)).astype(BF16)
-        sums = jnp.concatenate([jnp.sum(v, axis=0) for v in (dy_f, d_h2 * x_hat2, d_h2, d_x1, d_h1 * x_hat1, d_h1)])
+        sums = jnp.stack([jnp.sum(v, axis=0) for v in (dy_f, d_h2 * x_hat2, d_h2, d_x1, d_h1 * x_hat1, d_h1)])
         gb = []
         for part in (bwd_a[3], jnp.concatenate([bwd_b[3], bwd_c[3]])):
             part = jnp.transpose(part[:, :3], (1, 0, 2))
-            gb += [part[..., :HD].reshape(-1), part[..., HD:].reshape(-1)]
-        packs = [jnp.concatenate([sums, v]) for v in gb]
-        packs = [packs[0]] + [xor_move(packs[s], s) for s in (1, 2, 3)]
-        totals = (packs[0] + packs[1]) + (packs[2] + packs[3])
-        sums, grad_b_qkv = totals[:6 * dim].reshape(6, dim), totals[6 * dim:].reshape(3, heads, HD)
+            gb += [part[..., :HD], part[..., HD:]]
+        sums = [sums] + [xor_move(sums, s) for s in (1, 2, 3)]
+        sums = (sums[0] + sums[1]) + (sums[2] + sums[3])
+        gb = [gb[0]] + [xor_move(gb[s], s) for s in (1, 2, 3)]
+        grad_b_qkv = (gb[0] + gb[1]) + (gb[2] + gb[3])
         grad_x = to_blocks(grad_x_seq)
 
         far, diag = me ^ 2, me ^ 3
         dy_far = join([[(dyb2, core), (dyb3, core), (grad_y, far), (dy1, far), (dyb3, oth), (dyb2, oth), (dy1, diag), (grad_y, diag)]])[0]
         h2_other = jnp.concatenate([after(h2_far, grad_x_seq), h2_far_next])
-        pre_act = jnp.dot(h2_other, w_up, preferred_element_type=F32) + b_up
-        act, gelu_slope = gelu_terms(pre_act)
-        grad_w_down = near_down + grad_dot(act.astype(BF16), dy_far)
-        d_pre = lax.dot_general(dy_far, w_down, NT, preferred_element_type=F32) * gelu_slope
-        grad_w_up = near_up + grad_dot(h2_other, d_pre.astype(BF16))
-        grad_b_up = (sum0[0] + sum_next[0]) + jnp.sum(d_pre, axis=0)
+        act, d_pre, sum_far = mlp_chain(h2_other, dy_far, b_ups[0], ups[:1], downs[:1], emit=True, chain=False)
+        grad_w_down = near_down + grad_dot(act, dy_far)
+        grad_w_up = near_up + grad_dot(h2_other, d_pre)
+        grad_b_up = (sum0[0] + sum_next[0]) + sum_far[0]
         grads_q, grad_w_out = add_grads(bwd_a[1], xor_move(bwd_a[2], 1), g_across, g_across_c)
         grad_w_qkv = jnp.transpose(grads_q.reshape(3, heads, HD, dim), (0, 3, 1, 2))
         grad_w_out = grad_w_out.reshape(heads, HD, dim)

time: 843 us -> 930 us (1.10)
  waiting for transfers between devices: 274 us -> 355 us
  Pallas kernels: 338 us -> 368 us
  matrix products: 101 us -> 77 us
    ppermute x45 -> x48, waiting for transfers between devices: 243 us -> 324 us  [xor_move(): return lax.ppermute(value, 'tp', [(i, i ^ bits) for i in range(4)])]
    dot_general x2 -> x0, matrix products: 25.7 us -> none  [the longest x1 13.9 us: layer(): lax.dot_general(dy_far, w_down, NT, preferred_element_type=F32) * gelu_slope]
    pallas_call x4 -> x5, Pallas kernels: 85.9 us -> 107 us  [mlp_chain(): pl.pallas_call(functools.partial(mlp_kernel, len(ups), bool(before), emit...]
    ppermute x45 -> x48, starting transfers between devices: 26.6 us -> 27.2 us  [xor_move(): return lax.ppermute(value, 'tp', [(i, i ^ bits) for i in range(4)])]
  transfers between devices with their start and end apart: 47 -> 50, of which waited for: 12 -> 11; matrix products, arithmetic and copies ran while one was open for 21% -> 16% of each run, Pallas kernels for 31% -> 31%
where the time goes in v6:
time: 930 us; the launch traced here: 926 us
  Pallas kernels  368 us (40%)
  waiting for transfers between devices  355 us (38%)
  matrix products  77 us (8%)
  other arithmetic  64 us (7%)
  local copies, waits for them, and re-layouts  30.3 us (3%)
  starting transfers between devices  29.3 us (3%)
    ppermute x48, waiting for transfers between devices, xor_move(): return lax.ppermute(value, 'tp', [(i, i ^ bits) for i in range(4)])  324 us
    pallas_call x3, Pallas kernels, attn_bwd(): pl.pallas_call(attn_bwd_kernel, grid=(count,), in_specs=[whole(seq, dim),...  156 us
    pallas_call x5, Pallas kernels, mlp_chain(): pl.pallas_call(functools.partial(mlp_kernel, len(ups), bool(before), emit...  107 us
    pallas_call x2, Pallas kernels, attn_fwd(): pl.pallas_call(attn_fwd_kernel, grid=(heads,), in_specs=[whole(seq, dim),...  84 us
    dot_general x6, matrix products, grad_dot(): lax.dot_general(a, b, (((0,), (0,)), ((), ())), preferred_element_type=F32)  64.3 us
    ppermute x2, waiting for transfers between devices, swap_groups(): return lax.ppermute(value, 'dp', [(0, 1), (1, 0)])  31.1 us
    ppermute x48, starting transfers between devices, xor_move(): return lax.ppermute(value, 'tp', [(i, i ^ bits) for i in range(4)])  27.2 us
    reduce_sum x3, other arithmetic, layer(): jnp.sum(v, axis=0)  19.9 us
  transfers between devices with their start and end apart: 50, of which 11 were waited for; matrix products, arithmetic and copies ran while one was open for 16% of the time, Pallas kernels for 31%

profile of v6, /device:TPU:0, one launch (start us, length us, event | category | flops | bytes accessed | tf_op | source)
XLA Modules:
  0.0 925.6 jit_solution(8274089566613908216)
XLA Ops:
  22.6 67.1 %collective-permute-done.8 = f32[2240]{0:T(1024)S(1)} collective-permute-done((f32[2240]{0:T(1024)S(1)}, f32[2240]{0:T(1024)S(1)}, u32[]{:S(2)}, u32[]{:S(2)}) %collective-permute-start.8) | collective-permute-done | bytes 8992 | tf_op jit(solution)/shard_map/ppermute | solution.py:364
  103.8 13.8 %collective-permute-done.10.wo0_ref = bf16[5,64,1280]{2,1,0:T(8,128)(2,1)S(1)} collective-permute-done((bf16[5,64,1280]{2,1,0:T(8,128)(2,1)}, bf16[5,64,1280]{2,1,0:T(8,128)(2,1)S(1)}, u32[]{:S(2)}, u32[]{:S(2)}) %collective-permute-start.10) | collective-permute-done | bytes 819232 | tf_op jit(solution)/shard_map/ppermute | solution.py:364
  125.7 19.6 %collective-permute-done.13.refs_2_ = bf16[2,256,1280]{2,1,0:T(8,128)(2,1)} collective-permute-done((bf16[2,256,1280]{2,1,0:T(8,128)(2,1)}, bf16[2,256,1280]{2,1,0:T(8,128)(2,1)}, u32[]{:S(2)}, u32[]{:S(2)}) %collective-permute-start.13) | collective-permute-done | bytes 1310752 | tf_op jit(solution)/shard_map/ppermute | solution.py:364
  146.9 41.9 %attn_fwd.2 = (bf16[1024,640]{1,0:T(8,128)(2,1)}, bf16[1024,640]{1,0:T(8,128)(2,1)}, bf16[1024,640]{1,0:T(8,128)(2,1)}, bf16[1024,640]{1,0:T(8,128)(2,1)}, f32[5,8,1024]{2,1,0:T(8,128)}) custom-call(bf16[1024,1280]{1,0:T(8,128)(2,1)} %fusion.20.h_ref, bf16[3,320,1280]{2,1,0:T(8,128)(2,1)} %bitcast.85, bf16[3,320,1280]{2,1,0:T(8,128)(2,1)} %collective-permute-done.3.w1_ref, ...), custom_call_target="tpu_custom_call" | custom-call | flops 12079595520 | bytes 20000000 | tf_op jit(solution)/shard_map/attn_fwd/pallas_call | solution.py:121
  202.9 42.1 %attn_fwd.3 = (bf16[1024,640]{1,0:T(8,128)(2,1)}, bf16[1024,640]{1,0:T(8,128)(2,1)}, bf16[1024,640]{1,0:T(8,128)(2,1)}, bf16[1024,640]{1,0:T(8,128)(2,1)}, f32[5,8,1024]{2,1,0:T(8,128)}) custom-call(bf16[1024,1280]{1,0:T(8,128)(2,1)} %fusion.20.h_ref, bf16[3,320,1280]{2,1,0:T(8,128)(2,1)} %collective-permute-done.6.w0_ref, ...), custom_call_target="tpu_custom_call" | custom-call | flops 12079595520 | bytes 20000000 | tf_op jit(solution)/shard_map/attn_fwd/pallas_call | solution.py:121
  254.6 20.7 %mlp_chain.5 = (f32[1024,1280]{1,0:T(8,128)}, f32[1024,1280]{1,0:T(8,128)}, bf16[1024,1280]{1,0:T(8,128)(2,1)}, bf16[1024,1280]{1,0:T(8,128)(2,1)}, f32[8,1280]{1,0:T(8,128)}) custom-call(bf16[1024,1280]{1,0:T(8,128)(2,1)} %fusion.13.refs_0_, bf16[1024,1280]{1,0:T(8,128)(2,1)} %get-tuple-element.84.refs_1_, f32[1,1280]{1,0:T(1,128)} %reshape_reshape.8.refs_2_, ...), custom_call_target="tpu_custom_call" | custom-call | flops 13421772800 | bytes 20000000 | tf_op jit(solution)/shard_map/mlp_chain/pallas_call | solution.py:283
  275.3 22.4 %mlp_chain.6 = (f32[1024,1280]{1,0:T(8,128)}, f32[1024,1280]{1,0:T(8,128)}, bf16[1024,1280]{1,0:T(8,128)(2,1)}, bf16[1024,1280]{1,0:T(8,128)(2,1)}, f32[8,1280]{1,0:T(8,128)}) custom-call(bf16[1024,1280]{1,0:T(8,128)(2,1)} %fusion.13.refs_0_, bf16[1024,1280]{1,0:T(8,128)(2,1)} %get-tuple-element.84.refs_1_, f32[1,1280]{1,0:T(1,128)} %reshape_reshape.7.refs_2_, ...), custom_call_target="tpu_custom_call" | custom-call | flops 13421772800 | bytes 20000000 | tf_op jit(solution)/shard_map/mlp_chain/pallas_call | solution.py:283
  319.9 21.6 %mlp_chain.7 = (f32[1024,1280]{1,0:T(8,128)}, f32[1024,1280]{1,0:T(8,128)}) custom-call(bf16[1024,1280]{1,0:T(8,128)(2,1)} %fusion.13.refs_0_, bf16[1024,1280]{1,0:T(8,128)(2,1)} %get-tuple-element.84.refs_1_, f32[1,1280]{1,0:T(1,128)} %bitcast.81, bf16[1280,640]{1,0:T(8,128)(2,1)} %collective-permute-done.18.refs_3_, bf16[1280,640]{1,0:T(8,128)(2,1)} %copy-done.27, ...), custom_call_target="tpu_custom_call" | custom-call | flops 13421772800 | bytes 20000000 | tf_op jit(solution)/shard_map/mlp_chain/pallas_call | solution.py:283
  341.6 31.1 %collective-permute-done.24.refs_3_ = bf16[1280,640]{1,0:T(8,128)(2,1)} collective-permute-done((bf16[1280,640]{1,0:T(8,128)(2,1)}, bf16[1280,640]{1,0:T(8,128)(2,1)}, u32[]{:S(2)}, u32[]{:S(2)}) %collective-permute-start.24) | collective-permute-done | bytes 1638432 | tf_op jit(solution)/shard_map/ppermute | solution.py:368
  372.7 10.9 %convolution_add_fusion.2 = f32[1280,1280]{1,0:T(8,128)} fusion(f32[1280,1280]{1,0:T(8,128)} %fusion.45, bf16[1024,1280]{1,0:T(8,128)(2,1)} %collective-permute-done.23, bf16[1024,1280]{1,0:T(8,128)(2,1)} %get-tuple-element.94), kind=kOutput, calls=%fused_computation.2 | convolution fusion | flops 3357081600 | bytes 18350080 | tf_op jit(solution)/shard_map/dot_general | solution.py:454
  392.7 21.4 %mlp_chain.8 = (f32[1024,1280]{1,0:T(8,128)}, f32[1024,1280]{1,0:T(8,128)}) custom-call(bf16[1024,1280]{1,0:T(8,128)(2,1)} %fusion.13.refs_0_, bf16[1024,1280]{1,0:T(8,128)(2,1)} %get-tuple-element.84.refs_1_, f32[1,1280]{1,0:T(1,128)} %bitcast.80, bf16[1280,640]{1,0:T(8,128)(2,1)} %collective-permute-done.24.refs_3_, ...), custom_call_target="tpu_custom_call" | custom-call | flops 13421772800 | bytes 20000000 | tf_op jit(solution)/shard_map/mlp_chain/pallas_call | solution.py:283
  429.8 47.3 %attn_bwd.3 = (f32[1024,1280]{1,0:T(8,128)}, f32[4,192,1280]{2,1,0:T(8,128)}, f32[4,192,1280]{2,1,0:T(8,128)}, f32[3,8,128]{2,1,0:T(8,128)}) custom-call(bf16[1024,1280]{1,0:T(8,128)(2,1)} %fusion.20.h_ref, bf16[1024,1280]{1,0:T(8,128)(2,1)} %convert_element_type.47.dx_ref, bf16[3,320,1280]{2,1,0:T(8,128)(2,1)} %collective-permute-done.6.w0_ref, ...), custom_call_target="tpu_custom_call" | custom-call | flops 14495514624 | bytes 20000000 | tf_op jit(solution)/shard_map/attn_bwd/pallas_call | solution.py:204
  489.1 34.6 %attn_bwd.4 = (f32[1024,1280]{1,0:T(8,128)}, f32[4,128,1280]{2,1,0:T(8,128)}, f32[4,128,1280]{2,1,0:T(8,128)}, f32[2,8,128]{2,1,0:T(8,128)}) custom-call(bf16[1024,1280]{1,0:T(8,128)(2,1)} %fusion.20.h_ref, bf16[1024,1280]{1,0:T(8,128)(2,1)} %convert_element_type.47.dx_ref, bf16[3,320,1280]{2,1,0:T(8,128)(2,1)} %collective-permute-done.6.w0_ref, ...), custom_call_target="tpu_custom_call" | custom-call | flops 9663676416 | bytes 20000000 | tf_op jit(solution)/shard_map/attn_bwd/pallas_call | solution.py:204
  527.2 38.6 %collective-permute-done.47.refs_0_ = bf16[2,256,1280]{2,1,0:T(8,128)(2,1)} collective-permute-done((bf16[2,256,1280]{2,1,0:T(8,128)(2,1)}, bf16[2,256,1280]{2,1,0:T(8,128)(2,1)}, u32[]{:S(2)}, u32[]{:S(2)}) %collective-permute-start.47) | collective-permute-done | bytes 1310752 | tf_op jit(solution)/shard_map/ppermute | solution.py:364
  567.0 11.5 %collective-permute-done.28 = bf16[256,1280]{1,0:T(8,128)(2,1)S(1)} collective-permute-done((bf16[256,1280]{1,0:T(8,128)(2,1)}, bf16[256,1280]{1,0:T(8,128)(2,1)S(1)}, u32[]{:S(2)}, u32[]{:S(2)}) %collective-permute-start.28) | collective-permute-done | bytes 655392 | tf_op jit(solution)/shard_map/ppermute | solution.py:364
  579.6 13.4 %collective-permute-done.29 = bf16[256,1280]{1,0:T(8,128)(2,1)} collective-permute-done((bf16[256,1280]{1,0:T(8,128)(2,1)}, bf16[256,1280]{1,0:T(8,128)(2,1)}, u32[]{:S(2)}, u32[]{:S(2)}) %collective-permute-start.29) | collective-permute-done | bytes 655392 | tf_op jit(solution)/shard_map/ppermute | solution.py:364
  607.5 74.3 %attn_bwd.5 = (f32[1024,1280]{1,0:T(8,128)}, f32[4,320,1280]{2,1,0:T(8,128)}, f32[4,320,1280]{2,1,0:T(8,128)}, f32[5,8,128]{2,1,0:T(8,128)}) custom-call(bf16[1024,1280]{1,0:T(8,128)(2,1)} %fusion.20.h_ref, bf16[1024,1280]{1,0:T(8,128)(2,1)} %convert_element_type.47.dx_ref, bf16[3,320,1280]{2,1,0:T(8,128)(2,1)} %bitcast.86, ...), custom_call_target="tpu_custom_call" | custom-call | flops 24159191040 | bytes 20000000 | tf_op jit(solution)/shard_map/attn_bwd/pallas_call | solution.py:204
  702.6 20.9 %mlp_chain.9 = (bf16[2048,1280]{1,0:T(8,128)(2,1)}, bf16[2048,1280]{1,0:T(8,128)(2,1)}, f32[8,1280]{1,0:T(8,128)}) custom-call(bf16[2048,1280]{1,0:T(8,128)(2,1)} %constant_dynamic-update-slice_fusion.1.refs_0_, bf16[2048,1280]{1,0:T(8,128)(2,1)} %join_rows.3.refs_1_, f32[1,1280]{1,0:T(1,128)} %reshape_reshape.8.refs_2_, bf16[1280,1280]{1,0:T(8,128)(2,1)} %refs_3_.3, ...), custom_call_target="tpu_custom_call" | custom-call | flops 26843545600 | bytes 20000000 | tf_op jit(solution)/shard_map/mlp_chain/pallas_call | solution.py:283
  723.5 13.2 %convolution_add_fusion = f32[1280,1280]{1,0:T(8,128)} fusion(f32[1280,1280]{1,0:T(8,128)} %convolution_add_fusion.2, bf16[2048,1280]{1,0:T(8,128)(2,1)} %get-tuple-element.135, bf16[2048,1280]{1,0:T(8,128)(2,1)} %join_rows.3.refs_1_), kind=kOutput, calls=%fused_computation | convolution fusion | flops 6712524800 | bytes 23592960 | tf_op jit(solution)/shard_map/dot_general | solution.py:454
  740.7 13.2 %convolution_add_fusion.1 = f32[1280,1280]{1,0:T(8,128)} fusion(f32[1280,1280]{1,0:T(8,128)} %convolution_add_fusion.3, bf16[2048,1280]{1,0:T(8,128)(2,1)} %constant_dynamic-update-slice_fusion.1.refs_0_, bf16[2048,1280]{1,0:T(8,128)(2,1)} %get-tuple-element.131), kind=kOutput, calls=%fused_computation.1 | convolution fusion | flops 6712524800 | bytes 23592960 | tf_op jit(solution)/shard_map/dot_general | solution.py:454
  753.9 128.7 %collective-permute-done.37 = f32[6,1280]{1,0:T(8,128)S(1)} collective-permute-done((f32[6,1280]{1,0:T(8,128)S(1)}, f32[6,1280]{1,0:T(8,128)S(1)}, u32[]{:S(2)}, u32[]{:S(2)}) %collective-permute-start.37) | collective-permute-done | bytes 30752 | tf_op jit(solution)/shard_map/ppermute | solution.py:364
  884.1 12.0 %collective-permute-done.38 = f32[6,1280]{1,0:T(8,128)S(1)} collective-permute-done((f32[6,1280]{1,0:T(8,128)S(1)}, f32[6,1280]{1,0:T(8,128)S(1)}, u32[]{:S(2)}, u32[]{:S(2)}) %collective-permute-start.38) | collective-permute-done | bytes 30752 | tf_op jit(solution)/shard_map/ppermute | solution.py:364
  898.8 14.5 %collective-permute-done.34 = bf16[256,1280]{1,0:T(8,128)(2,1)S(1)} collective-permute-done((bf16[256,1280]{1,0:T(8,128)(2,1)S(1)}, bf16[256,1280]{1,0:T(8,128)(2,1)S(1)}, u32[]{:S(2)}, u32[]{:S(2)}) %collective-permute-start.34) | collective-permute-done | bytes 655392 | tf_op jit(solution)/shard_map/ppermute | solution.py:364
  915.4 10.0 %add_grads.1 = (f32[3,320,1280]{2,1,0:T(8,128)}, f32[320,1280]{1,0:T(8,128)}) custom-call(f32[4,320,1280]{2,1,0:T(8,128)} %get-tuple-element.119.a_ref, f32[4,320,1280]{2,1,0:T(8,128)} %collective-permute-done.39.b_ref, f32[4,192,1280]{2,1,0:T(8,128)} %collective-permute-done.40.c0_ref, f32[4,128,1280]{2,1,0:T(8,128)} %collective-permute-done.41.c1_ref), custom_call_target="tpu_custom_call" | custom-call | flops 10000000 | bytes 20000000 | tf_op jit(solution)/shard_map/add_grads/pallas_call | solution.py:351
  (257 shorter events, 179.1 us)
Async XLA Ops:
  3.9 92.4 %collective-permute-start = (bf16[256,1280]{1,0:T(8,128)(2,1)}, bf16[256,1280]{1,0:T(8,128)(2,1)}, u32[]{:S(2)}, u32[]{:S(2)}) collective-permute-start(bf16[256,1280]{1,0:T(8,128)(2,1)} %get-tuple-element.172), channel_id=1, source_target_pairs={{0,1},{1,0},{2,3},{3,2},{4,5},{5,4},{6,7},{7,6}} | collective-permute-start | bytes 1966088 | tf_op jit(solution)/shard_map/ppermute | solution.py:364
  4.7 91.6 %collective-permute-start.1 = (bf16[256,1280]{1,0:T(8,128)(2,1)}, bf16[256,1280]{1,0:T(8,128)(2,1)}, u32[]{:S(2)}, u32[]{:S(2)}) collective-permute-start(bf16[256,1280]{1,0:T(8,128)(2,1)} %get-tuple-element.174), channel_id=1, source_target_pairs={{0,2},{1,3},{2,0},{3,1},{4,6},{5,7},{6,4},{7,5}} | collective-permute-start | bytes 1966088 | tf_op jit(solution)/shard_map/ppermute | solution.py:364
  7.2 90.6 %collective-permute-start.2 = (bf16[256,1280]{1,0:T(8,128)(2,1)}, bf16[256,1280]{1,0:T(8,128)(2,1)}, u32[]{:S(2)}, u32[]{:S(2)}) collective-permute-start(bf16[256,1280]{1,0:T(8,128)(2,1)} %get-tuple-element.173), channel_id=1, source_target_pairs={{0,3},{1,2},{2,1},{3,0},{4,7},{5,6},{6,5},{7,4}} | collective-permute-start | bytes 1966088 | tf_op jit(solution)/shard_map/ppermute | solution.py:364
  7.5 110.1 %collective-permute-start.6 = (bf16[3,320,1280]{2,1,0:T(8,128)(2,1)}, bf16[3,320,1280]{2,1,0:T(8,128)(2,1)}, u32[]{:S(2)}, u32[]{:S(2)}) collective-permute-start(bf16[3,320,1280]{2,1,0:T(8,128)(2,1)} %bitcast.83), channel_id=1, source_target_pairs={{0,2},{1,3},{2,0},{3,1},{4,6},{5,7},{6,4},{7,5}} | collective-permute-start | bytes 7372808 | tf_op jit(solution)/shard_map/ppermute | solution.py:364
  103.8 92.5 %collective-permute-start.12 = (bf16[4,256,1280]{2,1,0:T(8,128)(2,1)S(1)}, bf16[4,256,1280]{2,1,0:T(8,128)(2,1)}, u32[]{:S(2)}, u32[]{:S(2)}) collective-permute-start(bf16[4,256,1280]{2,1,0:T(8,128)(2,1)S(1)} %copy-done.3), channel_id=1, source_target_pairs={{0,1},{1,0},{2,3},{3,2},{4,5},{5,4},{6,7},{7,6}} | collective-permute-start | bytes 7864328 | tf_op jit(solution)/shard_map/ppermute | solution.py:364
  117.6 85.2 %collective-permute-start.7 = (bf16[3,320,1280]{2,1,0:T(8,128)(2,1)}, bf16[3,320,1280]{2,1,0:T(8,128)(2,1)}, u32[]{:S(2)}, u32[]{:S(2)}) collective-permute-start(bf16[3,320,1280]{2,1,0:T(8,128)(2,1)} %collective-permute-done.6.w0_ref), channel_id=1, source_target_pairs={{0,1},{1,0},{2,3},{3,2},{4,5},{5,4},{6,7},{7,6}} | collective-permute-start | bytes 7372808 | tf_op jit(solution)/shard_map/ppermute | solution.py:364
  124.3 151.1 %collective-permute-start.15 = (bf16[1280,1280]{1,0:T(8,128)(2,1)}, bf16[1280,1280]{1,0:T(8,128)(2,1)}, u32[]{:S(2)}, u32[]{:S(2)}) collective-permute-start(bf16[1280,1280]{1,0:T(8,128)(2,1)} %refs_3_.3), channel_id=1, source_target_pairs={{0,1},{1,0},{2,3},{3,2},{4,5},{5,4},{6,7},{7,6}} | collective-permute-start | bytes 9830408 | tf_op jit(solution)/shard_map/ppermute | solution.py:364
  145.3 130.0 %collective-permute-start.16 = (bf16[1280,1280]{1,0:T(8,128)(2,1)}, bf16[1280,1280]{1,0:T(8,128)(2,1)}, u32[]{:S(2)}, u32[]{:S(2)}) collective-permute-start(bf16[1280,1280]{1,0:T(8,128)(2,1)} %refs_4_.3), channel_id=1, source_target_pairs={{0,1},{1,0},{2,3},{3,2},{4,5},{5,4},{6,7},{7,6}} | collective-permute-start | bytes 9830408 | tf_op jit(solution)/shard_map/ppermute | solution.py:364
  195.2 102.5 %collective-permute-start.18 = (bf16[1280,640]{1,0:T(8,128)(2,1)}, bf16[1280,640]{1,0:T(8,128)(2,1)}, u32[]{:S(2)}, u32[]{:S(2)}) collective-permute-start(bf16[1280,640]{1,0:T(8,128)(2,1)} %constant_dynamic-slice_fusion.2), channel_id=1, source_target_pairs={{0,2},{1,3},{2,0},{3,1},{4,6},{5,7},{6,4},{7,5}} | collective-permute-start | bytes 4915208 | tf_op jit(solution)/shard_map/ppermute | solution.py:364
  196.3 101.5 %collective-permute-start.20 = (bf16[640,1280]{1,0:T(8,128)(2,1)}, bf16[640,1280]{1,0:T(8,128)(2,1)}, u32[]{:S(2)}, u32[]{:S(2)}) collective-permute-start(bf16[640,1280]{1,0:T(8,128)(2,1)} %constant_dynamic-slice_fusion.1), channel_id=1, source_target_pairs={{0,2},{1,3},{2,0},{3,1},{4,6},{5,7},{6,4},{7,5}} | collective-permute-start | bytes 4915208 | tf_op jit(solution)/shard_map/ppermute | solution.py:364
  301.0 71.7 %collective-permute-start.23 = (bf16[1024,1280]{1,0:T(8,128)(2,1)}, bf16[1024,1280]{1,0:T(8,128)(2,1)}, u32[]{:S(2)}, u32[]{:S(2)}) collective-permute-start(bf16[1024,1280]{1,0:T(8,128)(2,1)} %get-tuple-element.92), channel_id=1, source_target_pairs={{0,1},{1,0},{2,3},{3,2},{4,5},{5,4},{6,7},{7,6}} | collective-permute-start | bytes 7864328 | tf_op jit(solution)/shard_map/ppermute | solution.py:364
  311.1 72.5 %collective-permute-start.22 = (bf16[1024,1280]{1,0:T(8,128)(2,1)}, bf16[1024,1280]{1,0:T(8,128)(2,1)}, u32[]{:S(2)}, u32[]{:S(2)}) collective-permute-start(bf16[1024,1280]{1,0:T(8,128)(2,1)} %get-tuple-element.91), channel_id=1, source_target_pairs={{0,1},{1,0},{2,3},{3,2},{4,5},{5,4},{6,7},{7,6}} | collective-permute-start | bytes 7864328 | tf_op jit(solution)/shard_map/ppermute | solution.py:364
  477.7 88.1 %collective-permute-start.45 = (bf16[1024,1280]{1,0:T(8,128)(2,1)}, bf16[1024,1280]{1,0:T(8,128)(2,1)}, u32[]{:S(2)}, u32[]{:S(2)}) collective-permute-start(bf16[1024,1280]{1,0:T(8,128)(2,1)} %fusion.13.refs_0_), channel_id=1, source_target_pairs={{0,2},{1,3},{2,0},{3,1},{4,6},{5,7},{6,4},{7,5}} | collective-permute-start | bytes 7864328 | tf_op jit(solution)/shard_map/ppermute | solution.py:364
  478.8 87.1 %collective-permute-start.47 = (bf16[2,256,1280]{2,1,0:T(8,128)(2,1)}, bf16[2,256,1280]{2,1,0:T(8,128)(2,1)}, u32[]{:S(2)}, u32[]{:S(2)}) collective-permute-start(bf16[2,256,1280]{2,1,0:T(8,128)(2,1)} %get-tuple-element.129), channel_id=1, source_target_pairs={{0,2},{1,3},{2,0},{3,1},{4,6},{5,7},{6,4},{7,5}} | collective-permute-start | bytes 3932168 | tf_op jit(solution)/shard_map/ppermute | solution.py:364
  523.7 80.2 %collective-permute-start.32 = (f32[4,128,1280]{2,1,0:T(8,128)}, f32[4,128,1280]{2,1,0:T(8,128)}, u32[]{:S(2)}, u32[]{:S(2)}) collective-permute-start(f32[4,128,1280]{2,1,0:T(8,128)} %get-tuple-element.112), channel_id=1, source_target_pairs={{0,1},{1,0},{2,3},{3,2},{4,5},{5,4},{6,7},{7,6}} | collective-permute-start | bytes 7864328 | tf_op jit(solution)/shard_map/ppermute | solution.py:364
  578.5 158.6 %collective-permute-start.49 = (f32[8,1280]{1,0:T(8,128)S(1)}, f32[8,1280]{1,0:T(8,128)S(1)}, u32[]{:S(2)}, u32[]{:S(2)}) collective-permute-start(f32[8,1280]{1,0:T(8,128)S(1)} %copy-done.29), channel_id=1, source_target_pairs={{0,1},{1,0},{2,3},{3,2},{4,5},{5,4},{6,7},{7,6}} | collective-permute-start | bytes 122888 | tf_op jit(solution)/shard_map/ppermute | solution.py:364
  593.0 106.2 %collective-permute-start.46 = (bf16[1024,1280]{1,0:T(8,128)(2,1)}, bf16[1024,1280]{1,0:T(8,128)(2,1)}, u32[]{:S(2)}, u32[]{:S(2)}) collective-permute-start(bf16[1024,1280]{1,0:T(8,128)(2,1)} %collective-permute-done.45), channel_id=1, source_target_pairs={{0,1},{1,0},{2,3},{3,2},{4,5},{5,4},{6,7},{7,6}} | collective-permute-start | bytes 7864328 | tf_op jit(solution)/shard_map/ppermute | solution.py:364
  602.1 135.5 %collective-permute-start.43 = (f32[3,5,64]{2,0,1:T(4,128)S(1)}, f32[3,5,64]{2,0,1:T(4,128)S(1)}, u32[]{:S(2)}, u32[]{:S(2)}) collective-permute-start(f32[3,5,64]{2,0,1:T(4,128)S(1)} %get-tuple-element.176), channel_id=1, source_target_pairs={{0,2},{1,3},{2,0},{3,1},{4,6},{5,7},{6,4},{7,5}} | collective-permute-start | bytes 11528 | tf_op jit(solution)/shard_map/ppermute | solution.py:364
  603.2 135.5 %collective-permute-start.44 = (f32[3,5,64]{2,0,1:T(4,128)S(1)}, f32[3,5,64]{2,0,1:T(4,128)S(1)}, u32[]{:S(2)}, u32[]{:S(2)}) collective-permute-start(f32[3,5,64]{2,0,1:T(4,128)S(1)} %get-tuple-element.175), channel_id=1, source_target_pairs={{0,3},{1,2},{2,1},{3,0},{4,7},{5,6},{6,5},{7,4}} | collective-permute-start | bytes 11528 | tf_op jit(solution)/shard_map/ppermute | solution.py:364
  695.5 220.0 %collective-permute-start.39 = (f32[4,320,1280]{2,1,0:T(8,128)}, f32[4,320,1280]{2,1,0:T(8,128)}, u32[]{:S(2)}, u32[]{:S(2)}) collective-permute-start(f32[4,320,1280]{2,1,0:T(8,128)} %get-tuple-element.120), channel_id=1, source_target_pairs={{0,1},{1,0},{2,3},{3,2},{4,5},{5,4},{6,7},{7,6}} | collective-permute-start | bytes 19660808 | tf_op jit(solution)/shard_map/ppermute | solution.py:364
  737.6 177.8 %collective-permute-start.40 = (f32[4,192,1280]{2,1,0:T(8,128)}, f32[4,192,1280]{2,1,0:T(8,128)}, u32[]{:S(2)}, u32[]{:S(2)}) collective-permute-start(f32[4,192,1280]{2,1,0:T(8,128)} %add.212), channel_id=1, source_target_pairs={{0,2},{1,3},{2,0},{3,1},{4,6},{5,7},{6,4},{7,5}} | collective-permute-start | bytes 11796488 | tf_op jit(solution)/shard_map/ppermute | solution.py:364
  738.7 176.7 %collective-permute-start.41 = (f32[4,128,1280]{2,1,0:T(8,128)}, f32[4,128,1280]{2,1,0:T(8,128)}, u32[]{:S(2)}, u32[]{:S(2)}) collective-permute-start(f32[4,128,1280]{2,1,0:T(8,128)} %add.214), channel_id=1, source_target_pairs={{0,2},{1,3},{2,0},{3,1},{4,6},{5,7},{6,4},{7,5}} | collective-permute-start | bytes 7864328 | tf_op jit(solution)/shard_map/ppermute | solution.py:364
  739.6 143.1 %collective-permute-start.37 = (f32[6,1280]{1,0:T(8,128)S(1)}, f32[6,1280]{1,0:T(8,128)S(1)}, u32[]{:S(2)}, u32[]{:S(2)}) collective-permute-start(f32[6,1280]{1,0:T(8,128)S(1)} %stack.130), channel_id=1, source_target_pairs={{0,2},{1,3},{2,0},{3,1},{4,6},{5,7},{6,4},{7,5}} | collective-permute-start | bytes 92168 | tf_op jit(solution)/shard_map/ppermute | solution.py:364
  740.7 156.5 %collective-permute-start.33 = (bf16[256,1280]{1,0:T(8,128)(2,1)S(1)}, bf16[256,1280]{1,0:T(8,128)(2,1)S(1)}, u32[]{:S(2)}, u32[]{:S(2)}) collective-permute-start(bf16[256,1280]{1,0:T(8,128)(2,1)S(1)} %get-tuple-element.167), channel_id=1, source_target_pairs={{0,3},{1,2},{2,1},{3,0},{4,7},{5,6},{6,5},{7,4}} | collective-permute-start | bytes 1966088 | tf_op jit(solution)/shard_map/ppermute | solution.py:364
  (60 other events, 1926.4 us)
